TPU v7x, 32 devices: a whole 2x2x4 slice. The times are simulated.
32 devices in a mesh: rep: 2 (over x), dp: 16 (over y, z, core).
Axes of the slice: x: 2, y: 2, z: 4, core: 2. Of those that a mesh axis runs over, the one named last changes fastest.
Arguments:
- x: bfloat16 [32, 2048, 896], P(('rep', 'dp')), parts along dimension 0
- dy: bfloat16 [32, 2048, 896], P(('rep', 'dp')), parts along dimension 0
- w_gate: bfloat16 [2, 896, 2304], P(None, 'dp')
- w_up: bfloat16 [2, 896, 2304], P(None, 'dp')
- w_down: bfloat16 [2, 2304, 896], P(None, 'dp')
Outputs:
- output 1: bfloat16 [32, 2048, 896], P(('rep', 'dp')), parts along dimension 0
- output 2: bfloat16 [4, 896, 2304], P('rep', 'dp'), parts along dimension 0
- output 3: bfloat16 [4, 896, 2304], P('rep', 'dp'), parts along dimension 0
- output 4: bfloat16 [4, 2304, 896], P('rep', 'dp'), parts along dimension 0
There are 2 independent parts. A program takes and returns all parts, laid end to end along the dimension named above; an argument that names none is the same for every part.
All inputs are finite; a program needn't handle non-finite values.
Results may differ from a plain program's by a relative error of at most 0.018.
Values are sent between devices in bfloat16 or wider.
A program may use at most 2 GiB of HBM per device.

v0:
```python
import jax
import jax.numpy as jnp
from jax import lax

NAMES = ("w_gate", "w_up", "w_down")


def matmul(a, w):
    return jnp.dot(a, w, preferred_element_type=jnp.float32).astype(jnp.bfloat16)


def normed(h):
    wide = h.astype(jnp.float32)
    scale = lax.rsqrt(jnp.mean(wide**2, -1, keepdims=True) + 1e-6)
    return (wide * scale).astype(jnp.bfloat16)


def layer(h, w):
    a = normed(h)
    gate = jnp.dot(a, w["w_gate"], preferred_element_type=jnp.float32)
    up = jnp.dot(a, w["w_up"], preferred_element_type=jnp.float32)
    return h + matmul((jax.nn.silu(gate) * up).astype(jnp.bfloat16), w["w_down"])


def stack(weights, h):
    for number in range(weights["w_gate"].shape[0]):
        h = layer(h, {name: w[number] for name, w in weights.items()})
    return h


def solution(mesh):
    groups = mesh.shape["rep"]

    def step(x, dy, *weights):
        shape = x.shape
        x, dy = (t.reshape(groups, -1, *t.shape[1:]) for t in (x, dy))

        def of_a_group(x, dy):
            _, back = jax.vjp(stack, dict(zip(NAMES, weights, strict=True)), x)
            by_weights, by_x = back(dy)
            return (by_x, *(by_weights[name] for name in NAMES))

        by_x, *by_weights = jax.vmap(of_a_group)(x, dy)
        return (by_x.reshape(shape), *(t.reshape(-1, *t.shape[2:]) for t in by_weights))

    return step
```

profile of v0, /device:TPU:4, one launch (start us, length us, event | category | flops | bytes accessed | tf_op | source)
XLA Modules:
  0.0 1298.0 jit_solution(7833688709081142173)
XLA Ops:
  17.7 6.1 copy.1
  23.9 6.1 copy
  30.0 6.1 copy.3
  36.8 24.1 %all-gather.30.cloned.1.call-done = bf16[1,896,2304]{2,1,0:T(8,128)(2,1)} async-done(((bf16[1,56,2304]{2,1,0:T(8,128)(2,1)}), bf16[1,896,2304]{2,1,0:T(8,128)(2,1)}) %all-gather.30.cloned.1.call-update) | async-done | bytes 4128784 | tf_op jit(solution)/vmap(jvp())/squeeze | solution.py:27
  60.9 16.5 %fusion.192 = f32[2048,2304]{1,0:T(8,128)} fusion(bf16[1,896,2304]{2,1,0:T(8,128)(2,1)} %all-gather.30.cloned.1.call-done, bf16[1,2048,896]{2,1,0:T(8,128)(2,1)} %param.13, f32[2048]{0:T(1024)S(1)} %get-tuple-element.267), kind=kOutput, calls=%fused_computation.243 | convolution fusion | flops 8461221888 | bytes 26681344 | tf_op jit(solution)/vmap(jvp())/dot_general | solution.py:20
  77.3 34.8 %all-gather.32.cloned.1.call-done = bf16[1,896,2304]{2,1,0:T(8,128)(2,1)} async-done(((bf16[1,56,2304]{2,1,0:T(8,128)(2,1)}), bf16[1,896,2304]{2,1,0:T(8,128)(2,1)}) %all-gather.32.cloned.1.call-update) | async-done | bytes 4128784 | tf_op jit(solution)/vmap(jvp())/squeeze | solution.py:27
  112.2 21.3 %fusion.160 = (bf16[1,1,2048,2304]{3,2,1,0:T(8,128)(2,1)}, f32[2048,2304]{1,0:T(8,128)}) fusion(f32[2048,2304]{1,0:T(8,128)} %fusion.192, bf16[1,896,2304]{2,1,0:T(8,128)(2,1)} %all-gather.32.cloned.1.call-done, bf16[1,2048,896]{2,1,0:T(8,128)(2,1)} %param.13, f32[2048]{0:T(1024)S(1)} %get-tuple-element.267), kind=kOutput, calls=%fused_computation.195 | convolution fusion | flops 8489533440 | bytes 54992896 | tf_op jit(solution)/vmap(jvp())/dot_general | solution.py:21
  133.4 30.1 %all-gather.34.cloned.1.call-done = bf16[1,2304,896]{2,1,0:T(8,128)(2,1)} async-done(((bf16[1,144,896]{2,1,0:T(8,128)(2,1)}), bf16[1,2304,896]{2,1,0:T(8,128)(2,1)}) %all-gather.34.cloned.1.call-update) | async-done | bytes 4128784 | tf_op jit(solution)/vmap(jvp())/squeeze | solution.py:27
  163.5 13.8 %fusion.176 = (f32[2048]{0:T(1024)S(1)}, bf16[1,1,2048,896]{2,3,1,0:T(8,128)(2,1)S(1)}) fusion(bf16[1,2304,896]{2,1,0:T(8,128)(2,1)} %all-gather.34.cloned.1.call-done, bf16[1,1,2048,2304]{3,2,1,0:T(8,128)(2,1)} %get-tuple-element.268, bf16[1,2048,896]{1,2,0:T(8,128)(2,1)} %copy.1), kind=kOutput, calls=%fused_computation.227 | convolution fusion | flops 8464889856 | bytes 20914176 | tf_op jit(solution)/vmap(jvp())/dot_general | solution.py:9
  181.9 32.8 %all-gather.36.cloned.1.call-done = bf16[1,896,2304]{2,1,0:T(8,128)(2,1)} async-done(((bf16[1,56,2304]{2,1,0:T(8,128)(2,1)}), bf16[1,896,2304]{2,1,0:T(8,128)(2,1)}) %all-gather.36.cloned.1.call-update) | async-done | bytes 4128784 | tf_op jit(solution)/vmap(jvp())/squeeze | solution.py:27
  214.7 16.5 %fusion.184 = f32[2048,2304]{1,0:T(8,128)} fusion(bf16[1,896,2304]{2,1,0:T(8,128)(2,1)} %all-gather.36.cloned.1.call-done, bf16[1,1,2048,896]{2,3,1,0:T(8,128)(2,1)} %fusion.177), kind=kOutput, calls=%fused_computation.235 | convolution fusion | flops 8455716864 | bytes 26673152 | tf_op jit(solution)/vmap(jvp())/dot_general | solution.py:20
  231.2 34.6 %all-gather.40.cloned.1.call-done = bf16[1,896,2304]{2,1,0:T(8,128)(2,1)} async-done(((bf16[1,56,2304]{2,1,0:T(8,128)(2,1)}), bf16[1,896,2304]{2,1,0:T(8,128)(2,1)}) %all-gather.40.cloned.1.call-update) | async-done | bytes 4128784 | tf_op jit(solution)/vmap(jvp())/squeeze | solution.py:27
  265.8 23.4 %fusion.154 = (bf16[1,1,2048,2304]{3,2,1,0:T(8,128)(2,1)}, f32[2048,2304]{1,0:T(8,128)}) fusion(f32[2048,2304]{1,0:T(8,128)} %fusion.184, bf16[1,896,2304]{2,1,0:T(8,128)(2,1)} %all-gather.40.cloned.1.call-done, bf16[1,1,2048,896]{2,3,1,0:T(8,128)(2,1)} %fusion.177), kind=kOutput, calls=%fused_computation.185 | convolution fusion | flops 8484028416 | bytes 54984704 | tf_op jit(solution)/vmap(jvp())/dot_general | solution.py:21
  289.2 12.6 copy.4
  301.9 12.8 copy.2
  314.6 135.9 %while.16 = (bf16[1,1,2048,2304]{2,3,1,0:T(8,128)(2,1)}, bf16[1,1,2048,896]{3,2,1,0:T(8,128)(2,1)}, f32[1,144,896]{2,1,0:T(8,128)S(1)}, f32[1,144,896]{2,1,0:T(8...) while((bf16[1,1,2048,2304]{2,3,1,0:T(8,128)(2,1)}, ...), condition=%wide.windowed_dot_general_cond_rs.4.clone, body=%wide.windowed_dot_general_body_rs.4.clone.sunk | while | flops 2119421952 | bytes 44794468 | solution.py:9
  324.9 6.0 collective-permute-done.16
  339.9 5.9 collective-permute-done.18
  372.6 7.1 collective-permute-done.18
  391.9 6.4 collective-permute-done.16
  407.4 7.6 collective-permute-done.18
  427.2 5.8 collective-permute-done.16
  442.0 7.5 collective-permute-done.18
  450.5 31.5 %convert_multiply_fusion.3 = (bf16[1,1,2048,2304]{3,2,1,0:T(8,128)(2,1)}, bf16[1,1,2048,2304]{3,2,1,0:T(8,128)(2,1)}) fusion(f32[2048,2304]{1,0:T(8,128)} %fusion.184, f32[2048,2304]{1,0:T(8,128)} %get-tuple-element.276, bf16[1,2304,896]{2,1,0:T(8,128)(2,1)} %all-gather.38.cloned.1.call-done, bf16[1,2048,896]{2,1,0:T(8,128)(2,1)} %param.12), kind=kOutput, calls=%fused_computation.173 | convolution fusion | flops 8531214336 | bytes 64421888 | tf_op jit(solution)/vmap(transpose(jvp()))/dot_general | solution.py:9
  482.0 14.0 %fusion.152 = bf16[2048,896]{0,1:T(8,128)(2,1)} fusion(bf16[1,1,2048,2304]{3,2,1,0:T(8,128)(2,1)} %get-tuple-element.551, bf16[1,896,2304]{2,1,0:T(8,128)(2,1)} %all-gather.36.cloned.1.call-done), kind=kOutput, calls=%fused_computation.182 | convolution fusion | flops 8455716864 | bytes 17235968 | tf_op jit(solution)/vmap(transpose(jvp()))/dot_general | solution.py:20
  496.0 11.1 fusion.178
  511.6 6.1 copy.5
  517.8 137.0 %while.17 = (bf16[1,1,2048,2304]{2,3,1,0:T(8,128)(2,1)}, bf16[1,1,2048,896]{3,2,1,0:T(8,128)(2,1)}, f32[1,144,896]{2,1,0:T(8,128)S(1)}, f32[1,144,896]{2,1,0:T(8...) while((bf16[1,1,2048,2304]{2,3,1,0:T(8,128)(2,1)}, ...), condition=%wide.windowed_dot_general_cond_rs.5.clone, body=%wide.windowed_dot_general_body_rs.5.clone.sunk | while | flops 2119421952 | bytes 44794468 | solution.py:9
  542.4 7.1 collective-permute-done.22
  562.0 6.1 collective-permute-done.20
  577.2 7.4 collective-permute-done.22
  611.8 7.6 collective-permute-done.22
  646.4 7.4 collective-permute-done.22
  655.6 142.1 %while.14 = (bf16[1,1,2048,896]{2,3,1,0:T(8,128)(2,1)}, bf16[1,1,2048,2304]{3,2,1,0:T(8,128)(2,1)}, f32[1,56,2304]{2,1,0:T(8,128)S(1)}, f32[1,56,2304]{2,1,0:T(8...) while((bf16[1,1,2048,896]{2,3,1,0:T(8,128)(2,1)}, ...), condition=%wide.windowed_dot_general_cond_rs.2.clone, body=%wide.windowed_dot_general_body_rs.2.clone.sunk | while | flops 2116538368 | bytes 97223328 | solution.py:21
  662.8 5.5 fusion.294
  668.3 8.7 collective-permute-done.8
  683.2 6.3 collective-permute-done.10
  717.3 9.3 collective-permute-done.10
  752.2 9.3 collective-permute-done.10
  787.1 9.3 collective-permute-done.10
  797.7 30.8 %convert_multiply_fusion.1 = (bf16[1,1,2048,2304]{3,2,1,0:T(8,128)(2,1)}, bf16[1,1,2048,2304]{3,2,1,0:T(8,128)(2,1)}) fusion(f32[2048,2304]{1,0:T(8,128)} %fusion.192, f32[2048,2304]{1,0:T(8,128)} %get-tuple-element.269, bf16[1,2304,896]{2,1,0:T(8,128)(2,1)} %all-gather.34.cloned.1.call-done, bf16[1,1,2048,896]{2,3,1,0:T(8,128)(2,1)} %fusion.196), kind=kOutput, calls=%fused_computation.171 | convolution fusion | flops 8531214336 | bytes 64421888 | tf_op jit(solution)/vmap(transpose(jvp()))/dot_general | solution.py:9
  828.6 13.9 %fusion.148 = bf16[2048,896]{0,1:T(8,128)(2,1)} fusion(bf16[1,1,2048,2304]{3,2,1,0:T(8,128)(2,1)} %get-tuple-element.512, bf16[1,896,2304]{2,1,0:T(8,128)(2,1)} %all-gather.30.cloned.1.call-done), kind=kOutput, calls=%fused_computation.178 | convolution fusion | flops 8455716864 | bytes 17235968 | tf_op jit(solution)/vmap(transpose(jvp()))/dot_general | solution.py:20
  842.6 13.1 %fusion.175 = (bf16[1,1,2048,896]{2,3,1,0:T(8,128)(2,1)}, f32[2048]{0:T(1024)}, bf16[2048,896]{0,1:T(8,128)(2,1)}) fusion(bf16[1,2048,896]{1,2,0:T(8,128)(2,1)S(1)} %copy-done.22, f32[2048]{0:T(1024)S(1)} %bitcast.578, bf16[2048,896]{0,1:T(8,128)(2,1)} %fusion.148, bf16[1,896,2304]{2,1,0:T(8,128)(2,1)S(1)} %copy-done.38, ...), kind=kOutput, calls=%fused_computation.226 | convolution fusion | flops 8468559872 | bytes 28262400 | tf_op jit(solution)/vmap(transpose(jvp()))/dot_general | solution.py:21
  855.6 133.2 %while.15 = (bf16[1,1,2048,896]{2,3,1,0:T(8,128)(2,1)}, bf16[1,1,2048,2304]{3,2,1,0:T(8,128)(2,1)}, f32[1,56,2304]{2,1,0:T(8,128)S(1)}, f32[1,56,2304]{2,1,0:T(8...) while((bf16[1,1,2048,896]{2,3,1,0:T(8,128)(2,1)}, ...), condition=%wide.windowed_dot_general_cond_rs.3.clone, body=%wide.windowed_dot_general_body_rs.3.clone.sunk | while | flops 2116538368 | bytes 97223328 | solution.py:21
  876.5 10.6 collective-permute-done.14
  896.3 5.5 fusion.302
  910.8 9.2 collective-permute-done.14
  944.5 8.9 collective-permute-done.14
  977.5 9.2 collective-permute-done.14
  988.8 133.8 %while.12 = (bf16[1,1,2048,896]{2,3,1,0:T(8,128)(2,1)}, bf16[1,1,2048,2304]{3,2,1,0:T(8,128)(2,1)}, f32[1,56,2304]{2,1,0:T(8,128)S(1)}, f32[1,56,2304]{2,1,0:T(8...) while((bf16[1,1,2048,896]{2,3,1,0:T(8,128)(2,1)}, ...), condition=%wide.windowed_dot_general_cond_rs.clone, body=%wide.windowed_dot_general_body_rs.clone.sunk | while | flops 2116538368 | bytes 97223328 | solution.py:20
  1012.2 9.3 collective-permute-done.2
  1045.5 9.3 collective-permute-done.2
  1078.3 9.1 collective-permute-done.2
  1096.0 5.5 fusion.278
  1112.0 9.3 collective-permute-done.2
  1123.4 133.5 %while.13 = (bf16[1,1,2048,896]{2,3,1,0:T(8,128)(2,1)}, bf16[1,1,2048,2304]{3,2,1,0:T(8,128)(2,1)}, f32[1,56,2304]{2,1,0:T(8,128)S(1)}, f32[1,56,2304]{2,1,0:T(8...) while((bf16[1,1,2048,896]{2,3,1,0:T(8,128)(2,1)}, ...), condition=%wide.windowed_dot_general_cond_rs.1.clone, body=%wide.windowed_dot_general_body_rs.1.clone.sunk | while | flops 2116538368 | bytes 97223328 | solution.py:20
  1146.8 9.3 collective-permute-done.6
  1163.4 5.5 fusion.286
  1179.7 9.0 collective-permute-done.6
  1212.8 9.3 collective-permute-done.6
  1246.6 9.3 collective-permute-done.6
  1257.7 9.0 fusion.195
  1266.7 6.2 copy.6
  1276.3 8.0 collective-permute-done.24
  (514 shorter events, 540.8 us)
Async XLA Ops:
  7.2 53.7 %all-gather.30.cloned.1.call-start = ((), (), s32[]{:S(2)}) async-start(), calls=%async_computation | async-start | bytes 4386816 | tf_op jit(solution)/vmap(jvp())/squeeze | solution.py:27
  9.2 103.0 %all-gather.32.cloned.1.call-start = ((), (), s32[]{:S(2)}) async-start(), calls=%async_computation.1 | async-start | bytes 4386816 | tf_op jit(solution)/vmap(jvp())/squeeze | solution.py:27
  11.2 152.4 %all-gather.34.cloned.1.call-start = ((), (), s32[]{:S(2)}) async-start(), calls=%async_computation.2 | async-start | bytes 4386816 | tf_op jit(solution)/vmap(jvp())/squeeze | solution.py:27
  13.2 201.5 %all-gather.36.cloned.1.call-start = ((), (), s32[]{:S(2)}) async-start(), calls=%async_computation.3 | async-start | bytes 4386816 | tf_op jit(solution)/vmap(jvp())/squeeze | solution.py:27
  13.7 252.1 %all-gather.40.cloned.1.call-start = ((), (), s32[]{:S(2)}) async-start(), calls=%async_computation.5 | async-start | bytes 4386816 | tf_op jit(solution)/vmap(jvp())/squeeze | solution.py:27
  14.3 436.2 %all-gather.38.cloned.1.call-start = ((), (), s32[]{:S(2)}) async-start(), calls=%async_computation.4 | async-start | bytes 4386816 | tf_op jit(solution)/vmap(jvp())/squeeze | solution.py:27
  314.7 16.2 %collective-permute-start.16 = (f32[1,144,896]{2,1,0:T(8,128)S(1)}, f32[1,144,896]{2,1,0:T(8,128)S(1)}, u32[]{:S(2)}, u32[]{:S(2)}) collective-permute-start(f32[1,144,896]{2,1,0:T(8,128)S(1)} %broadcast_select_fusion.32), channel_id=39, source_target_pairs={{0,1},{1,2},{2,3},{3,4},{4,5},{5,6},{6,7},{7,8},{8,9},{9,10},{10,1... | collective-permute-start | bytes 1548296 | tf_op jit(solution)/vmap(transpose(jvp()))/dot_general | solution.py:9
  363.4 16.3 %collective-permute-start.18 = (f32[1,144,896]{2,1,0:T(8,128)S(1)}, f32[1,144,896]{2,1,0:T(8,128)S(1)}, u32[]{:S(2)}, u32[]{:S(2)}) collective-permute-start(f32[1,144,896]{2,1,0:T(8,128)S(1)} %get-tuple-element.498), channel_id=41, source_target_pairs={{0,1},{1,2},{2,3},{3,4},{4,5},{5,6},{6,7},{7,8},{8,9},{9,10},{10,1... | collective-permute-start | bytes 1548296 | tf_op jit(solution)/vmap(transpose(jvp()))/dot_general | solution.py:9
  363.5 16.2 %collective-permute-start.19 = (f32[1,144,896]{2,1,0:T(8,128)S(1)}, f32[1,144,896]{2,1,0:T(8,128)S(1)}, u32[]{:S(2)}, u32[]{:S(2)}) collective-permute-start(f32[1,144,896]{2,1,0:T(8,128)S(1)} %get-tuple-element.499), channel_id=40, source_target_pairs={{0,15},{1,0},{2,1},{3,2},{4,3},{5,4},{6,5},{7,6},{8,7},{9,8},{10,9... | collective-permute-start | bytes 1548296 | tf_op jit(solution)/vmap(transpose(jvp()))/dot_general | solution.py:9
  381.7 16.7 %collective-permute-start.16 = (f32[1,144,896]{2,1,0:T(8,128)S(1)}, f32[1,144,896]{2,1,0:T(8,128)S(1)}, u32[]{:S(2)}, u32[]{:S(2)}) collective-permute-start(f32[1,144,896]{2,1,0:T(8,128)S(1)} %broadcast_select_fusion.32), channel_id=39, source_target_pairs={{0,1},{1,2},{2,3},{3,4},{4,5},{5,6},{6,7},{7,8},{8,9},{9,10},{10,1... | collective-permute-start | bytes 1548296 | tf_op jit(solution)/vmap(transpose(jvp()))/dot_general | solution.py:9
  381.8 16.5 %collective-permute-start.17 = (f32[1,144,896]{2,1,0:T(8,128)S(1)}, f32[1,144,896]{2,1,0:T(8,128)S(1)}, u32[]{:S(2)}, u32[]{:S(2)}) collective-permute-start(f32[1,144,896]{2,1,0:T(8,128)S(1)} %broadcast_select_fusion.33), channel_id=38, source_target_pairs={{0,15},{1,0},{2,1},{3,2},{4,3},{5,4},{6,5},{7,6},{8,7},{9,8},{10,9... | collective-permute-start | bytes 1548296 | tf_op jit(solution)/vmap(transpose(jvp()))/dot_general | solution.py:9
  398.5 16.5 %collective-permute-start.18 = (f32[1,144,896]{2,1,0:T(8,128)S(1)}, f32[1,144,896]{2,1,0:T(8,128)S(1)}, u32[]{:S(2)}, u32[]{:S(2)}) collective-permute-start(f32[1,144,896]{2,1,0:T(8,128)S(1)} %get-tuple-element.498), channel_id=41, source_target_pairs={{0,1},{1,2},{2,3},{3,4},{4,5},{5,6},{6,7},{7,8},{8,9},{9,10},{10,1... | collective-permute-start | bytes 1548296 | tf_op jit(solution)/vmap(transpose(jvp()))/dot_general | solution.py:9
  398.6 16.4 %collective-permute-start.19 = (f32[1,144,896]{2,1,0:T(8,128)S(1)}, f32[1,144,896]{2,1,0:T(8,128)S(1)}, u32[]{:S(2)}, u32[]{:S(2)}) collective-permute-start(f32[1,144,896]{2,1,0:T(8,128)S(1)} %get-tuple-element.499), channel_id=40, source_target_pairs={{0,15},{1,0},{2,1},{3,2},{4,3},{5,4},{6,5},{7,6},{8,7},{9,8},{10,9... | collective-permute-start | bytes 1548296 | tf_op jit(solution)/vmap(transpose(jvp()))/dot_general | solution.py:9
  433.1 16.5 %collective-permute-start.18 = (f32[1,144,896]{2,1,0:T(8,128)S(1)}, f32[1,144,896]{2,1,0:T(8,128)S(1)}, u32[]{:S(2)}, u32[]{:S(2)}) collective-permute-start(f32[1,144,896]{2,1,0:T(8,128)S(1)} %get-tuple-element.498), channel_id=41, source_target_pairs={{0,1},{1,2},{2,3},{3,4},{4,5},{5,6},{6,7},{7,8},{8,9},{9,10},{10,1... | collective-permute-start | bytes 1548296 | tf_op jit(solution)/vmap(transpose(jvp()))/dot_general | solution.py:9
  433.2 16.4 %collective-permute-start.19 = (f32[1,144,896]{2,1,0:T(8,128)S(1)}, f32[1,144,896]{2,1,0:T(8,128)S(1)}, u32[]{:S(2)}, u32[]{:S(2)}) collective-permute-start(f32[1,144,896]{2,1,0:T(8,128)S(1)} %get-tuple-element.499), channel_id=40, source_target_pairs={{0,15},{1,0},{2,1},{3,2},{4,3},{5,4},{6,5},{7,6},{8,7},{9,8},{10,9... | collective-permute-start | bytes 1548296 | tf_op jit(solution)/vmap(transpose(jvp()))/dot_general | solution.py:9
  450.5 822.3 %collective-permute-start.28 = (f32[1,144,896]{2,1,0:T(8,128)}, f32[1,144,896]{2,1,0:T(8,128)}, u32[]{:S(2)}, u32[]{:S(2)}) collective-permute-start(f32[1,144,896]{2,1,0:T(8,128)} %get-tuple-element.45), channel_id=42, source_target_pairs={{0,1},{1,2},{2,3},{3,4},{4,5},{5,6},{6,7},{7,8},{8,9},{9,10},{10,1... | collective-permute-start | bytes 1548296 | tf_op jit(solution)/vmap(transpose(jvp()))/dot_general | solution.py:9
  533.2 16.3 %collective-permute-start.22 = (f32[1,144,896]{2,1,0:T(8,128)S(1)}, f32[1,144,896]{2,1,0:T(8,128)S(1)}, u32[]{:S(2)}, u32[]{:S(2)}) collective-permute-start(f32[1,144,896]{2,1,0:T(8,128)S(1)} %get-tuple-element.507), channel_id=47, source_target_pairs={{0,1},{1,2},{2,3},{3,4},{4,5},{5,6},{6,7},{7,8},{8,9},{9,10},{10,1... | collective-permute-start | bytes 1548296 | tf_op jit(solution)/vmap(transpose(jvp()))/dot_general | solution.py:9
  533.3 16.2 %collective-permute-start.23 = (f32[1,144,896]{2,1,0:T(8,128)S(1)}, f32[1,144,896]{2,1,0:T(8,128)S(1)}, u32[]{:S(2)}, u32[]{:S(2)}) collective-permute-start(f32[1,144,896]{2,1,0:T(8,128)S(1)} %get-tuple-element.508), channel_id=46, source_target_pairs={{0,15},{1,0},{2,1},{3,2},{4,3},{5,4},{6,5},{7,6},{8,7},{9,8},{10,9... | collective-permute-start | bytes 1548296 | tf_op jit(solution)/vmap(transpose(jvp()))/dot_general | solution.py:9
  551.6 16.5 %collective-permute-start.20 = (f32[1,144,896]{2,1,0:T(8,128)S(1)}, f32[1,144,896]{2,1,0:T(8,128)S(1)}, u32[]{:S(2)}, u32[]{:S(2)}) collective-permute-start(f32[1,144,896]{2,1,0:T(8,128)S(1)} %broadcast_select_fusion.34), channel_id=45, source_target_pairs={{0,1},{1,2},{2,3},{3,4},{4,5},{5,6},{6,7},{7,8},{8,9},{9,10},{10,1... | collective-permute-start | bytes 1548296 | tf_op jit(solution)/vmap(transpose(jvp()))/dot_general | solution.py:9
  551.7 16.4 %collective-permute-start.21 = (f32[1,144,896]{2,1,0:T(8,128)S(1)}, f32[1,144,896]{2,1,0:T(8,128)S(1)}, u32[]{:S(2)}, u32[]{:S(2)}) collective-permute-start(f32[1,144,896]{2,1,0:T(8,128)S(1)} %broadcast_select_fusion.35), channel_id=44, source_target_pairs={{0,15},{1,0},{2,1},{3,2},{4,3},{5,4},{6,5},{7,6},{8,7},{9,8},{10,9... | collective-permute-start | bytes 1548296 | tf_op jit(solution)/vmap(transpose(jvp()))/dot_general | solution.py:9
  568.2 16.4 %collective-permute-start.22 = (f32[1,144,896]{2,1,0:T(8,128)S(1)}, f32[1,144,896]{2,1,0:T(8,128)S(1)}, u32[]{:S(2)}, u32[]{:S(2)}) collective-permute-start(f32[1,144,896]{2,1,0:T(8,128)S(1)} %get-tuple-element.507), channel_id=47, source_target_pairs={{0,1},{1,2},{2,3},{3,4},{4,5},{5,6},{6,7},{7,8},{8,9},{9,10},{10,1... | collective-permute-start | bytes 1548296 | tf_op jit(solution)/vmap(transpose(jvp()))/dot_general | solution.py:9
  568.3 16.3 %collective-permute-start.23 = (f32[1,144,896]{2,1,0:T(8,128)S(1)}, f32[1,144,896]{2,1,0:T(8,128)S(1)}, u32[]{:S(2)}, u32[]{:S(2)}) collective-permute-start(f32[1,144,896]{2,1,0:T(8,128)S(1)} %get-tuple-element.508), channel_id=46, source_target_pairs={{0,15},{1,0},{2,1},{3,2},{4,3},{5,4},{6,5},{7,6},{8,7},{9,8},{10,9... | collective-permute-start | bytes 1548296 | tf_op jit(solution)/vmap(transpose(jvp()))/dot_general | solution.py:9
  602.8 16.6 %collective-permute-start.22 = (f32[1,144,896]{2,1,0:T(8,128)S(1)}, f32[1,144,896]{2,1,0:T(8,128)S(1)}, u32[]{:S(2)}, u32[]{:S(2)}) collective-permute-start(f32[1,144,896]{2,1,0:T(8,128)S(1)} %get-tuple-element.507), channel_id=47, source_target_pairs={{0,1},{1,2},{2,3},{3,4},{4,5},{5,6},{6,7},{7,8},{8,9},{9,10},{10,1... | collective-permute-start | bytes 1548296 | tf_op jit(solution)/vmap(transpose(jvp()))/dot_general | solution.py:9
  602.9 16.6 %collective-permute-start.23 = (f32[1,144,896]{2,1,0:T(8,128)S(1)}, f32[1,144,896]{2,1,0:T(8,128)S(1)}, u32[]{:S(2)}, u32[]{:S(2)}) collective-permute-start(f32[1,144,896]{2,1,0:T(8,128)S(1)} %get-tuple-element.508), channel_id=46, source_target_pairs={{0,15},{1,0},{2,1},{3,2},{4,3},{5,4},{6,5},{7,6},{8,7},{9,8},{10,9... | collective-permute-start | bytes 1548296 | tf_op jit(solution)/vmap(transpose(jvp()))/dot_general | solution.py:9
  637.4 16.4 %collective-permute-start.22 = (f32[1,144,896]{2,1,0:T(8,128)S(1)}, f32[1,144,896]{2,1,0:T(8,128)S(1)}, u32[]{:S(2)}, u32[]{:S(2)}) collective-permute-start(f32[1,144,896]{2,1,0:T(8,128)S(1)} %get-tuple-element.507), channel_id=47, source_target_pairs={{0,1},{1,2},{2,3},{3,4},{4,5},{5,6},{6,7},{7,8},{8,9},{9,10},{10,1... | collective-permute-start | bytes 1548296 | tf_op jit(solution)/vmap(transpose(jvp()))/dot_general | solution.py:9
  637.4 16.3 %collective-permute-start.23 = (f32[1,144,896]{2,1,0:T(8,128)S(1)}, f32[1,144,896]{2,1,0:T(8,128)S(1)}, u32[]{:S(2)}, u32[]{:S(2)}) collective-permute-start(f32[1,144,896]{2,1,0:T(8,128)S(1)} %get-tuple-element.508), channel_id=46, source_target_pairs={{0,15},{1,0},{2,1},{3,2},{4,3},{5,4},{6,5},{7,6},{8,7},{9,8},{10,9... | collective-permute-start | bytes 1548296 | tf_op jit(solution)/vmap(transpose(jvp()))/dot_general | solution.py:9
  654.8 629.6 %collective-permute-start.29 = (f32[1,144,896]{2,1,0:T(8,128)}, f32[1,144,896]{2,1,0:T(8,128)}, u32[]{:S(2)}, u32[]{:S(2)}) collective-permute-start(f32[1,144,896]{2,1,0:T(8,128)} %get-tuple-element.47), channel_id=48, source_target_pairs={{0,1},{1,2},{2,3},{3,4},{4,5},{5,6},{6,7},{7,8},{8,9},{9,10},{10,1... | collective-permute-start | bytes 1548296 | tf_op jit(solution)/vmap(transpose(jvp()))/dot_general | solution.py:9
  655.6 21.4 %collective-permute-start.8 = (f32[1,56,2304]{2,1,0:T(8,128)S(1)}, f32[1,56,2304]{2,1,0:T(8,128)S(1)}, u32[]{:S(2)}, u32[]{:S(2)}) collective-permute-start(f32[1,56,2304]{2,1,0:T(8,128)S(1)} %broadcast_select_fusion.28), channel_id=27, source_target_pairs={{0,1},{1,2},{2,3},{3,4},{4,5},{5,6},{6,7},{7,8},{8,9},{9,10},{10,1... | collective-permute-start | bytes 1548296 | tf_op jit(solution)/vmap(transpose(jvp()))/dot_general | solution.py:21
  655.8 21.3 %collective-permute-start.9 = (f32[1,56,2304]{2,1,0:T(8,128)S(1)}, f32[1,56,2304]{2,1,0:T(8,128)S(1)}, u32[]{:S(2)}, u32[]{:S(2)}) collective-permute-start(f32[1,56,2304]{2,1,0:T(8,128)S(1)} %broadcast_select_fusion.29), channel_id=26, source_target_pairs={{0,15},{1,0},{2,1},{3,2},{4,3},{5,4},{6,5},{7,6},{8,7},{9,8},{10,9... | collective-permute-start | bytes 1548296 | tf_op jit(solution)/vmap(transpose(jvp()))/dot_general | solution.py:21
  695.0 16.2 %collective-permute-start.8 = (f32[1,56,2304]{2,1,0:T(8,128)S(1)}, f32[1,56,2304]{2,1,0:T(8,128)S(1)}, u32[]{:S(2)}, u32[]{:S(2)}) collective-permute-start(f32[1,56,2304]{2,1,0:T(8,128)S(1)} %broadcast_select_fusion.28), channel_id=27, source_target_pairs={{0,1},{1,2},{2,3},{3,4},{4,5},{5,6},{6,7},{7,8},{8,9},{9,10},{10,1... | collective-permute-start | bytes 1548296 | tf_op jit(solution)/vmap(transpose(jvp()))/dot_general | solution.py:21
  695.1 16.1 %collective-permute-start.9 = (f32[1,56,2304]{2,1,0:T(8,128)S(1)}, f32[1,56,2304]{2,1,0:T(8,128)S(1)}, u32[]{:S(2)}, u32[]{:S(2)}) collective-permute-start(f32[1,56,2304]{2,1,0:T(8,128)S(1)} %broadcast_select_fusion.29), channel_id=26, source_target_pairs={{0,15},{1,0},{2,1},{3,2},{4,3},{5,4},{6,5},{7,6},{8,7},{9,8},{10,9... | collective-permute-start | bytes 1548296 | tf_op jit(solution)/vmap(transpose(jvp()))/dot_general | solution.py:21
  711.4 16.3 %collective-permute-start.11 = (f32[1,56,2304]{2,1,0:T(8,128)S(1)}, f32[1,56,2304]{2,1,0:T(8,128)S(1)}, u32[]{:S(2)}, u32[]{:S(2)}) collective-permute-start(f32[1,56,2304]{2,1,0:T(8,128)S(1)} %get-tuple-element.481), channel_id=28, source_target_pairs={{0,15},{1,0},{2,1},{3,2},{4,3},{5,4},{6,5},{7,6},{8,7},{9,8},{10,9... | collective-permute-start | bytes 1548296 | tf_op jit(solution)/vmap(transpose(jvp()))/dot_general | solution.py:21
  729.9 16.2 %collective-permute-start.8 = (f32[1,56,2304]{2,1,0:T(8,128)S(1)}, f32[1,56,2304]{2,1,0:T(8,128)S(1)}, u32[]{:S(2)}, u32[]{:S(2)}) collective-permute-start(f32[1,56,2304]{2,1,0:T(8,128)S(1)} %broadcast_select_fusion.28), channel_id=27, source_target_pairs={{0,1},{1,2},{2,3},{3,4},{4,5},{5,6},{6,7},{7,8},{8,9},{9,10},{10,1... | collective-permute-start | bytes 1548296 | tf_op jit(solution)/vmap(transpose(jvp()))/dot_general | solution.py:21
  730.0 16.1 %collective-permute-start.9 = (f32[1,56,2304]{2,1,0:T(8,128)S(1)}, f32[1,56,2304]{2,1,0:T(8,128)S(1)}, u32[]{:S(2)}, u32[]{:S(2)}) collective-permute-start(f32[1,56,2304]{2,1,0:T(8,128)S(1)} %broadcast_select_fusion.29), channel_id=26, source_target_pairs={{0,15},{1,0},{2,1},{3,2},{4,3},{5,4},{6,5},{7,6},{8,7},{9,8},{10,9... | collective-permute-start | bytes 1548296 | tf_op jit(solution)/vmap(transpose(jvp()))/dot_general | solution.py:21
  746.3 16.4 %collective-permute-start.11 = (f32[1,56,2304]{2,1,0:T(8,128)S(1)}, f32[1,56,2304]{2,1,0:T(8,128)S(1)}, u32[]{:S(2)}, u32[]{:S(2)}) collective-permute-start(f32[1,56,2304]{2,1,0:T(8,128)S(1)} %get-tuple-element.481), channel_id=28, source_target_pairs={{0,15},{1,0},{2,1},{3,2},{4,3},{5,4},{6,5},{7,6},{8,7},{9,8},{10,9... | collective-permute-start | bytes 1548296 | tf_op jit(solution)/vmap(transpose(jvp()))/dot_general | solution.py:21
  764.8 16.2 %collective-permute-start.8 = (f32[1,56,2304]{2,1,0:T(8,128)S(1)}, f32[1,56,2304]{2,1,0:T(8,128)S(1)}, u32[]{:S(2)}, u32[]{:S(2)}) collective-permute-start(f32[1,56,2304]{2,1,0:T(8,128)S(1)} %broadcast_select_fusion.28), channel_id=27, source_target_pairs={{0,1},{1,2},{2,3},{3,4},{4,5},{5,6},{6,7},{7,8},{8,9},{9,10},{10,1... | collective-permute-start | bytes 1548296 | tf_op jit(solution)/vmap(transpose(jvp()))/dot_general | solution.py:21
  764.9 16.1 %collective-permute-start.9 = (f32[1,56,2304]{2,1,0:T(8,128)S(1)}, f32[1,56,2304]{2,1,0:T(8,128)S(1)}, u32[]{:S(2)}, u32[]{:S(2)}) collective-permute-start(f32[1,56,2304]{2,1,0:T(8,128)S(1)} %broadcast_select_fusion.29), channel_id=26, source_target_pairs={{0,15},{1,0},{2,1},{3,2},{4,3},{5,4},{6,5},{7,6},{8,7},{9,8},{10,9... | collective-permute-start | bytes 1548296 | tf_op jit(solution)/vmap(transpose(jvp()))/dot_general | solution.py:21
  797.7 476.3 %collective-permute-start.26 = (f32[1,56,2304]{2,1,0:T(8,128)}, f32[1,56,2304]{2,1,0:T(8,128)}, u32[]{:S(2)}, u32[]{:S(2)}) collective-permute-start(f32[1,56,2304]{2,1,0:T(8,128)} %get-tuple-element.41), channel_id=30, source_target_pairs={{0,1},{1,2},{2,3},{3,4},{4,5},{5,6},{6,7},{7,8},{8,9},{9,10},{10,1... | collective-permute-start | bytes 1548296 | tf_op jit(solution)/vmap(transpose(jvp()))/dot_general | solution.py:21
  870.5 16.6 %collective-permute-start.14 = (f32[1,56,2304]{2,1,0:T(8,128)S(1)}, f32[1,56,2304]{2,1,0:T(8,128)S(1)}, u32[]{:S(2)}, u32[]{:S(2)}) collective-permute-start(f32[1,56,2304]{2,1,0:T(8,128)S(1)} %get-tuple-element.489), channel_id=35, source_target_pairs={{0,1},{1,2},{2,3},{3,4},{4,5},{5,6},{6,7},{7,8},{8,9},{9,10},{10,1... | collective-permute-start | bytes 1548296 | tf_op jit(solution)/vmap(transpose(jvp()))/dot_general | solution.py:21
  870.6 16.6 %collective-permute-start.15 = (f32[1,56,2304]{2,1,0:T(8,128)S(1)}, f32[1,56,2304]{2,1,0:T(8,128)S(1)}, u32[]{:S(2)}, u32[]{:S(2)}) collective-permute-start(f32[1,56,2304]{2,1,0:T(8,128)S(1)} %get-tuple-element.490), channel_id=34, source_target_pairs={{0,15},{1,0},{2,1},{3,2},{4,3},{5,4},{6,5},{7,6},{8,7},{9,8},{10,9... | collective-permute-start | bytes 1548296 | tf_op jit(solution)/vmap(transpose(jvp()))/dot_general | solution.py:21
  921.9 16.4 %collective-permute-start.12 = (f32[1,56,2304]{2,1,0:T(8,128)S(1)}, f32[1,56,2304]{2,1,0:T(8,128)S(1)}, u32[]{:S(2)}, u32[]{:S(2)}) collective-permute-start(f32[1,56,2304]{2,1,0:T(8,128)S(1)} %broadcast_select_fusion.30), channel_id=33, source_target_pairs={{0,1},{1,2},{2,3},{3,4},{4,5},{5,6},{6,7},{7,8},{8,9},{9,10},{10,1... | collective-permute-start | bytes 1548296 | tf_op jit(solution)/vmap(transpose(jvp()))/dot_general | solution.py:21
  922.1 16.3 %collective-permute-start.13 = (f32[1,56,2304]{2,1,0:T(8,128)S(1)}, f32[1,56,2304]{2,1,0:T(8,128)S(1)}, u32[]{:S(2)}, u32[]{:S(2)}) collective-permute-start(f32[1,56,2304]{2,1,0:T(8,128)S(1)} %broadcast_select_fusion.31), channel_id=32, source_target_pairs={{0,15},{1,0},{2,1},{3,2},{4,3},{5,4},{6,5},{7,6},{8,7},{9,8},{10,9... | collective-permute-start | bytes 1548296 | tf_op jit(solution)/vmap(transpose(jvp()))/dot_general | solution.py:21
  955.3 16.1 %collective-permute-start.12 = (f32[1,56,2304]{2,1,0:T(8,128)S(1)}, f32[1,56,2304]{2,1,0:T(8,128)S(1)}, u32[]{:S(2)}, u32[]{:S(2)}) collective-permute-start(f32[1,56,2304]{2,1,0:T(8,128)S(1)} %broadcast_select_fusion.30), channel_id=33, source_target_pairs={{0,1},{1,2},{2,3},{3,4},{4,5},{5,6},{6,7},{7,8},{8,9},{9,10},{10,1... | collective-permute-start | bytes 1548296 | tf_op jit(solution)/vmap(transpose(jvp()))/dot_general | solution.py:21
  971.6 16.3 %collective-permute-start.15 = (f32[1,56,2304]{2,1,0:T(8,128)S(1)}, f32[1,56,2304]{2,1,0:T(8,128)S(1)}, u32[]{:S(2)}, u32[]{:S(2)}) collective-permute-start(f32[1,56,2304]{2,1,0:T(8,128)S(1)} %get-tuple-element.490), channel_id=34, source_target_pairs={{0,15},{1,0},{2,1},{3,2},{4,3},{5,4},{6,5},{7,6},{8,7},{9,8},{10,9... | collective-permute-start | bytes 1548296 | tf_op jit(solution)/vmap(transpose(jvp()))/dot_general | solution.py:21
  988.9 16.2 %collective-permute-start = (f32[1,56,2304]{2,1,0:T(8,128)S(1)}, f32[1,56,2304]{2,1,0:T(8,128)}, u32[]{:S(2)}, u32[]{:S(2)}) collective-permute-start(f32[1,56,2304]{2,1,0:T(8,128)S(1)} %broadcast_select_fusion.24), channel_id=15, source_target_pairs={{0,1},{1,2},{2,3},{3,4},{4,5},{5,6},{6,7},{7,8},{8,9},{9,10},{10,1... | collective-permute-start | bytes 1548296 | tf_op jit(solution)/vmap(transpose(jvp()))/dot_general | solution.py:20
  989.0 16.1 %collective-permute-start.1 = (f32[1,56,2304]{2,1,0:T(8,128)S(1)}, f32[1,56,2304]{2,1,0:T(8,128)S(1)}, u32[]{:S(2)}, u32[]{:S(2)}) collective-permute-start(f32[1,56,2304]{2,1,0:T(8,128)S(1)} %broadcast_select_fusion.25), channel_id=14, source_target_pairs={{0,15},{1,0},{2,1},{3,2},{4,3},{5,4},{6,5},{7,6},{8,7},{9,8},{10,9... | collective-permute-start | bytes 1548296 | tf_op jit(solution)/vmap(transpose(jvp()))/dot_general | solution.py:20
  1022.1 16.2 %collective-permute-start = (f32[1,56,2304]{2,1,0:T(8,128)S(1)}, f32[1,56,2304]{2,1,0:T(8,128)}, u32[]{:S(2)}, u32[]{:S(2)}) collective-permute-start(f32[1,56,2304]{2,1,0:T(8,128)S(1)} %broadcast_select_fusion.24), channel_id=15, source_target_pairs={{0,1},{1,2},{2,3},{3,4},{4,5},{5,6},{6,7},{7,8},{8,9},{9,10},{10,1... | collective-permute-start | bytes 1548296 | tf_op jit(solution)/vmap(transpose(jvp()))/dot_general | solution.py:20
  1022.2 16.1 %collective-permute-start.1 = (f32[1,56,2304]{2,1,0:T(8,128)S(1)}, f32[1,56,2304]{2,1,0:T(8,128)S(1)}, u32[]{:S(2)}, u32[]{:S(2)}) collective-permute-start(f32[1,56,2304]{2,1,0:T(8,128)S(1)} %broadcast_select_fusion.25), channel_id=14, source_target_pairs={{0,15},{1,0},{2,1},{3,2},{4,3},{5,4},{6,5},{7,6},{8,7},{9,8},{10,9... | collective-permute-start | bytes 1548296 | tf_op jit(solution)/vmap(transpose(jvp()))/dot_general | solution.py:20
  1055.0 16.2 %collective-permute-start = (f32[1,56,2304]{2,1,0:T(8,128)S(1)}, f32[1,56,2304]{2,1,0:T(8,128)}, u32[]{:S(2)}, u32[]{:S(2)}) collective-permute-start(f32[1,56,2304]{2,1,0:T(8,128)S(1)} %broadcast_select_fusion.24), channel_id=15, source_target_pairs={{0,1},{1,2},{2,3},{3,4},{4,5},{5,6},{6,7},{7,8},{8,9},{9,10},{10,1... | collective-permute-start | bytes 1548296 | tf_op jit(solution)/vmap(transpose(jvp()))/dot_general | solution.py:20
  1055.1 16.1 %collective-permute-start.1 = (f32[1,56,2304]{2,1,0:T(8,128)S(1)}, f32[1,56,2304]{2,1,0:T(8,128)S(1)}, u32[]{:S(2)}, u32[]{:S(2)}) collective-permute-start(f32[1,56,2304]{2,1,0:T(8,128)S(1)} %broadcast_select_fusion.25), channel_id=14, source_target_pairs={{0,15},{1,0},{2,1},{3,2},{4,3},{5,4},{6,5},{7,6},{8,7},{9,8},{10,9... | collective-permute-start | bytes 1548296 | tf_op jit(solution)/vmap(transpose(jvp()))/dot_general | solution.py:20
  1088.6 16.2 %collective-permute-start = (f32[1,56,2304]{2,1,0:T(8,128)S(1)}, f32[1,56,2304]{2,1,0:T(8,128)}, u32[]{:S(2)}, u32[]{:S(2)}) collective-permute-start(f32[1,56,2304]{2,1,0:T(8,128)S(1)} %broadcast_select_fusion.24), channel_id=15, source_target_pairs={{0,1},{1,2},{2,3},{3,4},{4,5},{5,6},{6,7},{7,8},{8,9},{9,10},{10,1... | collective-permute-start | bytes 1548296 | tf_op jit(solution)/vmap(transpose(jvp()))/dot_general | solution.py:20
  1088.7 16.1 %collective-permute-start.1 = (f32[1,56,2304]{2,1,0:T(8,128)S(1)}, f32[1,56,2304]{2,1,0:T(8,128)S(1)}, u32[]{:S(2)}, u32[]{:S(2)}) collective-permute-start(f32[1,56,2304]{2,1,0:T(8,128)S(1)} %broadcast_select_fusion.25), channel_id=14, source_target_pairs={{0,15},{1,0},{2,1},{3,2},{4,3},{5,4},{6,5},{7,6},{8,7},{9,8},{10,9... | collective-permute-start | bytes 1548296 | tf_op jit(solution)/vmap(transpose(jvp()))/dot_general | solution.py:20
  1106.1 16.3 %collective-permute-start.3 = (f32[1,56,2304]{2,1,0:T(8,128)S(1)}, f32[1,56,2304]{2,1,0:T(8,128)S(1)}, u32[]{:S(2)}, u32[]{:S(2)}) collective-permute-start(f32[1,56,2304]{2,1,0:T(8,128)S(1)} %get-tuple-element.463), channel_id=16, source_target_pairs={{0,15},{1,0},{2,1},{3,2},{4,3},{5,4},{6,5},{7,6},{8,7},{9,8},{10,9... | collective-permute-start | bytes 1548296 | tf_op jit(solution)/vmap(transpose(jvp()))/dot_general | solution.py:20
  1123.4 16.2 %collective-permute-start.4 = (f32[1,56,2304]{2,1,0:T(8,128)S(1)}, f32[1,56,2304]{2,1,0:T(8,128)}, u32[]{:S(2)}, u32[]{:S(2)}) collective-permute-start(f32[1,56,2304]{2,1,0:T(8,128)S(1)} %broadcast_select_fusion.26), channel_id=21, source_target_pairs={{0,1},{1,2},{2,3},{3,4},{4,5},{5,6},{6,7},{7,8},{8,9},{9,10},{10,1... | collective-permute-start | bytes 1548296 | tf_op jit(solution)/vmap(transpose(jvp()))/dot_general | solution.py:20
  1123.5 16.1 %collective-permute-start.5 = (f32[1,56,2304]{2,1,0:T(8,128)S(1)}, f32[1,56,2304]{2,1,0:T(8,128)S(1)}, u32[]{:S(2)}, u32[]{:S(2)}) collective-permute-start(f32[1,56,2304]{2,1,0:T(8,128)S(1)} %broadcast_select_fusion.27), channel_id=20, source_target_pairs={{0,15},{1,0},{2,1},{3,2},{4,3},{5,4},{6,5},{7,6},{8,7},{9,8},{10,9... | collective-permute-start | bytes 1548296 | tf_op jit(solution)/vmap(transpose(jvp()))/dot_general | solution.py:20
  1156.2 16.3 %collective-permute-start.4 = (f32[1,56,2304]{2,1,0:T(8,128)S(1)}, f32[1,56,2304]{2,1,0:T(8,128)}, u32[]{:S(2)}, u32[]{:S(2)}) collective-permute-start(f32[1,56,2304]{2,1,0:T(8,128)S(1)} %broadcast_select_fusion.26), channel_id=21, source_target_pairs={{0,1},{1,2},{2,3},{3,4},{4,5},{5,6},{6,7},{7,8},{8,9},{9,10},{10,1... | collective-permute-start | bytes 1548296 | tf_op jit(solution)/vmap(transpose(jvp()))/dot_general | solution.py:20
  1156.4 16.2 %collective-permute-start.5 = (f32[1,56,2304]{2,1,0:T(8,128)S(1)}, f32[1,56,2304]{2,1,0:T(8,128)S(1)}, u32[]{:S(2)}, u32[]{:S(2)}) collective-permute-start(f32[1,56,2304]{2,1,0:T(8,128)S(1)} %broadcast_select_fusion.27), channel_id=20, source_target_pairs={{0,15},{1,0},{2,1},{3,2},{4,3},{5,4},{6,5},{7,6},{8,7},{9,8},{10,9... | collective-permute-start | bytes 1548296 | tf_op jit(solution)/vmap(transpose(jvp()))/dot_general | solution.py:20
  1189.5 16.2 %collective-permute-start.4 = (f32[1,56,2304]{2,1,0:T(8,128)S(1)}, f32[1,56,2304]{2,1,0:T(8,128)}, u32[]{:S(2)}, u32[]{:S(2)}) collective-permute-start(f32[1,56,2304]{2,1,0:T(8,128)S(1)} %broadcast_select_fusion.26), channel_id=21, source_target_pairs={{0,1},{1,2},{2,3},{3,4},{4,5},{5,6},{6,7},{7,8},{8,9},{9,10},{10,1... | collective-permute-start | bytes 1548296 | tf_op jit(solution)/vmap(transpose(jvp()))/dot_general | solution.py:20
  1189.6 16.1 %collective-permute-start.5 = (f32[1,56,2304]{2,1,0:T(8,128)S(1)}, f32[1,56,2304]{2,1,0:T(8,128)S(1)}, u32[]{:S(2)}, u32[]{:S(2)}) collective-permute-start(f32[1,56,2304]{2,1,0:T(8,128)S(1)} %broadcast_select_fusion.27), channel_id=20, source_target_pairs={{0,15},{1,0},{2,1},{3,2},{4,3},{5,4},{6,5},{7,6},{8,7},{9,8},{10,9... | collective-permute-start | bytes 1548296 | tf_op jit(solution)/vmap(transpose(jvp()))/dot_general | solution.py:20
  1206.9 16.1 %collective-permute-start.7 = (f32[1,56,2304]{2,1,0:T(8,128)S(1)}, f32[1,56,2304]{2,1,0:T(8,128)S(1)}, u32[]{:S(2)}, u32[]{:S(2)}) collective-permute-start(f32[1,56,2304]{2,1,0:T(8,128)S(1)} %get-tuple-element.472), channel_id=22, source_target_pairs={{0,15},{1,0},{2,1},{3,2},{4,3},{5,4},{6,5},{7,6},{8,7},{9,8},{10,9... | collective-permute-start | bytes 1548296 | tf_op jit(solution)/vmap(transpose(jvp()))/dot_general | solution.py:20
  1223.2 16.2 %collective-permute-start.4 = (f32[1,56,2304]{2,1,0:T(8,128)S(1)}, f32[1,56,2304]{2,1,0:T(8,128)}, u32[]{:S(2)}, u32[]{:S(2)}) collective-permute-start(f32[1,56,2304]{2,1,0:T(8,128)S(1)} %broadcast_select_fusion.26), channel_id=21, source_target_pairs={{0,1},{1,2},{2,3},{3,4},{4,5},{5,6},{6,7},{7,8},{8,9},{9,10},{10,1... | collective-permute-start | bytes 1548296 | tf_op jit(solution)/vmap(transpose(jvp()))/dot_general | solution.py:20
  1223.3 16.1 %collective-permute-start.5 = (f32[1,56,2304]{2,1,0:T(8,128)S(1)}, f32[1,56,2304]{2,1,0:T(8,128)S(1)}, u32[]{:S(2)}, u32[]{:S(2)}) collective-permute-start(f32[1,56,2304]{2,1,0:T(8,128)S(1)} %broadcast_select_fusion.27), channel_id=20, source_target_pairs={{0,15},{1,0},{2,1},{3,2},{4,3},{5,4},{6,5},{7,6},{8,7},{9,8},{10,9... | collective-permute-start | bytes 1548296 | tf_op jit(solution)/vmap(transpose(jvp()))/dot_general | solution.py:20
  1256.9 18.3 %collective-permute-start.27 = (f32[1,56,2304]{2,1,0:T(8,128)}, f32[1,56,2304]{2,1,0:T(8,128)}, u32[]{:S(2)}, u32[]{:S(2)}) collective-permute-start(f32[1,56,2304]{2,1,0:T(8,128)} %get-tuple-element.43), channel_id=36, source_target_pairs={{0,1},{1,2},{2,3},{3,4},{4,5},{5,6},{6,7},{7,8},{8,9},{9,10},{10,1... | collective-permute-start | bytes 1548296 | tf_op jit(solution)/vmap(transpose(jvp()))/dot_general | solution.py:21
  1272.9 16.9 %collective-permute-start.25 = (f32[1,56,2304]{2,1,0:T(8,128)}, f32[1,56,2304]{2,1,0:T(8,128)S(1)}, u32[]{:S(2)}, u32[]{:S(2)}) collective-permute-start(f32[1,56,2304]{2,1,0:T(8,128)} %copy-done.26), channel_id=24, source_target_pairs={{0,1},{1,2},{2,3},{3,4},{4,5},{5,6},{6,7},{7,8},{8,9},{9,10},{10,1... | collective-permute-start | bytes 1548296 | tf_op jit(solution)/vmap(transpose(jvp()))/dot_general | solution.py:20
  (109 other events, 2478.4 us)
Sparse Core Ops, SparseCore 0:
  10.2 50.6 all-gather.29
  63.1 49.0 all-gather.31
  114.4 49.0 all-gather.33
  165.6 49.0 all-gather.35
  216.8 49.0 all-gather.39
  267.9 49.2 all-gather.37
where the time goes:
time: 1310 us; the launch traced here: 1300 us
  waiting for transfers between devices  487 us (37%)
  matrix products  378 us (29%)
  starting transfers between devices  220 us (17%)
  local copies, waits for them, and re-layouts  80.8 us (6%)
  other arithmetic  68.8 us (5%)
  loops' own time  48.7 us (4%)
  between operations  15 us (1%)
    squeeze x6, waiting for transfers between devices, stack(): h = layer(h, {name: w[number] for name, w in weights.items()})  156 us
    dot_general x19, matrix products, matmul(): jnp.dot(a, w, preferred_element_type=jnp.float32).astype(jnp.bfloat16)  137 us
    dot_general x20, matrix products, layer(): up = jnp.dot(a, w['w_up'], preferred_element_type=jnp.float32)  125 us
    dot_general x20, matrix products, layer(): gate = jnp.dot(a, w['w_gate'], preferred_element_type=jnp.float32)  117 us
    dot_general x34, waiting for transfers between devices, layer(): gate = jnp.dot(a, w['w_gate'], preferred_element_type=jnp.float32)  116 us
    dot_general x34, waiting for transfers between devices, layer(): up = jnp.dot(a, w['w_up'], preferred_element_type=jnp.float32)  110 us
    dot_general x34, waiting for transfers between devices, matmul(): jnp.dot(a, w, preferred_element_type=jnp.float32).astype(jnp.bfloat16)  103 us
    dot_general x34, starting transfers between devices, layer(): gate = jnp.dot(a, w['w_gate'], preferred_element_type=jnp.float32)  73.4 us
  transfers between devices with their start and end apart: 108, of which 68 were waited for; matrix products, arithmetic and copies ran while one was open for 40% of the time, Pallas kernels for 0%

commit v1 on v0

v1 whole, which is shorter than its diff:
```python
import jax
import jax.numpy as jnp
from jax import lax
from jax.experimental import pallas as pl
from jax.experimental.pallas import tpu as pltpu
from jax.sharding import PartitionSpec as P


MESH = pl.DeviceIdType.MESH
Z = 4


def gather_kernel(gu_ref, d_ref, gu_out, d_out, s1s, s1r, s2s, s2r, s3s, s3r, s4s, s4r, loc):
    x, me = lax.axis_index("rep"), lax.axis_index("dp")
    y, z, c = me // 8, (me // 2) % 4, me % 2

    def at(yy, zz, cc):
        return (yy * Z + zz) * 2 + cc

    def zx(k):
        if k == 2:
            return (z + 2) % 4
        other = z + 1 - 2 * (z % 2)
        return other if k == 1 else 3 - z

    zs = [z, zx(1), zx(2), zx(3)]
    y_peer, c_peer, x_peer = (x, at(1 - y, z, c)), (x, at(y, z, 1 - c)), (1 - x, me)
    peers = [(x, at(y, zs[k], c)) for k in (1, 2, 3)] + [y_peer, c_peer, x_peer]
    barrier = pltpu.get_barrier_semaphore()
    for peer in peers:
        pl.semaphore_signal(barrier, inc=1, device_id=peer, device_id_type=MESH)
    pl.semaphore_wait(barrier, len(peers))

    pending = []

    def send(src, dst, ss, rs, peer):
        copy = pltpu.make_async_remote_copy(src, dst, ss, rs, device_id=peer, device_id_type=MESH)
        copy.start()
        pending.append(copy)
        return copy

    locals_ = []
    groups = [(0, True), (0, False), (1, True), (1, False)]
    first, second, third, fourth = {}, {}, {}, []

    def own(l, gu):
        return gu_ref.at[x, l] if gu else d_ref.at[l]

    def place(l, gu, b, m=None):
        return gu_out.at[x if m is None else m, l, b] if gu else d_out.at[l, b]

    for g, (l, gu) in enumerate(groups):
        for k in (1, 2, 3):
            first[g, k] = send(own(l, gu), place(l, gu, me), s1s.at[g, k - 1], s1r.at[g, k - 1], (x, at(y, zs[k], c)))
    fourth_count = [0] * 4

    def to_core(g, src, dst):
        n = fourth_count[g]
        fourth_count[g] += 1
        fourth.append(send(src, dst, s4s.at[g, n], s4r.at[g, n], c_peer))

    for g, (l, gu) in enumerate(groups):
        second[g, 0] = send(own(l, gu), place(l, gu, me), s2s.at[g, 0], s2r.at[g, 0], y_peer)
        for m in (0, 1) if gu else (0,):
            src = gu_ref.at[m, l] if gu else d_ref.at[l]
            dst = gu_out.at[m, l, me] if gu else d_out.at[l, me]
            to_core(g, src, dst)
            copy = pltpu.make_async_copy(src, dst, loc.at[2 * g + m])
            copy.start()
            locals_.append(copy)

    def arrive_first(g, k):
        l, gu = groups[g]
        first[g, k].wait_recv()
        b = at(y, zs[k], c)
        ref = place(l, gu, b)
        second[g, k] = send(ref, ref, s2s.at[g, k], s2r.at[g, k], y_peer)
        if gu:
            third[g, k - 1] = send(ref, ref, s3s.at[g // 2, k - 1], s3r.at[g // 2, k - 1], x_peer)
        to_core(g, ref, ref)

    def arrive_second(g, k):
        l, gu = groups[g]
        second[g, k].wait_recv()
        ref = place(l, gu, at(1 - y, zs[k], c))
        if gu:
            third[g, 3 + k] = send(ref, ref, s3s.at[g // 2, 3 + k], s3r.at[g // 2, 3 + k], x_peer)
        to_core(g, ref, ref)

    def arrive_third(g, j):
        l, gu = groups[g]
        third[g, j].wait_recv()
        b = at(y, zs[j + 1], c) if j < 3 else at(1 - y, zs[j - 3], c)
        ref = place(l, gu, b, 1 - x)
        to_core(g, ref, ref)

    events = []
    for g, (l, gu) in enumerate(groups):
        events += [(4 * g + k + 1.0, 0, arrive_first, g, k) for k in (1, 2, 3)]
        events += [(4 * g + k + 2.5, 1, arrive_second, g, k) for k in range(4)]
        if gu:
            events += [(7 * (g // 2) + j + 3.7, 2, arrive_third, g, j) for j in range(7)]
    for _, _, what, g, k in sorted(events, key=lambda e: e[:2]):
        what(g, k)
    for copy in fourth:
        copy.wait_recv()
    for copy in pending:
        copy.wait_send()
    for copy in locals_:
        copy.wait()


def gather(w_gate, w_up, w_down):
    gu = jnp.stack([w_gate, w_up])
    any_ = pl.BlockSpec(memory_space=pl.ANY)
    dma = pltpu.SemaphoreType.DMA
    _, layers, rows, ff = gu.shape
    _, rows_d, d = w_down.shape
    n = 16
    gu, down = pl.pallas_call(
        gather_kernel,
        out_shape=(
            jax.ShapeDtypeStruct((2, layers, n, rows, ff), gu.dtype),
            jax.ShapeDtypeStruct((layers, n, rows_d, d), gu.dtype),
        ),
        in_specs=[any_] * 2,
        out_specs=(any_, any_),
        scratch_shapes=[
            dma((4, 3)), dma((4, 3)), dma((4, 4)), dma((4, 4)), dma((2, 7)), dma((2, 7)),
            dma((4, 16)), dma((4, 16)), dma((8,)),
        ],
        compiler_params=pltpu.CompilerParams(collective_id=0, has_side_effects=True),
    )(gu, w_down)
    gu = gu.reshape(2, layers, n * rows, ff)
    down = down.reshape(layers, n * rows_d, d)
    return [(gu[0, l], gu[1, l], down[l]) for l in range(layers)]


def dot(a, b, ca, cb):
    return lax.dot_general(a, b, (((ca,), (cb,)), ((), ())), preferred_element_type=jnp.float32)


def pairs(of):
    return [((y * Z + z) * 2 + c, of(y, z, c)) for y in range(2) for z in range(Z) for c in range(2)]


def scatter_sum(term):
    me = lax.axis_index("dp")
    y, z, c = me // 8, (me // 2) % 4, me % 2
    term = term.reshape(2, Z, 2, -1, term.shape[-1])

    def pick(t, i, axis):
        return lax.dynamic_index_in_dim(t, i, axis, keepdims=False)

    def swap(t, of):
        t = t.astype(jnp.bfloat16)
        t = lax.ppermute(t, "dp", pairs(of))
        return t.astype(jnp.float32)

    got = swap(pick(term, 1 - c, 2), lambda y, z, c: (y * Z + z) * 2 + 1 - c)
    term = pick(term, c, 2) + got
    got = swap(pick(term, 1 - y, 0), lambda y, z, c: ((1 - y) * Z + z) * 2 + c)
    term = pick(term, y, 0) + got
    total = pick(term, z, 0)
    for k in (1, 2, 3):
        total += swap(pick(term, z ^ k, 0), lambda y, z, c: (y * Z + (z ^ k)) * 2 + c)
    return total.astype(jnp.bfloat16)


def solution(mesh):
    def step(*args):
        return work(*args)

    def work(x, dy, w_gate, w_up, w_down):
        x, dy = x[0], dy[0]
        bf16, f32 = jnp.bfloat16, jnp.float32
        weights = gather(w_gate, w_up, w_down)
        h, saved = x, []
        for wg, wu, wd in weights:
            wide = h.astype(f32)
            scale = lax.rsqrt(jnp.mean(wide**2, -1, keepdims=True) + 1e-6)
            a = (wide * scale).astype(bf16)
            gate, up = dot(a, wg, 1, 0), dot(a, wu, 1, 0)
            p = (jax.nn.silu(gate) * up).astype(bf16)
            saved.append((h, scale, a, gate, up, p))
            if len(saved) < len(weights):
                h = h + dot(p, wd, 1, 0).astype(bf16)
        outs = []
        for l in reversed(range(len(weights))):
            wg, wu, wd = weights[l]
            h, scale, a, gate, up, p = saved[l]
            by_d = scatter_sum(dot(p, dy, 0, 0))
            dp = dot(dy, wd, 1, 1).astype(bf16).astype(f32)
            s = jax.nn.sigmoid(gate)
            silu = gate * s
            dup = (dp * silu).astype(bf16)
            dgate = (dp * up * (s * (1 + gate * (1 - s)))).astype(bf16)
            by_g = scatter_sum(dot(a, dgate, 0, 0))
            by_u = scatter_sum(dot(a, dup, 0, 0))
            da = (dot(dgate, wg, 1, 1).astype(bf16) + dot(dup, wu, 1, 1).astype(bf16)).astype(f32)
            wide = h.astype(f32)
            dh = scale * (da - wide * (scale**2 * jnp.mean(da * wide, -1, keepdims=True)))
            dy = dy + dh.astype(bf16)
            outs.append((by_g, by_u, by_d))
        outs = outs[::-1]
        return (dy[None], *(jnp.stack([o[i] for o in outs]) for i in range(3)))

    rows = P(("rep", "dp"), None, None)
    w = P(None, "dp", None)
    g = P("rep", "dp", None)
    step = jax.shard_map(step, mesh=mesh, in_specs=(rows, rows, w, w, w), out_specs=(rows, g, g, g), check_vma=False)
    return step
```

time: 1310 us -> 757 us (0.58)
  waiting for transfers between devices: 487 us -> 148 us
  starting transfers between devices: 220 us -> 73 us
  Pallas kernels: 0 us -> 115 us
  matrix products: 378 us -> 277 us
  loops' own time: 48.7 us -> 0 us
  between operations: 15 us -> 1.58 us
    dot_general x102 -> x0, waiting for transfers between devices: 329 us -> none  [the longest x34 116 us: layer(): gate = jnp.dot(a, w['w_gate'], preferred_element_type=jnp.float32)]
    dot_general x102 -> x0, starting transfers between devices: 219 us -> none  [the longest x34 73.4 us: layer(): gate = jnp.dot(a, w['w_gate'], preferred_element_type=jnp.float32)]
    squeeze x6 -> x0, waiting for transfers between devices: 156 us -> none  [stack(): h = layer(h, {name: w[number] for name, w in weights.items()})]
    ppermute x0 -> x30, waiting for transfers between devices: none -> 148 us  [swap(): t = lax.ppermute(t, 'dp', pairs(of))]
    pallas_call x0 -> x1, Pallas kernels: none -> 115 us  [gather(): pl.pallas_call(gather_kernel, out_shape=(jax.ShapeDtypeStruct((2, layers,...]
    dot_general x59 -> x17, matrix products: 378 us -> 277 us  [dot(): lax.dot_general(a, b, (((ca,), (cb,)), ((), ())), preferred_element_type=...]
    ppermute x0 -> x30, starting transfers between devices: none -> 73 us  [swap(): t = lax.ppermute(t, 'dp', pairs(of))]
    another operation x6 -> x0, loops' own time: 48.7 us -> none  [the longest x2 16.4 us: layer(): up = jnp.dot(a, w['w_up'], preferred_element_type=jnp.float32)]
  transfers between devices with their start and end apart: 108 -> 30, of which waited for: 68 -> 12; matrix products, arithmetic and copies ran while one was open for 40% -> 28% of each run, Pallas kernels for 0% -> 0%
where the time goes in v1:
time: 757 us; the launch traced here: 743 us
  matrix products  277 us (37%)
  waiting for transfers between devices  148 us (20%)
  Pallas kernels  115 us (15%)
  starting transfers between devices  73 us (10%)
  local copies, waits for them, and re-layouts  69.4 us (9%)
  other arithmetic  59.2 us (8%)
    dot_general x17, matrix products, dot(): lax.dot_general(a, b, (((ca,), (cb,)), ((), ())), preferred_element_type=...  277 us
    ppermute x30, waiting for transfers between devices, swap(): t = lax.ppermute(t, 'dp', pairs(of))  148 us
    pallas_call x1, Pallas kernels, gather(): pl.pallas_call(gather_kernel, out_shape=(jax.ShapeDtypeStruct((2, layers,...  115 us
    ppermute x30, starting transfers between devices, swap(): t = lax.ppermute(t, 'dp', pairs(of))  73 us
    unnamed x55, local copies, waits for them, and re-layouts  33.6 us
    convert_element_type x18, local copies, waits for them, and re-layouts, swap(): t = t.astype(jnp.bfloat16)  17.8 us
    convert_element_type x1, other arithmetic, work(): p = (jax.nn.silu(gate) * up).astype(bf16)  17.3 us
    add x6, other arithmetic, scatter_sum(): term = pick(term, c, 2) + got  16.6 us
  transfers between devices with their start and end apart: 30, of which 12 were waited for; matrix products, arithmetic and copies ran while one was open for 28% of the time, Pallas kernels for 0%

profile of v1, /device:TPU:4, one launch (start us, length us, event | category | flops | bytes accessed | tf_op | source)
XLA Modules:
  0.0 743.3 jit_solution(5652885638063633995)
XLA Ops:
  0.7 6.1 copy.17
  6.8 2.8 fusion.19
  11.4 115.0 %shard_map.84 = (bf16[2,2,16,56,2304]{4,3,2,1,0:T(8,128)(2,1)}, bf16[2,16,144,896]{3,2,1,0:T(8,128)(2,1)}) custom-call(bf16[2,2,56,2304]{3,2,1,0:T(8,128)(2,1)} %pad_maximum_fusion.gu_ref, bf16[2,144,896]{2,1,0:T(8,128)(2,1)} %d_ref.1), custom_call_target="tpu_custom_call" | custom-call | tf_op jit(solution)/shard_map/pallas_call | solution.py:120
  126.3 16.6 %fusion.33 = f32[2048,2304]{1,0:T(8,128)} fusion(bf16[2,2,896,2304]{3,2,1,0:T(8,128)(2,1)} %bitcast.302, bf16[1,2048,896]{2,1,0:T(8,128)(2,1)} %param.5, f32[2048]{0:T(1024)S(1)} %add_rsqrt_fusion.1), kind=kOutput, calls=%fused_computation.75 | convolution fusion | flops 8461221888 | bytes 26681344 | tf_op jit(solution)/shard_map/dot_general | solution.py:140
  142.9 21.5 %multiply_convert_fusion = (bf16[2048,2304]{1,0:T(8,128)(2,1)}, f32[2048,2304]{1,0:T(8,128)}) fusion(f32[2048,2304]{1,0:T(8,128)} %fusion.33, bf16[2,2,896,2304]{3,2,1,0:T(8,128)(2,1)} %bitcast.303, bf16[1,2048,896]{2,1,0:T(8,128)(2,1)} %param.5, f32[2048]{0:T(1024)S(1)} %add_rsqrt_fusion.1), kind=kOutput, calls=%fused_computation.18 | convolution fusion | flops 8489533440 | bytes 54992896 | tf_op jit(solution)/shard_map/dot_general | solution.py:140
  164.4 5.2 fusion.102
  170.3 13.8 %fusion.22 = (f32[2048]{0:T(1024)S(1)}, bf16[2048,896]{0,1:T(8,128)(2,1)}) fusion(bf16[2048,2304]{1,0:T(8,128)(2,1)} %get-tuple-element.42, bf16[2304,896]{1,0:T(8,128)(2,1)S(1)} %bitcast.297, bf16[1,2048,896]{1,2,0:T(8,128)(2,1)S(1)} %copy-done), kind=kOutput, calls=%fused_computation.44 | convolution fusion | flops 8464889856 | bytes 20914176 | tf_op jit(solution)/shard_map/dot_general | solution.py:140
  184.1 6.1 copy.16
  190.2 15.1 %convolution_convert_fusion.1 = bf16[2304,2048]{0,1:T(8,128)(2,1)} fusion(bf16[2304,896]{1,0:T(8,128)(2,1)} %bitcast.299, bf16[1,2048,896]{2,1,0:T(8,128)(2,1)} %param.6), kind=kOutput, calls=%fused_computation.30 | convolution fusion | flops 8460435456 | bytes 17235968 | tf_op jit(solution)/shard_map/dot_general | solution.py:140
  205.3 15.0 %fusion.39 = f32[2048,2304]{1,0:T(8,128)} fusion(bf16[2,2,896,2304]{3,2,1,0:T(8,128)(2,1)} %bitcast.304, bf16[2048,896]{0,1:T(8,128)(2,1)S(1)} %copy-done.9, f32[2048]{0:T(1024)S(1)} %add_rsqrt_fusion), kind=kOutput, calls=%fused_computation.81 | convolution fusion | flops 8461221888 | bytes 26681344 | tf_op jit(solution)/shard_map/dot_general | solution.py:140
  220.4 34.6 %fusion.8 = (bf16[2048,2304]{1,0:T(8,128)(2,1)}, bf16[2048,2304]{1,0:T(8,128)(2,1)}, f32[2048,2304]{1,0:T(8,128)}) fusion(bf16[2304,2048]{0,1:T(8,128)(2,1)} %convolution_convert_fusion.1, f32[2048,2304]{1,0:T(8,128)} %fusion.39, bf16[2,2,896,2304]{3,2,1,0:T(8,128)(2,1)} %bitcast.305, bf16[2048,896]{0,1:T(8,128)(2,1)} %get-tuple-element.45, ...), kind=kOutput, calls=%fused_computation.15 | convolution fusion | flops 8527282176 | bytes 73867264 | tf_op jit(solution)/shard_map/dot_general | solution.py:140
  255.0 12.7 %fusion.36 = bf16[2048,896]{0,1:T(8,128)(2,1)S(1)} fusion(bf16[2048,2304]{1,0:T(8,128)(2,1)} %get-tuple-element.19, bf16[2,2,896,2304]{3,2,1,0:T(8,128)(2,1)} %bitcast.306), kind=kOutput, calls=%fused_computation.78 | convolution fusion | flops 8455716864 | bytes 17235968 | tf_op jit(solution)/shard_map/dot_general | solution.py:140
  267.7 13.3 %fusion.24 = (f32[2048]{0:T(1024)S(1)}, bf16[2048,896]{0,1:T(8,128)(2,1)S(1)}) fusion(bf16[2048,896]{0,1:T(8,128)(2,1)S(1)} %copy-done.10, bf16[2048,896]{0,1:T(8,128)(2,1)S(1)} %fusion.36, bf16[2048,2304]{1,0:T(8,128)(2,1)} %get-tuple-element.18, bf16[2,2,896,2304]{3,2,1,0:T(8,128)(2,1)} %bitcast.307), kind=kOutput, calls=%fused_computation.46 | convolution fusion | flops 8466724864 | bytes 24584192 | tf_op jit(solution)/shard_map/dot_general | solution.py:140
  281.0 3.0 fusion.28
  284.1 1.8 copy-done.3
  285.9 14.5 %fusion.103 = f32[2304,896]{1,0:T(8,128)} fusion(bf16[2048,2304]{1,0:T(8,128)(2,1)} %get-tuple-element.42, bf16[2048,896]{0,1:T(8,128)(2,1)S(1)} %fusion.28), kind=kOutput, calls=%fused_computation.183 | convolution fusion | flops 8455716864 | bytes 21364736 | tf_op jit(solution)/shard_map/dot_general | solution.py:140
  300.4 3.7 fusion.51
  304.7 17.3 %fusion.3 = bf16[2304,2048]{0,1:T(8,128)(2,1)} fusion(f32[2048,2304]{1,0:T(8,128)} %get-tuple-element.46, f32[2048,2304]{1,0:T(8,128)} %fusion.39), kind=kLoop, calls=%fused_computation.6 | loop fusion | flops 28311552 | bytes 47185920 | tf_op jit(solution)/shard_map/convert_element_type | solution.py:184
  321.9 12.7 %copy.22 = bf16[2304,2048]{1,0:T(8,128)(2,1)} copy(bf16[2304,2048]{0,1:T(8,128)(2,1)} %fusion.3) | data formatting | bytes 18874368 | tf_op jit(solution)/shard_map/convert_element_type | solution.py:184
  334.7 14.1 %fusion.30 = f32[2,4,2,144,896]{4,3,2,1,0:T(8,128)S(1)} fusion(bf16[2,4,2,144,2048]{4,3,2,1,0:T(8,128)(2,1)} %bitcast.284, bf16[1,2048,896]{2,1,0:T(8,128)(2,1)} %param.6), kind=kOutput, calls=%fused_computation.69 | convolution fusion | flops 8455716864 | bytes 21364736 | tf_op jit(solution)/shard_map/dot_general | solution.py:140
  348.8 3.3 copy-done.4
  353.6 30.8 %fusion.2 = (bf16[2048,2304]{1,0:T(8,128)(2,1)}, bf16[2048,2304]{1,0:T(8,128)(2,1)}) fusion(f32[2048,2304]{1,0:T(8,128)} %fusion.33, f32[2048,2304]{1,0:T(8,128)} %get-tuple-element.43, bf16[2048,896]{0,1:T(8,128)(2,1)} %copy-done.3, bf16[2304,896]{1,0:T(8,128)(2,1)} %bitcast.298), kind=kOutput, calls=%fused_computation.4 | convolution fusion | flops 8526495744 | bytes 64421888 | tf_op jit(solution)/shard_map/dot_general | solution.py:140
  384.4 12.7 %fusion.32 = bf16[2048,896]{0,1:T(8,128)(2,1)S(1)} fusion(bf16[2048,2304]{1,0:T(8,128)(2,1)} %get-tuple-element.17, bf16[2,2,896,2304]{3,2,1,0:T(8,128)(2,1)} %bitcast.308), kind=kOutput, calls=%fused_computation.74 | convolution fusion | flops 8455716864 | bytes 17235968 | tf_op jit(solution)/shard_map/dot_general | solution.py:140
  397.2 14.5 %fusion.21 = (bf16[2048,896]{0,1:T(8,128)(2,1)S(1)}, f32[2048]{0:T(1024)S(1)}, bf16[2048,896]{0,1:T(8,128)(2,1)}) fusion(bf16[1,2048,896]{1,2,0:T(8,128)(2,1)S(1)} %copy-done.1, f32[2048]{0:T(1024)S(1)} %copy-done.17, bf16[2048,896]{0,1:T(8,128)(2,1)S(1)} %fusion.32, bf16[2048,2304]{1,0:T(8,128)(2,1)} %get-tuple-element.16, ...), kind=kOutput, calls=%fused_computation.43 | convolution fusion | flops 8470394880 | bytes 28262400 | tf_op jit(solution)/shard_map/dot_general | solution.py:140
  411.7 11.2 %fusion.11 = f32[2,4,2,56,2304]{4,3,2,1,0:T(8,128)S(1)} fusion(bf16[2,4,2,56,2048]{4,3,2,1,0:T(8,128)(2,1)S(1)} %bitcast.310, bf16[2048,2304]{1,0:T(8,128)(2,1)} %get-tuple-element.16), kind=kOutput, calls=%fused_computation.31 | convolution fusion | flops 8455716864 | bytes 21364736 | tf_op jit(solution)/shard_map/dot_general | solution.py:140
  424.4 3.2 copy-done.7
  428.1 11.0 %fusion.40 = f32[896,2304]{1,0:T(8,128)S(1)} fusion(bf16[2048,2304]{1,0:T(8,128)(2,1)} %get-tuple-element.19, bf16[2048,896]{0,1:T(8,128)(2,1)S(1)} %copy-done.11, f32[2048]{0:T(1024)S(1)} %copy-done.19), kind=kOutput, calls=%fused_computation.82 | convolution fusion | flops 8461221888 | bytes 21372928 | tf_op jit(solution)/shard_map/dot_general | solution.py:140
  439.2 1.7 fusion.50
  440.8 2.2 copy-done.6
  443.0 11.2 %fusion.13 = f32[2,4,2,56,2304]{4,3,2,1,0:T(8,128)S(1)} fusion(bf16[2,4,2,56,2048]{4,3,2,1,0:T(8,128)(2,1)S(1)} %bitcast.311, bf16[2048,2304]{1,0:T(8,128)(2,1)} %get-tuple-element.17), kind=kOutput, calls=%fused_computation.33 | convolution fusion | flops 8455716864 | bytes 21364736 | tf_op jit(solution)/shard_map/dot_general | solution.py:140
  454.3 3.3 copy-done.5
  458.3 14.5 %fusion.42 = f32[896,2304]{1,0:T(8,128)} fusion(bf16[2048,2304]{1,0:T(8,128)(2,1)} %get-tuple-element.18, bf16[2048,896]{0,1:T(8,128)(2,1)S(1)} %copy-done.11, f32[2048]{0:T(1024)S(1)} %copy-done.19), kind=kOutput, calls=%fused_computation.83 | convolution fusion | flops 8461221888 | bytes 21372928 | tf_op jit(solution)/shard_map/dot_general | solution.py:140
  472.8 9.0 %fusion.27 = bf16[1,2048,896]{1,2,0:T(8,128)(2,1)} fusion(bf16[2048,896]{0,1:T(8,128)(2,1)} %copy-done.3, bf16[2048,896]{0,1:T(8,128)(2,1)} %get-tuple-element.49, bf16[1,2048,896]{1,2,0:T(8,128)(2,1)} %copy.17, f32[2048]{0:T(1024)S(1)} %multiply_multiply_fusion, f32[2048]{0:T(1024)S(1)} %copy-done.17), kind=kLoop, calls=%fused_computation.66 | loop fusion | flops 12845056 | bytes 14696448 | tf_op jit(solution)/shard_map/broadcast_in_dim | solution.py:206
  481.8 6.3 copy.24
  488.1 3.9 fusion.49
  492.1 3.3 bitcast_add_fusion.1
  497.4 2.4 bitcast_add_fusion
  501.8 2.1 bitcast_add_fusion.3
  506.1 3.3 bitcast_add_fusion.2
  511.4 3.4 bitcast_add_fusion.5
  516.0 2.1 bitcast_add_fusion.4
  518.2 4.3 collective-permute-done.21
  524.9 19.6 %collective-permute-done.26 = bf16[4,144,896]{2,1,0:T(8,128)(2,1)} collective-permute-done((bf16[4,144,896]{2,1,0:T(8,128)(2,1)}, bf16[4,144,896]{2,1,0:T(8,128)(2,1)}, u32[]{:S(2)}, u32[]{:S(2)}) %collective-permute-start.26) | collective-permute-done | bytes 1032224 | tf_op jit(solution)/shard_map/ppermute | solution.py:157
  544.6 4.3 collective-permute-start.22
  550.4 16.2 %collective-permute-done.11 = bf16[4,56,2304]{2,1,0:T(8,128)(2,1)} collective-permute-done((bf16[4,56,2304]{2,1,0:T(8,128)(2,1)}, bf16[4,56,2304]{2,1,0:T(8,128)(2,1)}, u32[]{:S(2)}, u32[]{:S(2)}) %collective-permute-start.11) | collective-permute-done | bytes 1032224 | tf_op jit(solution)/shard_map/ppermute | solution.py:157
  566.7 4.8 collective-permute-start.23
  573.0 15.8 %collective-permute-done.16 = bf16[4,56,2304]{2,1,0:T(8,128)(2,1)} collective-permute-done((bf16[4,56,2304]{2,1,0:T(8,128)(2,1)}, bf16[4,56,2304]{2,1,0:T(8,128)(2,1)}, u32[]{:S(2)}, u32[]{:S(2)}) %collective-permute-start.16) | collective-permute-done | bytes 1032224 | tf_op jit(solution)/shard_map/ppermute | solution.py:157
  588.8 4.3 collective-permute-start.12
  594.7 16.1 %collective-permute-done.1 = bf16[4,56,2304]{2,1,0:T(8,128)(2,1)S(1)} collective-permute-done((bf16[4,56,2304]{2,1,0:T(8,128)(2,1)S(1)}, bf16[4,56,2304]{2,1,0:T(8,128)(2,1)S(1)}, u32[]{:S(2)}, u32[]{:S(2)}) %collective-permute-start.1) | collective-permute-done | bytes 1032224 | tf_op jit(solution)/shard_map/ppermute | solution.py:157
  610.8 4.8 collective-permute-start.13
  615.9 16.6 %collective-permute-done.6 = bf16[4,56,2304]{2,1,0:T(8,128)(2,1)S(1)} collective-permute-done((bf16[4,56,2304]{2,1,0:T(8,128)(2,1)S(1)}, bf16[4,56,2304]{2,1,0:T(8,128)(2,1)S(1)}, u32[]{:S(2)}, u32[]{:S(2)}) %collective-permute-start.6) | collective-permute-done | bytes 1032224 | tf_op jit(solution)/shard_map/ppermute | solution.py:157
  632.5 2.4 collective-permute-start.14
  635.2 3.0 collective-permute-start.17
  638.8 4.7 collective-permute-done.14
  643.4 2.4 collective-permute-start.19
  647.7 4.2 collective-permute-start.27
  651.8 18.1 %collective-permute-done.18 = bf16[56,2304]{1,0:T(8,128)(2,1)S(1)} collective-permute-done((bf16[56,2304]{1,0:T(8,128)(2,1)S(1)}, bf16[56,2304]{1,0:T(8,128)(2,1)S(1)}, u32[]{:S(2)}, u32[]{:S(2)}) %collective-permute-start.18) | collective-permute-done | bytes 258080 | tf_op jit(solution)/shard_map/ppermute | solution.py:157
  669.9 2.4 collective-permute-start.29
  672.5 16.3 %collective-permute-start.2 = (bf16[56,2304]{1,0:T(8,128)(2,1)S(1)}, bf16[56,2304]{1,0:T(8,128)(2,1)S(1)}, u32[]{:S(2)}, u32[]{:S(2)}) collective-permute-start(bf16[56,2304]{1,0:T(8,128)(2,1)S(1)} %get-tuple-element.36), channel_id=1, source_target_pairs={{0,2},{1,3},{2,0},{3,1},{4,6},{5,7},{6,4},{7,5},{8,10},{9,11},{10,... | collective-permute-start | bytes 774152 | tf_op jit(solution)/shard_map/ppermute | solution.py:157
  688.8 4.8 collective-permute-start.3
  695.2 13.5 %collective-permute-done.28 = bf16[144,896]{1,0:T(8,128)(2,1)S(1)} collective-permute-done((bf16[144,896]{1,0:T(8,128)(2,1)S(1)}, bf16[144,896]{1,0:T(8,128)(2,1)S(1)}, u32[]{:S(2)}, u32[]{:S(2)}) %collective-permute-start.28) | collective-permute-done | bytes 258080 | tf_op jit(solution)/shard_map/ppermute | solution.py:157
  708.7 7.0 collective-permute-start.8
  718.1 12.7 %collective-permute-done.3 = bf16[56,2304]{1,0:T(8,128)(2,1)S(1)} collective-permute-done((bf16[56,2304]{1,0:T(8,128)(2,1)S(1)}, bf16[56,2304]{1,0:T(8,128)(2,1)S(1)}, u32[]{:S(2)}, u32[]{:S(2)}) %collective-permute-start.3) | collective-permute-done | bytes 258080 | tf_op jit(solution)/shard_map/ppermute | solution.py:157
  731.8 10.1 %collective-permute-done.8 = bf16[56,2304]{1,0:T(8,128)(2,1)S(1)} collective-permute-done((bf16[56,2304]{1,0:T(8,128)(2,1)S(1)}, bf16[56,2304]{1,0:T(8,128)(2,1)S(1)}, u32[]{:S(2)}, u32[]{:S(2)}) %collective-permute-start.8) | collective-permute-done | bytes 258080 | tf_op jit(solution)/shard_map/ppermute | solution.py:157
  (122 shorter events, 33.1 us)
Async XLA Ops:
  0.6 9.6 %copy-start.12 = (bf16[2,56,2304]{2,1,0:T(8,128)(2,1)S(1)}, bf16[2,56,2304]{2,1,0:T(8,128)(2,1)}, u32[]{:S(2)}) copy-start(bf16[2,56,2304]{2,1,0:T(8,128)(2,1)} %param.8) | copy-start | bytes 1548292
  0.6 9.6 %copy-start.13 = (bf16[2,56,2304]{2,1,0:T(8,128)(2,1)S(1)}, bf16[2,56,2304]{2,1,0:T(8,128)(2,1)}, u32[]{:S(2)}) copy-start(bf16[2,56,2304]{2,1,0:T(8,128)(2,1)} %param.7) | copy-start | bytes 1548292
  9.6 0.6 copy-start.14
  10.2 132.7 %copy-start.16 = (f32[2048]{0:T(1024)}, f32[2048]{0:T(1024)S(1)}, u32[]{:S(2)}) copy-start(f32[2048]{0:T(1024)S(1)} %add_rsqrt_fusion.1) | copy-start | bytes 24580
  164.4 6.0 copy-start
  169.6 14.5 %copy-start.8 = (bf16[1,16,144,896]{3,2,1,0:T(8,128)(2,1)}, bf16[1,16,144,896]{3,2,1,0:T(8,128)(2,1)S(1)}, u32[]{:S(2)}) copy-start(bf16[1,16,144,896]{3,2,1,0:T(8,128)(2,1)S(1)} %get-tuple-element.21) | copy-start | bytes 12386308
  184.1 96.9 %copy-start.18 = (f32[2048]{0:T(1024)}, f32[2048]{0:T(1024)S(1)}, u32[]{:S(2)}) copy-start(f32[2048]{0:T(1024)S(1)} %add_rsqrt_fusion) | copy-start | bytes 24580
  190.2 15.1 %copy-start.9 = (bf16[2048,896]{0,1:T(8,128)(2,1)S(1)}, bf16[2048,896]{0,1:T(8,128)(2,1)}, u32[]{:S(2)}) copy-start(bf16[2048,896]{0,1:T(8,128)(2,1)} %get-tuple-element.45) | copy-start | bytes 11010052
  255.0 12.7 %copy-start.10 = (bf16[2048,896]{0,1:T(8,128)(2,1)S(1)}, bf16[2048,896]{0,1:T(8,128)(2,1)}, u32[]{:S(2)}) copy-start(bf16[2048,896]{0,1:T(8,128)(2,1)} %get-tuple-element.45) | copy-start | bytes 11010052
  267.7 13.3 %copy-start.2 = (bf16[1,2048,896]{1,2,0:T(8,128)(2,1)S(1)}, bf16[1,2048,896]{1,2,0:T(8,128)(2,1)}, u32[]{:S(2)}) copy-start(bf16[1,2048,896]{1,2,0:T(8,128)(2,1)} %copy.16) | copy-start | bytes 11010052
  284.1 1.8 copy-start.3
  304.2 187.8 %collective-permute-start.20 = (bf16[2,4,144,896]{3,2,1,0:T(8,128)(2,1)}, bf16[2,4,144,896]{3,2,1,0:T(8,128)(2,1)}, u32[]{:S(2)}, u32[]{:S(2)}) collective-permute-start(bf16[2,4,144,896]{3,2,1,0:T(8,128)(2,1)} %fusion.51), channel_id=1, source_target_pairs={{0,1},{1,0},{2,3},{3,2},{4,5},{5,4},{6,7},{7,6},{8,9},{9,8},{10,11... | collective-permute-start | bytes 6193160 | tf_op jit(solution)/shard_map/ppermute | solution.py:157
  348.8 3.3 copy-start.4
  353.6 142.8 %collective-permute-start.25 = (bf16[2,4,144,896]{3,2,1,0:T(8,128)(2,1)}, bf16[2,4,144,896]{3,2,1,0:T(8,128)(2,1)}, u32[]{:S(2)}, u32[]{:S(2)}) collective-permute-start(bf16[2,4,144,896]{3,2,1,0:T(8,128)(2,1)} %fusion.48), channel_id=1, source_target_pairs={{0,1},{1,0},{2,3},{3,2},{4,5},{5,4},{6,7},{7,6},{8,9},{9,8},{10,11... | collective-permute-start | bytes 6193160 | tf_op jit(solution)/shard_map/ppermute | solution.py:157
  384.4 12.7 %copy-start.1 = (bf16[1,2048,896]{1,2,0:T(8,128)(2,1)S(1)}, bf16[1,2048,896]{1,2,0:T(8,128)(2,1)}, u32[]{:S(2)}) copy-start(bf16[1,2048,896]{1,2,0:T(8,128)(2,1)} %copy.17) | copy-start | bytes 11010052
  384.4 12.7 %copy-start.17 = (f32[2048]{0:T(1024)S(1)}, f32[2048]{0:T(1024)}, u32[]{:S(2)}) copy-start(f32[2048]{0:T(1024)} %copy-done.16) | copy-start | bytes 24580
  422.9 4.7 copy-start.7
  422.9 5.2 copy-start.11
  422.9 5.2 copy-start.19
  427.6 73.2 %collective-permute-start.10 = (bf16[2,4,56,2304]{3,2,1,0:T(8,128)(2,1)}, bf16[2,4,56,2304]{3,2,1,0:T(8,128)(2,1)}, u32[]{:S(2)}, u32[]{:S(2)}) collective-permute-start(bf16[2,4,56,2304]{3,2,1,0:T(8,128)(2,1)} %fusion.47), channel_id=1, source_target_pairs={{0,1},{1,0},{2,3},{3,2},{4,5},{5,4},{6,7},{7,6},{8,9},{9,8},{10,11... | collective-permute-start | bytes 6193160 | tf_op jit(solution)/shard_map/ppermute | solution.py:157
  439.2 3.8 copy-start.6
  443.0 62.0 %collective-permute-start.15 = (bf16[2,4,56,2304]{3,2,1,0:T(8,128)(2,1)}, bf16[2,4,56,2304]{3,2,1,0:T(8,128)(2,1)}, u32[]{:S(2)}, u32[]{:S(2)}) collective-permute-start(bf16[2,4,56,2304]{3,2,1,0:T(8,128)(2,1)} %fusion.50), channel_id=1, source_target_pairs={{0,1},{1,0},{2,3},{3,2},{4,5},{5,4},{6,7},{7,6},{8,9},{9,8},{10,11... | collective-permute-start | bytes 6193160 | tf_op jit(solution)/shard_map/ppermute | solution.py:157
  454.2 3.3 copy-start.5
  457.7 15.0 %copy-start.15 = (f32[2048]{0:T(1024)S(1)}, f32[2048]{0:T(1024)}, u32[]{:S(2)}) copy-start(f32[2048]{0:T(1024)} %copy-done.14) | copy-start | bytes 24580
  457.7 52.7 %collective-permute-start = (bf16[2,4,56,2304]{3,2,1,0:T(8,128)(2,1)S(1)}, bf16[2,4,56,2304]{3,2,1,0:T(8,128)(2,1)}, u32[]{:S(2)}, u32[]{:S(2)}) collective-permute-start(bf16[2,4,56,2304]{3,2,1,0:T(8,128)(2,1)S(1)} %fusion.46), channel_id=1, source_target_pairs={{0,1},{1,0},{2,3},{3,2},{4,5},{5,4},{6,7},{7,6},{8,9},{9,8},{10,11... | collective-permute-start | bytes 6193160 | tf_op jit(solution)/shard_map/ppermute | solution.py:157
  488.1 9.3 %slice-start.2 = ((s8[8257536]{0:T(1024)(128)(4,1)}), s8[4194304]{0:T(1024)(128)(4,1)S(1)}, s32[]{:S(2)}) async-start(s8[8257536]{0:T(1024)(128)(4,1)} %bitcast.291), calls=%async_computation.2 | async-start | bytes 8388608
  492.0 5.4 slice-start.3
  492.0 23.0 %collective-permute-start.5 = (bf16[2,4,56,2304]{3,2,1,0:T(8,128)(2,1)}, bf16[2,4,56,2304]{3,2,1,0:T(8,128)(2,1)}, u32[]{:S(2)}, u32[]{:S(2)}) collective-permute-start(bf16[2,4,56,2304]{3,2,1,0:T(8,128)(2,1)} %fusion.49), channel_id=1, source_target_pairs={{0,1},{1,0},{2,3},{3,2},{4,5},{5,4},{6,7},{7,6},{8,9},{9,8},{10,11... | collective-permute-start | bytes 6193160 | tf_op jit(solution)/shard_map/ppermute | solution.py:157
  492.1 9.7 %slice-start.4 = ((s8[8257536]{0:T(1024)(128)(4,1)}), s8[4194304]{0:T(1024)(128)(4,1)S(1)}, s32[]{:S(2)}) async-start(s8[8257536]{0:T(1024)(128)(4,1)} %bitcast.295), calls=%async_computation.4 | async-start | bytes 8388608
  496.4 5.3 slice-start.5
  496.4 26.0 %collective-permute-start.21 = (bf16[4,144,896]{2,1,0:T(8,128)(2,1)}, bf16[4,144,896]{2,1,0:T(8,128)(2,1)}, u32[]{:S(2)}, u32[]{:S(2)}) collective-permute-start(bf16[4,144,896]{2,1,0:T(8,128)(2,1)} %fusion.58), channel_id=1, source_target_pairs={{0,8},{1,9},{2,10},{3,11},{4,12},{5,13},{6,14},{7,15},{8,0},{9,1},... | collective-permute-start | bytes 3096584 | tf_op jit(solution)/shard_map/ppermute | solution.py:157
  500.8 43.7 %collective-permute-start.26 = (bf16[4,144,896]{2,1,0:T(8,128)(2,1)}, bf16[4,144,896]{2,1,0:T(8,128)(2,1)}, u32[]{:S(2)}, u32[]{:S(2)}) collective-permute-start(bf16[4,144,896]{2,1,0:T(8,128)(2,1)} %fusion.59), channel_id=1, source_target_pairs={{0,8},{1,9},{2,10},{3,11},{4,12},{5,13},{6,14},{7,15},{8,0},{9,1},... | collective-permute-start | bytes 3096584 | tf_op jit(solution)/shard_map/ppermute | solution.py:157
  505.0 61.7 %collective-permute-start.11 = (bf16[4,56,2304]{2,1,0:T(8,128)(2,1)}, bf16[4,56,2304]{2,1,0:T(8,128)(2,1)}, u32[]{:S(2)}, u32[]{:S(2)}) collective-permute-start(bf16[4,56,2304]{2,1,0:T(8,128)(2,1)} %fusion.56), channel_id=1, source_target_pairs={{0,8},{1,9},{2,10},{3,11},{4,12},{5,13},{6,14},{7,15},{8,0},{9,1},... | collective-permute-start | bytes 3096584 | tf_op jit(solution)/shard_map/ppermute | solution.py:157
  506.1 9.9 %slice-start = ((s8[8257536]{0:T(1024)(128)(4,1)}), s8[4194304]{0:T(1024)(128)(4,1)S(1)}, s32[]{:S(2)}) async-start(s8[8257536]{0:T(1024)(128)(4,1)} %bitcast.288), calls=%async_computation | async-start | bytes 8388608
  510.5 5.5 slice-start.1
  510.5 78.3 %collective-permute-start.16 = (bf16[4,56,2304]{2,1,0:T(8,128)(2,1)}, bf16[4,56,2304]{2,1,0:T(8,128)(2,1)}, u32[]{:S(2)}, u32[]{:S(2)}) collective-permute-start(bf16[4,56,2304]{2,1,0:T(8,128)(2,1)} %fusion.57), channel_id=1, source_target_pairs={{0,8},{1,9},{2,10},{3,11},{4,12},{5,13},{6,14},{7,15},{8,0},{9,1},... | collective-permute-start | bytes 3096584 | tf_op jit(solution)/shard_map/ppermute | solution.py:157
  515.0 95.8 %collective-permute-start.1 = (bf16[4,56,2304]{2,1,0:T(8,128)(2,1)S(1)}, bf16[4,56,2304]{2,1,0:T(8,128)(2,1)S(1)}, u32[]{:S(2)}, u32[]{:S(2)}) collective-permute-start(bf16[4,56,2304]{2,1,0:T(8,128)(2,1)S(1)} %fusion.54), channel_id=1, source_target_pairs={{0,8},{1,9},{2,10},{3,11},{4,12},{5,13},{6,14},{7,15},{8,0},{9,1},... | collective-permute-start | bytes 3096584 | tf_op jit(solution)/shard_map/ppermute | solution.py:157
  522.4 110.1 %collective-permute-start.6 = (bf16[4,56,2304]{2,1,0:T(8,128)(2,1)S(1)}, bf16[4,56,2304]{2,1,0:T(8,128)(2,1)S(1)}, u32[]{:S(2)}, u32[]{:S(2)}) collective-permute-start(bf16[4,56,2304]{2,1,0:T(8,128)(2,1)S(1)} %fusion.55), channel_id=1, source_target_pairs={{0,8},{1,9},{2,10},{3,11},{4,12},{5,13},{6,14},{7,15},{8,0},{9,1},... | collective-permute-start | bytes 3096584 | tf_op jit(solution)/shard_map/ppermute | solution.py:157
  544.6 101.4 %collective-permute-start.22 = (bf16[144,896]{1,0:T(8,128)(2,1)S(1)}, bf16[144,896]{1,0:T(8,128)(2,1)S(1)}, u32[]{:S(2)}, u32[]{:S(2)}) collective-permute-start(bf16[144,896]{1,0:T(8,128)(2,1)S(1)} %get-tuple-element.24), channel_id=1, source_target_pairs={{0,2},{1,3},{2,0},{3,1},{4,6},{5,7},{6,4},{7,5},{8,10},{9,11},{10,... | collective-permute-start | bytes 774152 | tf_op jit(solution)/shard_map/ppermute | solution.py:157
  566.7 105.8 %collective-permute-start.23 = (bf16[144,896]{1,0:T(8,128)(2,1)S(1)}, bf16[144,896]{1,0:T(8,128)(2,1)S(1)}, u32[]{:S(2)}, u32[]{:S(2)}) collective-permute-start(bf16[144,896]{1,0:T(8,128)(2,1)S(1)} %get-tuple-element.26), channel_id=1, source_target_pairs={{0,4},{1,5},{2,6},{3,7},{4,0},{5,1},{6,2},{7,3},{8,12},{9,13},{10,... | collective-permute-start | bytes 774152 | tf_op jit(solution)/shard_map/ppermute | solution.py:157
  588.8 46.4 %collective-permute-start.12 = (bf16[56,2304]{1,0:T(8,128)(2,1)S(1)}, bf16[56,2304]{1,0:T(8,128)(2,1)S(1)}, u32[]{:S(2)}, u32[]{:S(2)}) collective-permute-start(bf16[56,2304]{1,0:T(8,128)(2,1)S(1)} %get-tuple-element.30), channel_id=1, source_target_pairs={{0,2},{1,3},{2,0},{3,1},{4,6},{5,7},{6,4},{7,5},{8,10},{9,11},{10,... | collective-permute-start | bytes 774152 | tf_op jit(solution)/shard_map/ppermute | solution.py:157
  610.8 27.4 %collective-permute-start.13 = (bf16[56,2304]{1,0:T(8,128)(2,1)S(1)}, bf16[56,2304]{1,0:T(8,128)(2,1)S(1)}, u32[]{:S(2)}, u32[]{:S(2)}) collective-permute-start(bf16[56,2304]{1,0:T(8,128)(2,1)S(1)} %get-tuple-element.32), channel_id=1, source_target_pairs={{0,4},{1,5},{2,6},{3,7},{4,0},{5,1},{6,2},{7,3},{8,12},{9,13},{10,... | collective-permute-start | bytes 774152 | tf_op jit(solution)/shard_map/ppermute | solution.py:157
  632.5 10.9 %collective-permute-start.14 = (bf16[56,2304]{1,0:T(8,128)(2,1)S(1)}, bf16[56,2304]{1,0:T(8,128)(2,1)S(1)}, u32[]{:S(2)}, u32[]{:S(2)}) collective-permute-start(bf16[56,2304]{1,0:T(8,128)(2,1)S(1)} %get-tuple-element.31), channel_id=1, source_target_pairs={{0,6},{1,7},{2,4},{3,5},{4,2},{5,3},{6,0},{7,1},{8,14},{9,15},{10,... | collective-permute-start | bytes 774152 | tf_op jit(solution)/shard_map/ppermute | solution.py:157
  635.2 12.4 %collective-permute-start.17 = (bf16[56,2304]{1,0:T(8,128)(2,1)S(1)}, bf16[56,2304]{1,0:T(8,128)(2,1)S(1)}, u32[]{:S(2)}, u32[]{:S(2)}) collective-permute-start(bf16[56,2304]{1,0:T(8,128)(2,1)S(1)} %get-tuple-element.33), channel_id=1, source_target_pairs={{0,2},{1,3},{2,0},{3,1},{4,6},{5,7},{6,4},{7,5},{8,10},{9,11},{10,... | collective-permute-start | bytes 774152 | tf_op jit(solution)/shard_map/ppermute | solution.py:157
  638.2 31.7 %collective-permute-start.18 = (bf16[56,2304]{1,0:T(8,128)(2,1)S(1)}, bf16[56,2304]{1,0:T(8,128)(2,1)S(1)}, u32[]{:S(2)}, u32[]{:S(2)}) collective-permute-start(bf16[56,2304]{1,0:T(8,128)(2,1)S(1)} %get-tuple-element.35), channel_id=1, source_target_pairs={{0,4},{1,5},{2,6},{3,7},{4,0},{5,1},{6,2},{7,3},{8,12},{9,13},{10,... | collective-permute-start | bytes 774152 | tf_op jit(solution)/shard_map/ppermute | solution.py:157
  643.4 26.5 %collective-permute-start.19 = (bf16[56,2304]{1,0:T(8,128)(2,1)S(1)}, bf16[56,2304]{1,0:T(8,128)(2,1)S(1)}, u32[]{:S(2)}, u32[]{:S(2)}) collective-permute-start(bf16[56,2304]{1,0:T(8,128)(2,1)S(1)} %get-tuple-element.34), channel_id=1, source_target_pairs={{0,6},{1,7},{2,4},{3,5},{4,2},{5,3},{6,0},{7,1},{8,14},{9,15},{10,... | collective-permute-start | bytes 774152 | tf_op jit(solution)/shard_map/ppermute | solution.py:157
  646.0 42.8 %collective-permute-start.24 = (bf16[144,896]{1,0:T(8,128)(2,1)S(1)}, bf16[144,896]{1,0:T(8,128)(2,1)S(1)}, u32[]{:S(2)}, u32[]{:S(2)}) collective-permute-start(bf16[144,896]{1,0:T(8,128)(2,1)S(1)} %get-tuple-element.25), channel_id=1, source_target_pairs={{0,6},{1,7},{2,4},{3,5},{4,2},{5,3},{6,0},{7,1},{8,14},{9,15},{10,... | collective-permute-start | bytes 774152 | tf_op jit(solution)/shard_map/ppermute | solution.py:157
  647.7 46.0 %collective-permute-start.27 = (bf16[144,896]{1,0:T(8,128)(2,1)S(1)}, bf16[144,896]{1,0:T(8,128)(2,1)S(1)}, u32[]{:S(2)}, u32[]{:S(2)}) collective-permute-start(bf16[144,896]{1,0:T(8,128)(2,1)S(1)} %get-tuple-element.27), channel_id=1, source_target_pairs={{0,2},{1,3},{2,0},{3,1},{4,6},{5,7},{6,4},{7,5},{8,10},{9,11},{10,... | collective-permute-start | bytes 774152 | tf_op jit(solution)/shard_map/ppermute | solution.py:157
  669.9 38.8 %collective-permute-start.28 = (bf16[144,896]{1,0:T(8,128)(2,1)S(1)}, bf16[144,896]{1,0:T(8,128)(2,1)S(1)}, u32[]{:S(2)}, u32[]{:S(2)}) collective-permute-start(bf16[144,896]{1,0:T(8,128)(2,1)S(1)} %get-tuple-element.29), channel_id=1, source_target_pairs={{0,4},{1,5},{2,6},{3,7},{4,0},{5,1},{6,2},{7,3},{8,12},{9,13},{10,... | collective-permute-start | bytes 774152 | tf_op jit(solution)/shard_map/ppermute | solution.py:157
  669.9 38.8 %collective-permute-start.29 = (bf16[144,896]{1,0:T(8,128)(2,1)S(1)}, bf16[144,896]{1,0:T(8,128)(2,1)S(1)}, u32[]{:S(2)}, u32[]{:S(2)}) collective-permute-start(bf16[144,896]{1,0:T(8,128)(2,1)S(1)} %get-tuple-element.28), channel_id=1, source_target_pairs={{0,6},{1,7},{2,4},{3,5},{4,2},{5,3},{6,0},{7,1},{8,14},{9,15},{10,... | collective-permute-start | bytes 774152 | tf_op jit(solution)/shard_map/ppermute | solution.py:157
  672.5 44.2 %collective-permute-start.2 = (bf16[56,2304]{1,0:T(8,128)(2,1)S(1)}, bf16[56,2304]{1,0:T(8,128)(2,1)S(1)}, u32[]{:S(2)}, u32[]{:S(2)}) collective-permute-start(bf16[56,2304]{1,0:T(8,128)(2,1)S(1)} %get-tuple-element.36), channel_id=1, source_target_pairs={{0,2},{1,3},{2,0},{3,1},{4,6},{5,7},{6,4},{7,5},{8,10},{9,11},{10,... | collective-permute-start | bytes 774152 | tf_op jit(solution)/shard_map/ppermute | solution.py:157
  688.8 42.1 %collective-permute-start.3 = (bf16[56,2304]{1,0:T(8,128)(2,1)S(1)}, bf16[56,2304]{1,0:T(8,128)(2,1)S(1)}, u32[]{:S(2)}, u32[]{:S(2)}) collective-permute-start(bf16[56,2304]{1,0:T(8,128)(2,1)S(1)} %get-tuple-element.38), channel_id=1, source_target_pairs={{0,4},{1,5},{2,6},{3,7},{4,0},{5,1},{6,2},{7,3},{8,12},{9,13},{10,... | collective-permute-start | bytes 774152 | tf_op jit(solution)/shard_map/ppermute | solution.py:157
  693.7 37.2 %collective-permute-start.4 = (bf16[56,2304]{1,0:T(8,128)(2,1)S(1)}, bf16[56,2304]{1,0:T(8,128)(2,1)S(1)}, u32[]{:S(2)}, u32[]{:S(2)}) collective-permute-start(bf16[56,2304]{1,0:T(8,128)(2,1)S(1)} %get-tuple-element.37), channel_id=1, source_target_pairs={{0,6},{1,7},{2,4},{3,5},{4,2},{5,3},{6,0},{7,1},{8,14},{9,15},{10,... | collective-permute-start | bytes 774152 | tf_op jit(solution)/shard_map/ppermute | solution.py:157
  708.7 23.1 %collective-permute-start.7 = (bf16[56,2304]{1,0:T(8,128)(2,1)S(1)}, bf16[56,2304]{1,0:T(8,128)(2,1)S(1)}, u32[]{:S(2)}, u32[]{:S(2)}) collective-permute-start(bf16[56,2304]{1,0:T(8,128)(2,1)S(1)} %get-tuple-element.39), channel_id=1, source_target_pairs={{0,2},{1,3},{2,0},{3,1},{4,6},{5,7},{6,4},{7,5},{8,10},{9,11},{10,... | collective-permute-start | bytes 774152 | tf_op jit(solution)/shard_map/ppermute | solution.py:157
  708.7 33.2 %collective-permute-start.8 = (bf16[56,2304]{1,0:T(8,128)(2,1)S(1)}, bf16[56,2304]{1,0:T(8,128)(2,1)S(1)}, u32[]{:S(2)}, u32[]{:S(2)}) collective-permute-start(bf16[56,2304]{1,0:T(8,128)(2,1)S(1)} %get-tuple-element.41), channel_id=1, source_target_pairs={{0,4},{1,5},{2,6},{3,7},{4,0},{5,1},{6,2},{7,3},{8,12},{9,13},{10,... | collective-permute-start | bytes 774152 | tf_op jit(solution)/shard_map/ppermute | solution.py:157
  716.7 25.2 %collective-permute-start.9 = (bf16[56,2304]{1,0:T(8,128)(2,1)S(1)}, bf16[56,2304]{1,0:T(8,128)(2,1)S(1)}, u32[]{:S(2)}, u32[]{:S(2)}) collective-permute-start(bf16[56,2304]{1,0:T(8,128)(2,1)S(1)} %get-tuple-element.40), channel_id=1, source_target_pairs={{0,6},{1,7},{2,4},{3,5},{4,2},{5,3},{6,0},{7,1},{8,14},{9,15},{10,... | collective-permute-start | bytes 774152 | tf_op jit(solution)/shard_map/ppermute | solution.py:157

commit v2 on v1

--- a/solution.py
+++ b/solution.py
@@ -131,9 +131,101 @@
         ],
         compiler_params=pltpu.CompilerParams(collective_id=0, has_side_effects=True),
     )(gu, w_down)
-    gu = gu.reshape(2, layers, n * rows, ff)
-    down = down.reshape(layers, n * rows_d, d)
-    return [(gu[0, l], gu[1, l], down[l]) for l in range(layers)]
+    return gu.reshape(2, layers, n * rows, ff), down.reshape(layers, n * rows_d, d)
+
+
+TILE, CHUNK = 512, 768
+
+
+def mm(a, b, cb=0):
+    return lax.dot_general(a, b, (((1,), (cb,)), ((), ())), preferred_element_type=jnp.float32)
+
+
+def normed(h):
+    wide = h.astype(jnp.float32)
+    scale = lax.rsqrt(jnp.mean(wide**2, -1, keepdims=True) + 1e-6)
+    return wide, scale
+
+
+def chunks(ff):
+    return [pl.ds(i, CHUNK) for i in range(0, ff, CHUNK)]
+
+
+def forward_kernel(h_ref, wg, wu, wd, next_ref, a_ref, p_ref, gate_ref, up_ref):
+    wide, scale = normed(h_ref[...])
+    a = (wide * scale).astype(jnp.bfloat16)
+    a_ref[...] = a
+    total = None
+    for c in chunks(wg.shape[-1]):
+        gate, up = mm(a, wg[:, c]), mm(a, wu[:, c])
+        gate_ref[:, c], up_ref[:, c] = gate, up
+        p = (gate * jax.nn.sigmoid(gate) * up).astype(jnp.bfloat16)
+        p_ref[:, c] = p
+        part = mm(p, wd[c, :])
+        total = part if total is None else total + part
+    next_ref[...] = (wide + total.astype(jnp.bfloat16).astype(jnp.float32)).astype(jnp.bfloat16)
+
+
+def through_gate(gate, up, dp):
+    dp = dp.astype(jnp.bfloat16).astype(jnp.float32)
+    s = jax.nn.sigmoid(gate)
+    silu = gate * s
+    dgate = (dp * up * (s * (1 + gate * (1 - s)))).astype(jnp.bfloat16)
+    return silu, dgate, (dp * silu).astype(jnp.bfloat16)
+
+
+def through_norm(wide, scale, dy, da_gate, da_up):
+    bf16, f32 = jnp.bfloat16, jnp.float32
+    da = (da_gate.astype(bf16).astype(f32) + da_up.astype(bf16).astype(f32)).astype(bf16).astype(f32)
+    dh = scale * (da - wide * (scale**2 * jnp.mean(da * wide, -1, keepdims=True)))
+    return (dy.astype(f32) + dh.astype(bf16).astype(f32)).astype(bf16)
+
+
+def last_kernel(h_ref, dy_ref, wg, wu, wd, dh_ref, a_ref, p_ref, dgate_ref, dup_ref):
+    wide, scale = normed(h_ref[...])
+    a = (wide * scale).astype(jnp.bfloat16)
+    a_ref[...] = a
+    dy = dy_ref[...]
+    da_gate = da_up = None
+    for c in chunks(wg.shape[-1]):
+        gate, up = mm(a, wg[:, c]), mm(a, wu[:, c])
+        silu, dgate, dup = through_gate(gate, up, mm(dy, wd[c, :], 1))
+        p_ref[:, c] = (silu * up).astype(jnp.bfloat16)
+        dgate_ref[:, c], dup_ref[:, c] = dgate, dup
+        g, u = mm(dgate, wg[:, c], 1), mm(dup, wu[:, c], 1)
+        da_gate, da_up = (g, u) if da_gate is None else (da_gate + g, da_up + u)
+    dh_ref[...] = through_norm(wide, scale, dy, da_gate, da_up)
+
+
+def gate_kernel(dy_ref, gate_ref, up_ref, wd, dgate_ref, dup_ref):
+    dy = dy_ref[...]
+    for c in chunks(gate_ref.shape[-1]):
+        _, dgate_ref[:, c], dup_ref[:, c] = through_gate(gate_ref[:, c], up_ref[:, c], mm(dy, wd[c, :], 1))
+
+
+def input_kernel(h_ref, dy_ref, dgate_ref, dup_ref, wg, wu, dh_ref):
+    wide, scale = normed(h_ref[...])
+    da_gate, da_up = mm(dgate_ref[...], wg[...], 1), mm(dup_ref[...], wu[...], 1)
+    dh_ref[...] = through_norm(wide, scale, dy_ref[...], da_gate, da_up)
+
+
+def call(kernel, tokens, weights, outs, matmuls):
+    t = tokens[0].shape[0]
+    d, ff = 896, 2304
+    specs = [pl.BlockSpec((TILE, v.shape[1]), lambda i: (i, 0)) for v in tokens]
+    for w, at in weights:
+        specs.append(
+            pl.BlockSpec((None,) * len(at) + w.shape[-2:], lambda i, at=at: (*at, 0, 0), pipeline_mode=pl.Buffered(1))
+        )
+    return pl.pallas_call(
+        kernel,
+        grid=(t // TILE,),
+        in_specs=specs,
+        out_specs=[pl.BlockSpec((TILE, n), lambda i: (i, 0)) for n, _ in outs],
+        out_shape=[jax.ShapeDtypeStruct((t, n), dtype) for n, dtype in outs],
+        compiler_params=pltpu.CompilerParams(vmem_limit_bytes=60 * 2**20, dimension_semantics=("arbitrary",)),
+        cost_estimate=pl.CostEstimate(flops=2 * t * d * ff * matmuls, bytes_accessed=30 * 2**20, transcendentals=t * ff),
+    )(*tokens, *(w for w, _ in weights))
 
 
 def dot(a, b, ca, cb):
@@ -147,7 +239,7 @@
 def scatter_sum(term):
     me = lax.axis_index("dp")
     y, z, c = me // 8, (me // 2) % 4, me % 2
-    term = term.reshape(2, Z, 2, -1, term.shape[-1])
+    term = lax.optimization_barrier(term).reshape(2, Z, 2, -1, term.shape[-1])
 
     def pick(t, i, axis):
         return lax.dynamic_index_in_dim(t, i, axis, keepdims=False)
@@ -174,36 +266,24 @@
     def work(x, dy, w_gate, w_up, w_down):
         x, dy = x[0], dy[0]
         bf16, f32 = jnp.bfloat16, jnp.float32
-        weights = gather(w_gate, w_up, w_down)
-        h, saved = x, []
-        for wg, wu, wd in weights:
-            wide = h.astype(f32)
-            scale = lax.rsqrt(jnp.mean(wide**2, -1, keepdims=True) + 1e-6)
-            a = (wide * scale).astype(bf16)
-            gate, up = dot(a, wg, 1, 0), dot(a, wu, 1, 0)
-            p = (jax.nn.silu(gate) * up).astype(bf16)
-            saved.append((h, scale, a, gate, up, p))
-            if len(saved) < len(weights):
-                h = h + dot(p, wd, 1, 0).astype(bf16)
-        outs = []
-        for l in reversed(range(len(weights))):
-            wg, wu, wd = weights[l]
-            h, scale, a, gate, up, p = saved[l]
-            by_d = scatter_sum(dot(p, dy, 0, 0))
-            dp = dot(dy, wd, 1, 1).astype(bf16).astype(f32)
-            s = jax.nn.sigmoid(gate)
-            silu = gate * s
-            dup = (dp * silu).astype(bf16)
-            dgate = (dp * up * (s * (1 + gate * (1 - s)))).astype(bf16)
-            by_g = scatter_sum(dot(a, dgate, 0, 0))
-            by_u = scatter_sum(dot(a, dup, 0, 0))
-            da = (dot(dgate, wg, 1, 1).astype(bf16) + dot(dup, wu, 1, 1).astype(bf16)).astype(f32)
-            wide = h.astype(f32)
-            dh = scale * (da - wide * (scale**2 * jnp.mean(da * wide, -1, keepdims=True)))
-            dy = dy + dh.astype(bf16)
-            outs.append((by_g, by_u, by_d))
-        outs = outs[::-1]
-        return (dy[None], *(jnp.stack([o[i] for o in outs]) for i in range(3)))
+        gu, down = gather(w_gate, w_up, w_down)
+        d, ff = x.shape[1], gu.shape[-1]
+        wg, wu, wd = [[(gu, (0, l)) for l in (0, 1)], [(gu, (1, l)) for l in (0, 1)], [(down, (l,)) for l in (0, 1)]]
+        h, a0, p0, gate, up = call(
+            forward_kernel, (x,), (wg[0], wu[0], wd[0]), [(d, bf16), (d, bf16), (ff, bf16), (ff, f32), (ff, f32)], 3
+        )
+        dy0, a1, p1, dgate1, dup1 = call(
+            last_kernel, (h, dy), (wg[1], wu[1], wd[1]), [(d, bf16), (d, bf16), (ff, bf16), (ff, bf16), (ff, bf16)], 5
+        )
+        d1 = scatter_sum(dot(p1, dy, 0, 0))
+        g1 = scatter_sum(dot(a1, dgate1, 0, 0))
+        u1 = scatter_sum(dot(a1, dup1, 0, 0))
+        d0 = scatter_sum(dot(p0, dy0, 0, 0))
+        dgate0, dup0 = call(gate_kernel, (dy0, gate, up), (wd[0],), [(ff, bf16), (ff, bf16)], 1)
+        g0 = scatter_sum(dot(a0, dgate0, 0, 0))
+        u0 = scatter_sum(dot(a0, dup0, 0, 0))
+        (dx,) = call(input_kernel, (x, dy0, dgate0, dup0), (wg[0], wu[0]), [(d, bf16)], 2)
+        return dx[None], jnp.stack([g0, g1]), jnp.stack([u0, u1]), jnp.stack([d0, d1])
 
     rows = P(("rep", "dp"), None, None)
     w = P(None, "dp", None)

time: 757 us -> 640 us (0.85)
  matrix products: 277 us -> 75.4 us
  Pallas kernels: 115 us -> 273 us
  local copies, waits for them, and re-layouts: 69.4 us -> 30.2 us
  other arithmetic: 59.2 us -> 28.3 us
    dot_general x17 -> x6, matrix products: 277 us -> 75.4 us  [dot(): lax.dot_general(a, b, (((ca,), (cb,)), ((), ())), preferred_element_type=...]
    pallas_call x0 -> x4, Pallas kernels: none -> 158 us  [call(): pl.pallas_call(kernel, grid=(t // TILE,), in_specs=specs, out_specs=[pl.B...]
    unnamed x55 -> x38, local copies, waits for them, and re-layouts: 33.6 us -> 12.5 us
    convert_element_type x1 -> x0, other arithmetic: 17.3 us -> none  [work(): p = (jax.nn.silu(gate) * up).astype(bf16)]
    convert_element_type x1 -> x0, local copies, waits for them, and re-layouts: 12.7 us -> none  [work(): p = (jax.nn.silu(gate) * up).astype(bf16)]
    broadcast_in_dim x1 -> x0, other arithmetic: 9.02 us -> none  [work(): return (dy[None], *(jnp.stack([o[i] for o in outs]) for i in range(3)))]
  transfers between devices with their start and end apart: 30 -> 30, of which waited for: 12 -> 12; matrix products, arithmetic and copies ran while one was open for 28% -> 16% of each run, Pallas kernels for 0% -> 9%
where the time goes in v2:
time: 640 us; the launch traced here: 630 us
  Pallas kernels  273 us (43%)
  waiting for transfers between devices  148 us (23%)
  matrix products  75.4 us (12%)
  starting transfers between devices  73.7 us (12%)
  local copies, waits for them, and re-layouts  30.2 us (5%)
  other arithmetic  28.3 us (4%)
    pallas_call x4, Pallas kernels, call(): pl.pallas_call(kernel, grid=(t // TILE,), in_specs=specs, out_specs=[pl.B...  158 us
    ppermute x30, waiting for transfers between devices, swap(): t = lax.ppermute(t, 'dp', pairs(of))  148 us
    pallas_call x1, Pallas kernels, gather(): pl.pallas_call(gather_kernel, out_shape=(jax.ShapeDtypeStruct((2, layers,...  115 us
    dot_general x6, matrix products, dot(): lax.dot_general(a, b, (((ca,), (cb,)), ((), ())), preferred_element_type=...  75.4 us
    ppermute x30, starting transfers between devices, swap(): t = lax.ppermute(t, 'dp', pairs(of))  73.7 us
    convert_element_type x18, local copies, waits for them, and re-layouts, swap(): t = t.astype(jnp.bfloat16)  17.7 us
    add x6, other arithmetic, scatter_sum(): term = pick(term, c, 2) + got  16.6 us
  transfers between devices with their start and end apart: 30, of which 12 were waited for; matrix products, arithmetic and copies ran while one was open for 16% of the time, Pallas kernels for 9%

profile of v2, /device:TPU:4, one launch (start us, length us, event | category | flops | bytes accessed | tf_op | source)
XLA Modules:
  0.0 629.8 jit_solution(11782973832681921038)
XLA Ops:
  0.6 2.3 pad_maximum_fusion.gu_ref
  2.9 115.0 %shard_map.84 = (bf16[2,2,16,56,2304]{4,3,2,1,0:T(8,128)(2,1)}, bf16[2,16,144,896]{3,2,1,0:T(8,128)(2,1)}) custom-call(bf16[2,2,56,2304]{3,2,1,0:T(8,128)(2,1)} %pad_maximum_fusion.gu_ref, bf16[2,144,896]{2,1,0:T(8,128)(2,1)} %d_ref.1), custom_call_target="tpu_custom_call" | custom-call | tf_op jit(solution)/shard_map/pallas_call | solution.py:120
  117.9 39.7 %shard_map.85 = (bf16[2048,896]{1,0:T(8,128)(2,1)}, bf16[2048,896]{1,0:T(8,128)(2,1)}, bf16[2048,2304]{1,0:T(8,128)(2,1)}, f32[2048,2304]{1,0:T(8,128)}, f32[2048,2304]{1,0:T(8,128)}) custom-call(bf16[2048,896]{1,0:T(8,128)(2,1)} %bitcast.235, bf16[2,2,896,2304]{3,2,1,0:T(8,128)(2,1)} %bitcast.206, bf16[2,2,896,2304]{3,2,1,0:T(8,128)(2,1)} %bitcast.207, ...), custom_call_target="tpu_custom_call" | custom-call | flops 25367150592 | bytes 31457280 | tf_op jit(solution)/shard_map/pallas_call | solution.py:220
  157.5 61.6 %shard_map.86 = (bf16[2048,896]{1,0:T(8,128)(2,1)}, bf16[2048,896]{1,0:T(8,128)(2,1)}, bf16[2048,2304]{1,0:T(8,128)(2,1)}, bf16[2048,2304]{1,0:T(8,128)(2,1)}, bf16[2048,2304]{1,0:T(8,128)(2,1)}) custom-call(bf16[2048,896]{1,0:T(8,128)(2,1)} %get-tuple-element.20.h_ref, bf16[2048,896]{1,0:T(8,128)(2,1)} %bitcast.240, bf16[2,2,896,2304]{3,2,1,0:T(8,128)(2,1)} %bitcast.208, ...), custom_call_target="tpu_custom_call" | custom-call | flops 42278584320 | bytes 31457280 | tf_op jit(solution)/shard_map/pallas_call | solution.py:220
  219.1 16.1 %fusion.60 = f32[2304,896]{1,0:T(8,128)} fusion(bf16[2048,2304]{1,0:T(8,128)(2,1)} %get-tuple-element.30, bf16[2048,896]{1,0:T(8,128)(2,1)} %get-tuple-element.21.dy_ref), kind=kOutput, calls=%fused_computation.112 | convolution fusion | flops 8455716864 | bytes 21364736 | tf_op jit(solution)/shard_map/dot_general | solution.py:232
  235.3 3.8 fusion.4
  239.6 12.8 %fusion.54 = f32[2304,896]{1,0:T(8,128)S(1)} fusion(bf16[2048,2304]{1,0:T(8,128)(2,1)} %get-tuple-element.31, bf16[1,2048,896]{2,1,0:T(8,128)(2,1)S(1)} %copy-done.4), kind=kOutput, calls=%fused_computation.106 | convolution fusion | flops 8455716864 | bytes 21364736 | tf_op jit(solution)/shard_map/dot_general | solution.py:232
  252.4 3.3 copy-done.2
  255.7 1.6 fusion.5
  257.3 27.3 %shard_map.87 = (bf16[2048,2304]{1,0:T(8,128)(2,1)}, bf16[2048,2304]{1,0:T(8,128)(2,1)}) custom-call(bf16[2048,896]{1,0:T(8,128)(2,1)} %get-tuple-element.21.dy_ref, f32[2048,2304]{1,0:T(8,128)} %get-tuple-element.22.gate_ref, f32[2048,2304]{1,0:T(8,128)} %get-tuple-element.23.up_ref, bf16[2,2304,896]{2,1,0:T(8,128)(2,1)} %bitcast.216), custom_call_target="tpu_custom_call" | custom-call | flops 8455716864 | bytes 31457280 | tf_op jit(solution)/shard_map/pallas_call | solution.py:220
  284.6 11.3 %fusion.58 = f32[896,2304]{1,0:T(8,128)S(1)} fusion(bf16[2048,896]{1,0:T(8,128)(2,1)S(1)} %copy-done.6, bf16[2048,2304]{1,0:T(8,128)(2,1)} %get-tuple-element.25.dup_ref), kind=kOutput, calls=%fused_computation.110 | convolution fusion | flops 8455716864 | bytes 21364736 | tf_op jit(solution)/shard_map/dot_general | solution.py:232
  295.9 1.5 fusion.2
  297.9 3.1 copy-done.3
  301.1 12.5 %fusion.59 = f32[896,2304]{1,0:T(8,128)S(1)} fusion(bf16[2048,896]{1,0:T(8,128)(2,1)S(1)} %copy-done.5, bf16[2048,2304]{1,0:T(8,128)(2,1)} %get-tuple-element.29), kind=kOutput, calls=%fused_computation.111 | convolution fusion | flops 8455716864 | bytes 21364736 | tf_op jit(solution)/shard_map/dot_general | solution.py:232
  313.6 1.6 fusion.3
  315.6 2.8 copy-done.1
  318.5 11.4 %fusion.56 = f32[896,2304]{1,0:T(8,128)S(1)} fusion(bf16[2048,896]{1,0:T(8,128)(2,1)} %get-tuple-element.26, bf16[2048,2304]{1,0:T(8,128)(2,1)S(1)} %bitcast.213), kind=kOutput, calls=%fused_computation.108 | convolution fusion | flops 8455716864 | bytes 21364736 | tf_op jit(solution)/shard_map/dot_general | solution.py:232
  329.8 3.2 copy-done
  333.8 11.4 %fusion.57 = f32[896,2304]{1,0:T(8,128)} fusion(bf16[2048,896]{1,0:T(8,128)(2,1)S(1)} %copy-done.5, bf16[2048,2304]{1,0:T(8,128)(2,1)S(1)} %bitcast.242), kind=kOutput, calls=%fused_computation.109 | convolution fusion | flops 8455716864 | bytes 21364736 | tf_op jit(solution)/shard_map/dot_general | solution.py:232
  345.2 3.7 fusion.1
  348.9 29.6 %shard_map.88 = bf16[2048,896]{1,0:T(8,128)(2,1)} custom-call(bf16[2048,896]{1,0:T(8,128)(2,1)} %bitcast.236, bf16[2048,896]{1,0:T(8,128)(2,1)} %get-tuple-element.21.dy_ref, bf16[2048,2304]{1,0:T(8,128)(2,1)} %get-tuple-element.24.dgate_ref, bf16[2048,2304]{1,0:T(8,128)(2,1)} %get-tuple-element.25.dup_ref, bf16[2,2,896,2304]{3,2,1,0:T(8,128)(2,1)} %bitcast.210, ...), custom_call_target="tpu_custom_call" | custom-call | flops 16911433728 | bytes 31457280 | tf_op jit(solution)/shard_map/pallas_call | solution.py:220
  378.6 3.3 bitcast_add_fusion.1
  381.9 1.1 fusion.10
  384.0 3.4 bitcast_add_fusion
  387.4 1.1 fusion.11
  389.5 2.2 bitcast_add_fusion.3
  391.7 1.1 fusion.8
  392.8 1.0 collective-permute-start.11
  393.8 2.2 bitcast_add_fusion.2
  396.1 1.1 fusion.9
  397.2 1.0 collective-permute-start.16
  398.2 3.4 bitcast_add_fusion.5
  401.7 1.1 collective-permute-start.1
  402.8 2.1 bitcast_add_fusion.4
  404.9 4.1 collective-permute-done.21
  410.0 1.4 bitcast_add_fusion.7
  411.5 19.6 %collective-permute-done.26 = bf16[4,144,896]{2,1,0:T(8,128)(2,1)} collective-permute-done((bf16[4,144,896]{2,1,0:T(8,128)(2,1)}, bf16[4,144,896]{2,1,0:T(8,128)(2,1)}, u32[]{:S(2)}, u32[]{:S(2)}) %collective-permute-start.26) | collective-permute-done | bytes 1032224 | tf_op jit(solution)/shard_map/ppermute | solution.py:249
  431.2 4.3 collective-permute-start.22
  435.5 1.4 bitcast_add_fusion.6
  437.0 16.2 %collective-permute-done.11 = bf16[4,56,2304]{2,1,0:T(8,128)(2,1)} collective-permute-done((bf16[4,56,2304]{2,1,0:T(8,128)(2,1)}, bf16[4,56,2304]{2,1,0:T(8,128)(2,1)}, u32[]{:S(2)}, u32[]{:S(2)}) %collective-permute-start.11) | collective-permute-done | bytes 1032224 | tf_op jit(solution)/shard_map/ppermute | solution.py:249
  453.3 4.8 collective-permute-start.23
  458.1 1.4 bitcast_add_fusion.9
  459.6 15.8 %collective-permute-done.16 = bf16[4,56,2304]{2,1,0:T(8,128)(2,1)} collective-permute-done((bf16[4,56,2304]{2,1,0:T(8,128)(2,1)}, bf16[4,56,2304]{2,1,0:T(8,128)(2,1)}, u32[]{:S(2)}, u32[]{:S(2)}) %collective-permute-start.16) | collective-permute-done | bytes 1032224 | tf_op jit(solution)/shard_map/ppermute | solution.py:249
  475.4 4.3 collective-permute-start.12
  479.7 1.4 bitcast_add_fusion.8
  481.3 16.1 %collective-permute-done.1 = bf16[4,56,2304]{2,1,0:T(8,128)(2,1)S(1)} collective-permute-done((bf16[4,56,2304]{2,1,0:T(8,128)(2,1)S(1)}, bf16[4,56,2304]{2,1,0:T(8,128)(2,1)S(1)}, u32[]{:S(2)}, u32[]{:S(2)}) %collective-permute-start.1) | collective-permute-done | bytes 1032224 | tf_op jit(solution)/shard_map/ppermute | solution.py:249
  497.4 4.8 collective-permute-start.13
  502.5 16.5 %collective-permute-done.6 = bf16[4,56,2304]{2,1,0:T(8,128)(2,1)S(1)} collective-permute-done((bf16[4,56,2304]{2,1,0:T(8,128)(2,1)S(1)}, bf16[4,56,2304]{2,1,0:T(8,128)(2,1)S(1)}, u32[]{:S(2)}, u32[]{:S(2)}) %collective-permute-start.6) | collective-permute-done | bytes 1032224 | tf_op jit(solution)/shard_map/ppermute | solution.py:249
  519.0 2.4 collective-permute-start.14
  521.7 3.1 collective-permute-start.17
  525.3 4.7 collective-permute-done.14
  530.0 2.4 collective-permute-start.19
  532.5 1.5 collective-permute-start.24
  534.1 4.2 collective-permute-start.27
  538.4 18.0 %collective-permute-done.18 = bf16[56,2304]{1,0:T(8,128)(2,1)S(1)} collective-permute-done((bf16[56,2304]{1,0:T(8,128)(2,1)S(1)}, bf16[56,2304]{1,0:T(8,128)(2,1)S(1)}, u32[]{:S(2)}, u32[]{:S(2)}) %collective-permute-start.18) | collective-permute-done | bytes 258080 | tf_op jit(solution)/shard_map/ppermute | solution.py:249
  556.4 2.4 collective-permute-start.29
  558.9 16.3 %collective-permute-start.2 = (bf16[56,2304]{1,0:T(8,128)(2,1)S(1)}, bf16[56,2304]{1,0:T(8,128)(2,1)S(1)}, u32[]{:S(2)}, u32[]{:S(2)}) collective-permute-start(bf16[56,2304]{1,0:T(8,128)(2,1)S(1)} %get-tuple-element.44), channel_id=1, source_target_pairs={{0,2},{1,3},{2,0},{3,1},{4,6},{5,7},{6,4},{7,5},{8,10},{9,11},{10,... | collective-permute-start | bytes 774152 | tf_op jit(solution)/shard_map/ppermute | solution.py:249
  575.2 4.8 collective-permute-start.3
  580.1 1.5 collective-permute-start.4
  581.6 13.5 %collective-permute-done.28 = bf16[144,896]{1,0:T(8,128)(2,1)S(1)} collective-permute-done((bf16[144,896]{1,0:T(8,128)(2,1)S(1)}, bf16[144,896]{1,0:T(8,128)(2,1)S(1)}, u32[]{:S(2)}, u32[]{:S(2)}) %collective-permute-start.28) | collective-permute-done | bytes 258080 | tf_op jit(solution)/shard_map/ppermute | solution.py:249
  595.1 7.0 %collective-permute-start.8 = (bf16[56,2304]{1,0:T(8,128)(2,1)S(1)}, bf16[56,2304]{1,0:T(8,128)(2,1)S(1)}, u32[]{:S(2)}, u32[]{:S(2)}) collective-permute-start(bf16[56,2304]{1,0:T(8,128)(2,1)S(1)} %get-tuple-element.49), channel_id=1, source_target_pairs={{0,4},{1,5},{2,6},{3,7},{4,0},{5,1},{6,2},{7,3},{8,12},{9,13},{10,... | collective-permute-start | bytes 774152 | tf_op jit(solution)/shard_map/ppermute | solution.py:249
  603.1 1.5 collective-permute-start.9
  604.6 12.7 %collective-permute-done.3 = bf16[56,2304]{1,0:T(8,128)(2,1)S(1)} collective-permute-done((bf16[56,2304]{1,0:T(8,128)(2,1)S(1)}, bf16[56,2304]{1,0:T(8,128)(2,1)S(1)}, u32[]{:S(2)}, u32[]{:S(2)}) %collective-permute-start.3) | collective-permute-done | bytes 258080 | tf_op jit(solution)/shard_map/ppermute | solution.py:249
  618.3 10.1 %collective-permute-done.8 = bf16[56,2304]{1,0:T(8,128)(2,1)S(1)} collective-permute-done((bf16[56,2304]{1,0:T(8,128)(2,1)S(1)}, bf16[56,2304]{1,0:T(8,128)(2,1)S(1)}, u32[]{:S(2)}, u32[]{:S(2)}) %collective-permute-start.8) | collective-permute-done | bytes 258080 | tf_op jit(solution)/shard_map/ppermute | solution.py:249
  (90 shorter events, 10.5 us)
Async XLA Ops:
  235.3 4.4 copy-start.4
  239.1 139.4 %collective-permute-start.20 = (bf16[2,4,144,896]{3,2,1,0:T(8,128)(2,1)}, bf16[2,4,144,896]{3,2,1,0:T(8,128)(2,1)}, u32[]{:S(2)}, u32[]{:S(2)}) collective-permute-start(bf16[2,4,144,896]{3,2,1,0:T(8,128)(2,1)} %fusion.4), channel_id=1, source_target_pairs={{0,1},{1,0},{2,3},{3,2},{4,5},{5,4},{6,7},{7,6},{8,9},{9,8},{10,11... | collective-permute-start | bytes 6193160 | tf_op jit(solution)/shard_map/ppermute | solution.py:249
  252.4 3.3 copy-start.2
  257.3 125.8 %collective-permute-start.25 = (bf16[2,4,144,896]{3,2,1,0:T(8,128)(2,1)}, bf16[2,4,144,896]{3,2,1,0:T(8,128)(2,1)}, u32[]{:S(2)}, u32[]{:S(2)}) collective-permute-start(bf16[2,4,144,896]{3,2,1,0:T(8,128)(2,1)} %fusion.5), channel_id=1, source_target_pairs={{0,1},{1,0},{2,3},{3,2},{4,5},{5,4},{6,7},{7,6},{8,9},{9,8},{10,11... | collective-permute-start | bytes 6193160 | tf_op jit(solution)/shard_map/ppermute | solution.py:249
  257.3 27.3 %copy-start.6 = (bf16[2048,896]{1,0:T(8,128)(2,1)S(1)}, bf16[2048,896]{1,0:T(8,128)(2,1)}, u32[]{:S(2)}) copy-start(bf16[2048,896]{1,0:T(8,128)(2,1)} %get-tuple-element.26) | copy-start | bytes 11010052
  295.9 5.2 copy-start.3
  295.9 5.2 copy-start.5
  295.9 22.5 %slice-start = ((s8[9437184]{0:T(1024)(128)(4,1)}), s8[4194304]{0:T(1024)(128)(4,1)S(1)}, s32[]{:S(2)}) async-start(s8[9437184]{0:T(1024)(128)(4,1)} %bitcast.212), calls=%async_computation | async-start | bytes 8388608
  297.5 91.0 %collective-permute-start.10 = (bf16[2,4,56,2304]{3,2,1,0:T(8,128)(2,1)}, bf16[2,4,56,2304]{3,2,1,0:T(8,128)(2,1)}, u32[]{:S(2)}, u32[]{:S(2)}) collective-permute-start(bf16[2,4,56,2304]{3,2,1,0:T(8,128)(2,1)} %fusion.2), channel_id=1, source_target_pairs={{0,1},{1,0},{2,3},{3,2},{4,5},{5,4},{6,7},{7,6},{8,9},{9,8},{10,11... | collective-permute-start | bytes 6193160 | tf_op jit(solution)/shard_map/ppermute | solution.py:249
  301.1 17.4 %slice-start.1 = ((s8[9437184]{0:T(1024)(128)(4,1)}), s8[4194304]{0:T(1024)(128)(4,1)S(1)}, s32[]{:S(2)}) async-start(s8[9437184]{0:T(1024)(128)(4,1)} %bitcast.212), calls=%async_computation.1 | async-start | bytes 8388608
  301.1 17.4 %slice-start.2 = ((s8[9437184]{0:T(1024)(128)(4,1)}), s8[1048576]{0:T(1024)(128)(4,1)S(1)}, s32[]{:S(2)}) async-start(s8[9437184]{0:T(1024)(128)(4,1)} %bitcast.212), calls=%async_computation.2 | async-start | bytes 2097152
  313.5 4.9 copy-start.1
  313.5 20.2 %slice-start.9 = ((s8[9437184]{0:T(1024)(128)(4,1)}), s8[4194304]{0:T(1024)(128)(4,1)S(1)}, s32[]{:S(2)}) async-start(s8[9437184]{0:T(1024)(128)(4,1)} %bitcast.241), calls=%async_computation.9 | async-start | bytes 8388608
  315.1 77.7 %collective-permute-start.15 = (bf16[2,4,56,2304]{3,2,1,0:T(8,128)(2,1)}, bf16[2,4,56,2304]{3,2,1,0:T(8,128)(2,1)}, u32[]{:S(2)}, u32[]{:S(2)}) collective-permute-start(bf16[2,4,56,2304]{3,2,1,0:T(8,128)(2,1)} %fusion.3), channel_id=1, source_target_pairs={{0,1},{1,0},{2,3},{3,2},{4,5},{5,4},{6,7},{7,6},{8,9},{9,8},{10,11... | collective-permute-start | bytes 6193160 | tf_op jit(solution)/shard_map/ppermute | solution.py:249
  318.4 15.4 %slice-start.10 = ((s8[9437184]{0:T(1024)(128)(4,1)}), s8[4194304]{0:T(1024)(128)(4,1)S(1)}, s32[]{:S(2)}) async-start(s8[9437184]{0:T(1024)(128)(4,1)} %bitcast.241), calls=%async_computation.10 | async-start | bytes 8388608
  318.5 15.3 %slice-start.11 = ((s8[9437184]{0:T(1024)(128)(4,1)}), s8[1048576]{0:T(1024)(128)(4,1)S(1)}, s32[]{:S(2)}) async-start(s8[9437184]{0:T(1024)(128)(4,1)} %bitcast.241), calls=%async_computation.11 | async-start | bytes 2097152
  329.8 3.2 copy-start
  333.2 63.9 %collective-permute-start = (bf16[2,4,56,2304]{3,2,1,0:T(8,128)(2,1)S(1)}, bf16[2,4,56,2304]{3,2,1,0:T(8,128)(2,1)}, u32[]{:S(2)}, u32[]{:S(2)}) collective-permute-start(bf16[2,4,56,2304]{3,2,1,0:T(8,128)(2,1)S(1)} %fusion), channel_id=1, source_target_pairs={{0,1},{1,0},{2,3},{3,2},{4,5},{5,4},{6,7},{7,6},{8,9},{9,8},{10,11... | collective-permute-start | bytes 6193160 | tf_op jit(solution)/shard_map/ppermute | solution.py:249
  378.5 23.2 %collective-permute-start.5 = (bf16[2,4,56,2304]{3,2,1,0:T(8,128)(2,1)}, bf16[2,4,56,2304]{3,2,1,0:T(8,128)(2,1)}, u32[]{:S(2)}, u32[]{:S(2)}) collective-permute-start(bf16[2,4,56,2304]{3,2,1,0:T(8,128)(2,1)} %fusion.1), channel_id=1, source_target_pairs={{0,1},{1,0},{2,3},{3,2},{4,5},{5,4},{6,7},{7,6},{8,9},{9,8},{10,11... | collective-permute-start | bytes 6193160 | tf_op jit(solution)/shard_map/ppermute | solution.py:249
  378.6 10.8 %slice-start.7 = ((s8[8257536]{0:T(1024)(128)(4,1)}), s8[4194304]{0:T(1024)(128)(4,1)S(1)}, s32[]{:S(2)}) async-start(s8[8257536]{0:T(1024)(128)(4,1)} %bitcast.232), calls=%async_computation.7 | async-start | bytes 8388608
  383.0 6.4 %slice-start.8 = ((s8[8257536]{0:T(1024)(128)(4,1)}), s8[4063232]{0:T(1024)(128)(4,1)S(1)}, s32[]{:S(2)}) async-start(s8[8257536]{0:T(1024)(128)(4,1)} %bitcast.232), calls=%async_computation.8 | async-start | bytes 8126464
  383.0 26.0 %collective-permute-start.21 = (bf16[4,144,896]{2,1,0:T(8,128)(2,1)}, bf16[4,144,896]{2,1,0:T(8,128)(2,1)}, u32[]{:S(2)}, u32[]{:S(2)}) collective-permute-start(bf16[4,144,896]{2,1,0:T(8,128)(2,1)} %fusion.10), channel_id=1, source_target_pairs={{0,8},{1,9},{2,10},{3,11},{4,12},{5,13},{6,14},{7,15},{8,0},{9,1},... | collective-permute-start | bytes 3096584 | tf_op jit(solution)/shard_map/ppermute | solution.py:249
  384.0 9.9 %slice-start.5 = ((s8[8257536]{0:T(1024)(128)(4,1)}), s8[4194304]{0:T(1024)(128)(4,1)S(1)}, s32[]{:S(2)}) async-start(s8[8257536]{0:T(1024)(128)(4,1)} %bitcast.224), calls=%async_computation.5 | async-start | bytes 8388608
  388.5 5.3 slice-start.6
  388.5 42.7 %collective-permute-start.26 = (bf16[4,144,896]{2,1,0:T(8,128)(2,1)}, bf16[4,144,896]{2,1,0:T(8,128)(2,1)}, u32[]{:S(2)}, u32[]{:S(2)}) collective-permute-start(bf16[4,144,896]{2,1,0:T(8,128)(2,1)} %fusion.11), channel_id=1, source_target_pairs={{0,8},{1,9},{2,10},{3,11},{4,12},{5,13},{6,14},{7,15},{8,0},{9,1},... | collective-permute-start | bytes 3096584 | tf_op jit(solution)/shard_map/ppermute | solution.py:249
  392.8 60.5 %collective-permute-start.11 = (bf16[4,56,2304]{2,1,0:T(8,128)(2,1)}, bf16[4,56,2304]{2,1,0:T(8,128)(2,1)}, u32[]{:S(2)}, u32[]{:S(2)}) collective-permute-start(bf16[4,56,2304]{2,1,0:T(8,128)(2,1)} %fusion.8), channel_id=1, source_target_pairs={{0,8},{1,9},{2,10},{3,11},{4,12},{5,13},{6,14},{7,15},{8,0},{9,1},... | collective-permute-start | bytes 3096584 | tf_op jit(solution)/shard_map/ppermute | solution.py:249
  393.8 8.9 %slice-start.3 = ((s8[8257536]{0:T(1024)(128)(4,1)}), s8[4194304]{0:T(1024)(128)(4,1)S(1)}, s32[]{:S(2)}) async-start(s8[8257536]{0:T(1024)(128)(4,1)} %bitcast.218), calls=%async_computation.3 | async-start | bytes 8388608
  397.2 5.6 slice-start.4
  397.2 78.2 %collective-permute-start.16 = (bf16[4,56,2304]{2,1,0:T(8,128)(2,1)}, bf16[4,56,2304]{2,1,0:T(8,128)(2,1)}, u32[]{:S(2)}, u32[]{:S(2)}) collective-permute-start(bf16[4,56,2304]{2,1,0:T(8,128)(2,1)} %fusion.9), channel_id=1, source_target_pairs={{0,8},{1,9},{2,10},{3,11},{4,12},{5,13},{6,14},{7,15},{8,0},{9,1},... | collective-permute-start | bytes 3096584 | tf_op jit(solution)/shard_map/ppermute | solution.py:249
  401.7 95.7 %collective-permute-start.1 = (bf16[4,56,2304]{2,1,0:T(8,128)(2,1)S(1)}, bf16[4,56,2304]{2,1,0:T(8,128)(2,1)S(1)}, u32[]{:S(2)}, u32[]{:S(2)}) collective-permute-start(bf16[4,56,2304]{2,1,0:T(8,128)(2,1)S(1)} %fusion.6), channel_id=1, source_target_pairs={{0,8},{1,9},{2,10},{3,11},{4,12},{5,13},{6,14},{7,15},{8,0},{9,1},... | collective-permute-start | bytes 3096584 | tf_op jit(solution)/shard_map/ppermute | solution.py:249
  409.0 110.0 %collective-permute-start.6 = (bf16[4,56,2304]{2,1,0:T(8,128)(2,1)S(1)}, bf16[4,56,2304]{2,1,0:T(8,128)(2,1)S(1)}, u32[]{:S(2)}, u32[]{:S(2)}) collective-permute-start(bf16[4,56,2304]{2,1,0:T(8,128)(2,1)S(1)} %fusion.7), channel_id=1, source_target_pairs={{0,8},{1,9},{2,10},{3,11},{4,12},{5,13},{6,14},{7,15},{8,0},{9,1},... | collective-permute-start | bytes 3096584 | tf_op jit(solution)/shard_map/ppermute | solution.py:249
  431.2 101.3 %collective-permute-start.22 = (bf16[144,896]{1,0:T(8,128)(2,1)S(1)}, bf16[144,896]{1,0:T(8,128)(2,1)S(1)}, u32[]{:S(2)}, u32[]{:S(2)}) collective-permute-start(bf16[144,896]{1,0:T(8,128)(2,1)S(1)} %get-tuple-element.32), channel_id=1, source_target_pairs={{0,2},{1,3},{2,0},{3,1},{4,6},{5,7},{6,4},{7,5},{8,10},{9,11},{10,... | collective-permute-start | bytes 774152 | tf_op jit(solution)/shard_map/ppermute | solution.py:249
  453.3 105.6 %collective-permute-start.23 = (bf16[144,896]{1,0:T(8,128)(2,1)S(1)}, bf16[144,896]{1,0:T(8,128)(2,1)S(1)}, u32[]{:S(2)}, u32[]{:S(2)}) collective-permute-start(bf16[144,896]{1,0:T(8,128)(2,1)S(1)} %get-tuple-element.34), channel_id=1, source_target_pairs={{0,4},{1,5},{2,6},{3,7},{4,0},{5,1},{6,2},{7,3},{8,12},{9,13},{10,... | collective-permute-start | bytes 774152 | tf_op jit(solution)/shard_map/ppermute | solution.py:249
  475.4 46.3 %collective-permute-start.12 = (bf16[56,2304]{1,0:T(8,128)(2,1)S(1)}, bf16[56,2304]{1,0:T(8,128)(2,1)S(1)}, u32[]{:S(2)}, u32[]{:S(2)}) collective-permute-start(bf16[56,2304]{1,0:T(8,128)(2,1)S(1)} %get-tuple-element.38), channel_id=1, source_target_pairs={{0,2},{1,3},{2,0},{3,1},{4,6},{5,7},{6,4},{7,5},{8,10},{9,11},{10,... | collective-permute-start | bytes 774152 | tf_op jit(solution)/shard_map/ppermute | solution.py:249
  497.4 27.4 %collective-permute-start.13 = (bf16[56,2304]{1,0:T(8,128)(2,1)S(1)}, bf16[56,2304]{1,0:T(8,128)(2,1)S(1)}, u32[]{:S(2)}, u32[]{:S(2)}) collective-permute-start(bf16[56,2304]{1,0:T(8,128)(2,1)S(1)} %get-tuple-element.40), channel_id=1, source_target_pairs={{0,4},{1,5},{2,6},{3,7},{4,0},{5,1},{6,2},{7,3},{8,12},{9,13},{10,... | collective-permute-start | bytes 774152 | tf_op jit(solution)/shard_map/ppermute | solution.py:249
  519.0 10.9 %collective-permute-start.14 = (bf16[56,2304]{1,0:T(8,128)(2,1)S(1)}, bf16[56,2304]{1,0:T(8,128)(2,1)S(1)}, u32[]{:S(2)}, u32[]{:S(2)}) collective-permute-start(bf16[56,2304]{1,0:T(8,128)(2,1)S(1)} %get-tuple-element.39), channel_id=1, source_target_pairs={{0,6},{1,7},{2,4},{3,5},{4,2},{5,3},{6,0},{7,1},{8,14},{9,15},{10,... | collective-permute-start | bytes 774152 | tf_op jit(solution)/shard_map/ppermute | solution.py:249
  521.7 12.4 %collective-permute-start.17 = (bf16[56,2304]{1,0:T(8,128)(2,1)S(1)}, bf16[56,2304]{1,0:T(8,128)(2,1)S(1)}, u32[]{:S(2)}, u32[]{:S(2)}) collective-permute-start(bf16[56,2304]{1,0:T(8,128)(2,1)S(1)} %get-tuple-element.41), channel_id=1, source_target_pairs={{0,2},{1,3},{2,0},{3,1},{4,6},{5,7},{6,4},{7,5},{8,10},{9,11},{10,... | collective-permute-start | bytes 774152 | tf_op jit(solution)/shard_map/ppermute | solution.py:249
  524.8 31.6 %collective-permute-start.18 = (bf16[56,2304]{1,0:T(8,128)(2,1)S(1)}, bf16[56,2304]{1,0:T(8,128)(2,1)S(1)}, u32[]{:S(2)}, u32[]{:S(2)}) collective-permute-start(bf16[56,2304]{1,0:T(8,128)(2,1)S(1)} %get-tuple-element.43), channel_id=1, source_target_pairs={{0,4},{1,5},{2,6},{3,7},{4,0},{5,1},{6,2},{7,3},{8,12},{9,13},{10,... | collective-permute-start | bytes 774152 | tf_op jit(solution)/shard_map/ppermute | solution.py:249
  530.0 26.4 %collective-permute-start.19 = (bf16[56,2304]{1,0:T(8,128)(2,1)S(1)}, bf16[56,2304]{1,0:T(8,128)(2,1)S(1)}, u32[]{:S(2)}, u32[]{:S(2)}) collective-permute-start(bf16[56,2304]{1,0:T(8,128)(2,1)S(1)} %get-tuple-element.42), channel_id=1, source_target_pairs={{0,6},{1,7},{2,4},{3,5},{4,2},{5,3},{6,0},{7,1},{8,14},{9,15},{10,... | collective-permute-start | bytes 774152 | tf_op jit(solution)/shard_map/ppermute | solution.py:249
  532.5 42.7 %collective-permute-start.24 = (bf16[144,896]{1,0:T(8,128)(2,1)S(1)}, bf16[144,896]{1,0:T(8,128)(2,1)S(1)}, u32[]{:S(2)}, u32[]{:S(2)}) collective-permute-start(bf16[144,896]{1,0:T(8,128)(2,1)S(1)} %get-tuple-element.33), channel_id=1, source_target_pairs={{0,6},{1,7},{2,4},{3,5},{4,2},{5,3},{6,0},{7,1},{8,14},{9,15},{10,... | collective-permute-start | bytes 774152 | tf_op jit(solution)/shard_map/ppermute | solution.py:249
  534.1 46.0 %collective-permute-start.27 = (bf16[144,896]{1,0:T(8,128)(2,1)S(1)}, bf16[144,896]{1,0:T(8,128)(2,1)S(1)}, u32[]{:S(2)}, u32[]{:S(2)}) collective-permute-start(bf16[144,896]{1,0:T(8,128)(2,1)S(1)} %get-tuple-element.35), channel_id=1, source_target_pairs={{0,2},{1,3},{2,0},{3,1},{4,6},{5,7},{6,4},{7,5},{8,10},{9,11},{10,... | collective-permute-start | bytes 774152 | tf_op jit(solution)/shard_map/ppermute | solution.py:249
  556.4 38.8 %collective-permute-start.28 = (bf16[144,896]{1,0:T(8,128)(2,1)S(1)}, bf16[144,896]{1,0:T(8,128)(2,1)S(1)}, u32[]{:S(2)}, u32[]{:S(2)}) collective-permute-start(bf16[144,896]{1,0:T(8,128)(2,1)S(1)} %get-tuple-element.37), channel_id=1, source_target_pairs={{0,4},{1,5},{2,6},{3,7},{4,0},{5,1},{6,2},{7,3},{8,12},{9,13},{10,... | collective-permute-start | bytes 774152 | tf_op jit(solution)/shard_map/ppermute | solution.py:249
  556.4 38.8 %collective-permute-start.29 = (bf16[144,896]{1,0:T(8,128)(2,1)S(1)}, bf16[144,896]{1,0:T(8,128)(2,1)S(1)}, u32[]{:S(2)}, u32[]{:S(2)}) collective-permute-start(bf16[144,896]{1,0:T(8,128)(2,1)S(1)} %get-tuple-element.36), channel_id=1, source_target_pairs={{0,6},{1,7},{2,4},{3,5},{4,2},{5,3},{6,0},{7,1},{8,14},{9,15},{10,... | collective-permute-start | bytes 774152 | tf_op jit(solution)/shard_map/ppermute | solution.py:249
  558.9 44.2 %collective-permute-start.2 = (bf16[56,2304]{1,0:T(8,128)(2,1)S(1)}, bf16[56,2304]{1,0:T(8,128)(2,1)S(1)}, u32[]{:S(2)}, u32[]{:S(2)}) collective-permute-start(bf16[56,2304]{1,0:T(8,128)(2,1)S(1)} %get-tuple-element.44), channel_id=1, source_target_pairs={{0,2},{1,3},{2,0},{3,1},{4,6},{5,7},{6,4},{7,5},{8,10},{9,11},{10,... | collective-permute-start | bytes 774152 | tf_op jit(solution)/shard_map/ppermute | solution.py:249
  575.2 42.1 %collective-permute-start.3 = (bf16[56,2304]{1,0:T(8,128)(2,1)S(1)}, bf16[56,2304]{1,0:T(8,128)(2,1)S(1)}, u32[]{:S(2)}, u32[]{:S(2)}) collective-permute-start(bf16[56,2304]{1,0:T(8,128)(2,1)S(1)} %get-tuple-element.46), channel_id=1, source_target_pairs={{0,4},{1,5},{2,6},{3,7},{4,0},{5,1},{6,2},{7,3},{8,12},{9,13},{10,... | collective-permute-start | bytes 774152 | tf_op jit(solution)/shard_map/ppermute | solution.py:249
  580.1 37.2 %collective-permute-start.4 = (bf16[56,2304]{1,0:T(8,128)(2,1)S(1)}, bf16[56,2304]{1,0:T(8,128)(2,1)S(1)}, u32[]{:S(2)}, u32[]{:S(2)}) collective-permute-start(bf16[56,2304]{1,0:T(8,128)(2,1)S(1)} %get-tuple-element.45), channel_id=1, source_target_pairs={{0,6},{1,7},{2,4},{3,5},{4,2},{5,3},{6,0},{7,1},{8,14},{9,15},{10,... | collective-permute-start | bytes 774152 | tf_op jit(solution)/shard_map/ppermute | solution.py:249
  595.1 23.1 %collective-permute-start.7 = (bf16[56,2304]{1,0:T(8,128)(2,1)S(1)}, bf16[56,2304]{1,0:T(8,128)(2,1)S(1)}, u32[]{:S(2)}, u32[]{:S(2)}) collective-permute-start(bf16[56,2304]{1,0:T(8,128)(2,1)S(1)} %get-tuple-element.47), channel_id=1, source_target_pairs={{0,2},{1,3},{2,0},{3,1},{4,6},{5,7},{6,4},{7,5},{8,10},{9,11},{10,... | collective-permute-start | bytes 774152 | tf_op jit(solution)/shard_map/ppermute | solution.py:249
  595.1 33.2 %collective-permute-start.8 = (bf16[56,2304]{1,0:T(8,128)(2,1)S(1)}, bf16[56,2304]{1,0:T(8,128)(2,1)S(1)}, u32[]{:S(2)}, u32[]{:S(2)}) collective-permute-start(bf16[56,2304]{1,0:T(8,128)(2,1)S(1)} %get-tuple-element.49), channel_id=1, source_target_pairs={{0,4},{1,5},{2,6},{3,7},{4,0},{5,1},{6,2},{7,3},{8,12},{9,13},{10,... | collective-permute-start | bytes 774152 | tf_op jit(solution)/shard_map/ppermute | solution.py:249
  603.1 25.3 %collective-permute-start.9 = (bf16[56,2304]{1,0:T(8,128)(2,1)S(1)}, bf16[56,2304]{1,0:T(8,128)(2,1)S(1)}, u32[]{:S(2)}, u32[]{:S(2)}) collective-permute-start(bf16[56,2304]{1,0:T(8,128)(2,1)S(1)} %get-tuple-element.48), channel_id=1, source_target_pairs={{0,6},{1,7},{2,4},{3,5},{4,2},{5,3},{6,0},{7,1},{8,14},{9,15},{10,... | collective-permute-start | bytes 774152 | tf_op jit(solution)/shard_map/ppermute | solution.py:249

commit v3 on v2

v3 whole, which is shorter than its diff:
```python
import jax
import jax.numpy as jnp
from jax import lax
from jax.experimental import pallas as pl
from jax.experimental.pallas import tpu as pltpu
from jax.sharding import PartitionSpec as P


MESH = pl.DeviceIdType.MESH
Z = 4


TILE, CHUNK = 512, 768
FIRST_TILE = 256


def mm(a, b, cb=0):
    return lax.dot_general(a, b, (((1,), (cb,)), ((), ())), preferred_element_type=jnp.float32)


def normed(h):
    wide = h.astype(jnp.float32)
    scale = lax.rsqrt(jnp.mean(wide**2, -1, keepdims=True) + 1e-6)
    return wide, scale


def chunks(ff):
    return [pl.ds(i, CHUNK) for i in range(0, ff, CHUNK)]


def forward_kernel(h_ref, wg, wu, wd, next_ref, a_ref, p_ref, gate_ref, up_ref):
    wide, scale = normed(h_ref[...])
    a = (wide * scale).astype(jnp.bfloat16)
    a_ref[...] = a
    total = None
    for c in chunks(wg.shape[-1]):
        gate, up = mm(a, wg[:, c]), mm(a, wu[:, c])
        gate_ref[:, c], up_ref[:, c] = gate, up
        p = (gate * jax.nn.sigmoid(gate) * up).astype(jnp.bfloat16)
        p_ref[:, c] = p
        part = mm(p, wd[c, :])
        total = part if total is None else total + part
    next_ref[...] = (wide + total.astype(jnp.bfloat16).astype(jnp.float32)).astype(jnp.bfloat16)


def gather_kernel(
    h_ref, gu_ref, d_ref, gu_out, d_out, next_ref, a_ref, p_ref, gate_ref, up_ref,
    wg, wu, wd, s1s, s1r, s2s, s2r, s3s, s3r, s4s, s4r, loc, load,
):
    step, steps = pl.program_id(0), pl.num_programs(0)
    x, me = lax.axis_index("rep"), lax.axis_index("dp")
    y, z, c = me // 8, (me // 2) % 4, me % 2
    rows, rows_d = gu_ref.shape[2], d_ref.shape[1]

    def at(yy, zz, cc):
        return (yy * Z + zz) * 2 + cc

    other = z + 1 - 2 * (z % 2)
    zs = [z, other, (z + 2) % 4, 3 - z]
    y_peer, c_peer, x_peer = (x, at(1 - y, z, c)), (x, at(y, z, 1 - c)), (1 - x, me)
    peers = [(x, at(y, zs[k], c)) for k in (1, 2, 3)] + [y_peer, c_peer, x_peer]

    groups = [(0, True), (0, False), (1, True), (1, False)]
    first, second, third = {}, {}, {}
    fourth = [[] for _ in groups]
    everything, locals_ = [], []

    def remote(src, dst, ss, rs, peer):
        copy = pltpu.make_async_remote_copy(src, dst, ss, rs, device_id=peer, device_id_type=MESH)
        everything.append(copy)
        return copy

    def own(l, gu, m):
        return gu_ref.at[m, l] if gu else d_ref.at[l]

    def place(l, gu, b, m):
        if gu:
            return gu_out.at[m, l, pl.ds(pl.multiple_of(b * rows, 8), rows)]
        return d_out.at[l, pl.ds(pl.multiple_of(b * rows_d, 16), rows_d)]

    def to_core(g, src, dst):
        n = len(fourth[g])
        copy = remote(src, dst, s4s.at[g, n], s4r.at[g, n], c_peer)
        fourth[g].append(copy)
        return copy

    begin, events = [], []
    for g, (l, gu) in enumerate(groups):
        for k in (1, 2, 3):
            peer = (x, at(y, zs[k], c))
            first[g, k] = remote(own(l, gu, x), place(l, gu, me, x), s1s.at[g, k - 1], s1r.at[g, k - 1], peer)
            begin.append(first[g, k])
    for g, (l, gu) in enumerate(groups):
        second[g, 0] = remote(own(l, gu, x), place(l, gu, me, x), s2s.at[g, 0], s2r.at[g, 0], y_peer)
        begin.append(second[g, 0])
        for m in (0, 1) if gu else (0,):
            src, dst = own(l, gu, m), place(l, gu, me, m)
            begin.append(to_core(g, src, dst))
            locals_.append(pltpu.make_async_copy(src, dst, loc.at[2 * g + m]))
            begin.append(locals_[-1])
    for g, (l, gu) in enumerate(groups):
        for k in (1, 2, 3):
            ref = place(l, gu, at(y, zs[k], c), x)
            second[g, k] = remote(ref, ref, s2s.at[g, k], s2r.at[g, k], y_peer)
            starts = [second[g, k]]
            if gu:
                third[g, k - 1] = remote(ref, ref, s3s.at[g // 2, k - 1], s3r.at[g // 2, k - 1], x_peer)
                starts.append(third[g, k - 1])
            events.append((4 * g + k + 1.0, l, first[g, k], starts + [to_core(g, ref, ref)]))
        for k in range(4):
            ref = place(l, gu, at(1 - y, zs[k], c), x)
            starts = []
            if gu:
                third[g, 3 + k] = remote(ref, ref, s3s.at[g // 2, 3 + k], s3r.at[g // 2, 3 + k], x_peer)
                starts.append(third[g, 3 + k])
            events.append((4 * g + k + 2.5, l, second[g, k], starts + [to_core(g, ref, ref)]))
        if gu:
            for j in range(7):
                b = at(y, zs[j + 1], c) if j < 3 else at(1 - y, zs[j - 3], c)
                ref = place(l, gu, b, 1 - x)
                events.append((7 * (g // 2) + j + 3.7, l, third[g, j], [to_core(g, ref, ref)]))
    events.sort(key=lambda e: (e[1], e[0]))

    def run(some):
        for _, _, arrival, starts in some:
            arrival.wait_recv()
            for copy in starts:
                copy.start()

    early = [e for e in events if e[1] == 0]
    late = [e for e in events if e[1] == 1]
    in_vmem = [
        pltpu.make_async_copy(src, dst, load.at[n])
        for n, (src, dst) in enumerate([(gu_out.at[0, 0], wg), (gu_out.at[1, 0], wu), (d_out.at[0], wd)])
    ]

    @pl.when(step == 0)
    def _():
        barrier = pltpu.get_barrier_semaphore()
        for peer in peers:
            pl.semaphore_signal(barrier, inc=1, device_id=peer, device_id_type=MESH)
        pl.semaphore_wait(barrier, len(peers))
        for copy in begin:
            copy.start()
        run(early)
        for copy in fourth[0] + fourth[1]:
            copy.wait_recv()
        for copy in locals_:
            copy.wait()
        for copy in in_vmem:
            copy.start()
        for copy in in_vmem:
            copy.wait()

    done = 0
    for n in range(1, TOKENS // FIRST_TILE):
        some = [e for e in late[done:] if e[0] <= 10.5 + 0.9 * n]
        done += len(some)
        if some:
            @pl.when(step == n)
            def _(some=some):
                run(some)

    forward_kernel(h_ref, wg, wu, wd, next_ref, a_ref, p_ref, gate_ref, up_ref)

    @pl.when(step == steps - 1)
    def _():
        run(late[done:])
        for copy in fourth[2] + fourth[3]:
            copy.wait_recv()
        for copy in everything:
            copy.wait_send()


TOKENS = 2048


def gather(h, w_gate, w_up, w_down):
    gu = jnp.stack([w_gate, w_up])
    any_ = pl.BlockSpec(memory_space=pl.ANY)
    dma = pltpu.SemaphoreType.DMA
    _, layers, rows, ff = gu.shape
    _, rows_d, d = w_down.shape
    n, t, bf16, f32 = 16, h.shape[0], gu.dtype, jnp.float32
    outs = [(d, bf16), (d, bf16), (ff, bf16), (ff, f32), (ff, f32)]

    def tile(width):
        return pl.BlockSpec((FIRST_TILE, width), lambda i: (i, 0))

    return pl.pallas_call(
        gather_kernel,
        grid=(t // FIRST_TILE,),
        out_shape=[
            jax.ShapeDtypeStruct((2, layers, n * rows, ff), bf16),
            jax.ShapeDtypeStruct((layers, n * rows_d, d), bf16),
        ] + [jax.ShapeDtypeStruct((t, width), dtype) for width, dtype in outs],
        in_specs=[tile(d), any_, any_],
        out_specs=[any_, any_] + [tile(width) for width, _ in outs],
        scratch_shapes=[
            pltpu.VMEM((n * rows, ff), bf16), pltpu.VMEM((n * rows, ff), bf16), pltpu.VMEM((n * rows_d, d), bf16),
            dma((4, 3)), dma((4, 3)), dma((4, 4)), dma((4, 4)), dma((2, 7)), dma((2, 7)),
            dma((4, 16)), dma((4, 16)), dma((8,)), dma((3,)),
        ],
        compiler_params=pltpu.CompilerParams(
            collective_id=0, has_side_effects=True, vmem_limit_bytes=60 * 2**20, dimension_semantics=("arbitrary",)
        ),
    )(h, gu, w_down)


def through_gate(gate, up, dp):
    dp = dp.astype(jnp.bfloat16).astype(jnp.float32)
    s = jax.nn.sigmoid(gate)
    silu = gate * s
    dgate = (dp * up * (s * (1 + gate * (1 - s)))).astype(jnp.bfloat16)
    return silu, dgate, (dp * silu).astype(jnp.bfloat16)


def through_norm(wide, scale, dy, da_gate, da_up):
    bf16, f32 = jnp.bfloat16, jnp.float32
    da = (da_gate.astype(bf16).astype(f32) + da_up.astype(bf16).astype(f32)).astype(bf16).astype(f32)
    dh = scale * (da - wide * (scale**2 * jnp.mean(da * wide, -1, keepdims=True)))
    return (dy.astype(f32) + dh.astype(bf16).astype(f32)).astype(bf16)


def last_kernel(h_ref, dy_ref, wg, wu, wd, dh_ref, a_ref, p_ref, dgate_ref, dup_ref):
    wide, scale = normed(h_ref[...])
    a = (wide * scale).astype(jnp.bfloat16)
    a_ref[...] = a
    dy = dy_ref[...]
    da_gate = da_up = None
    for c in chunks(wg.shape[-1]):
        gate, up = mm(a, wg[:, c]), mm(a, wu[:, c])
        silu, dgate, dup = through_gate(gate, up, mm(dy, wd[c, :], 1))
        p_ref[:, c] = (silu * up).astype(jnp.bfloat16)
        dgate_ref[:, c], dup_ref[:, c] = dgate, dup
        g, u = mm(dgate, wg[:, c], 1), mm(dup, wu[:, c], 1)
        da_gate, da_up = (g, u) if da_gate is None else (da_gate + g, da_up + u)
    dh_ref[...] = through_norm(wide, scale, dy, da_gate, da_up)


def gate_kernel(dy_ref, gate_ref, up_ref, wd, dgate_ref, dup_ref):
    dy = dy_ref[...]
    for c in chunks(gate_ref.shape[-1]):
        _, dgate_ref[:, c], dup_ref[:, c] = through_gate(gate_ref[:, c], up_ref[:, c], mm(dy, wd[c, :], 1))


def input_kernel(h_ref, dy_ref, dgate_ref, dup_ref, wg, wu, dh_ref):
    wide, scale = normed(h_ref[...])
    da_gate, da_up = mm(dgate_ref[...], wg[...], 1), mm(dup_ref[...], wu[...], 1)
    dh_ref[...] = through_norm(wide, scale, dy_ref[...], da_gate, da_up)


def call(kernel, tokens, weights, outs, matmuls, t=None, part=0):
    t = t or tokens[0].shape[0]
    d, ff, skip = 896, 2304, part * t // TILE
    specs = [pl.BlockSpec((TILE, v.shape[1]), lambda i: (i + skip, 0)) for v in tokens]
    for w, at in weights:
        specs.append(
            pl.BlockSpec((None,) * len(at) + w.shape[-2:], lambda i, at=at: (*at, 0, 0), pipeline_mode=pl.Buffered(1))
        )
    return pl.pallas_call(
        kernel,
        grid=(t // TILE,),
        in_specs=specs,
        out_specs=[pl.BlockSpec((TILE, n), lambda i: (i, 0)) for n, _ in outs],
        out_shape=[jax.ShapeDtypeStruct((t, n), dtype) for n, dtype in outs],
        compiler_params=pltpu.CompilerParams(vmem_limit_bytes=60 * 2**20, dimension_semantics=("arbitrary",)),
        cost_estimate=pl.CostEstimate(flops=2 * t * d * ff * matmuls, bytes_accessed=30 * 2**20, transcendentals=t * ff),
    )(*tokens, *(w for w, _ in weights))


def dot(a, b, ca, cb):
    return lax.dot_general(a, b, (((ca,), (cb,)), ((), ())), preferred_element_type=jnp.float32)


def pairs(of):
    return [((y * Z + z) * 2 + c, of(y, z, c)) for y in range(2) for z in range(Z) for c in range(2)]


def scatter_sum(term):
    me = lax.axis_index("dp")
    y, z, c = me // 8, (me // 2) % 4, me % 2
    term = lax.optimization_barrier(term).reshape(2, Z, 2, -1, term.shape[-1])

    def pick(t, i, axis):
        return lax.dynamic_index_in_dim(t, i, axis, keepdims=False)

    def swap(t, of):
        t = t.astype(jnp.bfloat16)
        t = lax.ppermute(t, "dp", pairs(of))
        return t.astype(jnp.float32)

    got = swap(pick(term, 1 - c, 2), lambda y, z, c: (y * Z + z) * 2 + 1 - c)
    term = pick(term, c, 2) + got
    got = swap(pick(term, 1 - y, 0), lambda y, z, c: ((1 - y) * Z + z) * 2 + c)
    term = pick(term, y, 0) + got
    total = pick(term, z, 0)
    for k in (1, 2, 3):
        total += swap(pick(term, z ^ k, 0), lambda y, z, c: (y * Z + (z ^ k)) * 2 + c)
    return total.astype(jnp.bfloat16)


def solution(mesh):
    def step(*args):
        return work(*args)

    def work(x, dy, w_gate, w_up, w_down):
        x, dy = x[0], dy[0]
        bf16 = jnp.bfloat16
        gu, down, h, a0, p0, gate, up = gather(x, w_gate, w_up, w_down)
        d, ff = x.shape[1], gu.shape[-1]
        wg, wu, wd = [[(gu, (0, l)) for l in (0, 1)], [(gu, (1, l)) for l in (0, 1)], [(down, (l,)) for l in (0, 1)]]
        dy0, a1, p1, dgate1, dup1 = call(
            last_kernel, (h, dy), (wg[1], wu[1], wd[1]), [(d, bf16), (d, bf16), (ff, bf16), (ff, bf16), (ff, bf16)], 5
        )
        d1 = scatter_sum(dot(p1, dy, 0, 0))
        g1 = scatter_sum(dot(a1, dgate1, 0, 0))
        u1 = scatter_sum(dot(a1, dup1, 0, 0))
        d0 = scatter_sum(dot(p0, dy0, 0, 0))
        dgate0, dup0 = call(gate_kernel, (dy0, gate, up), (wd[0],), [(ff, bf16), (ff, bf16)], 1)
        g0 = scatter_sum(dot(a0, dgate0, 0, 0))
        u0 = scatter_sum(dot(a0, dup0, 0, 0))
        half = x.shape[0] // 2
        dx = jnp.concatenate([
            call(input_kernel, (x, dy0, dgate0, dup0), (wg[0], wu[0]), [(d, bf16)], 1, half, n)[0]
            for n in (0, 1)
        ])
        return dx[None], jnp.stack([g0, g1]), jnp.stack([u0, u1]), jnp.stack([d0, d1])

    rows = P(("rep", "dp"), None, None)
    w = P(None, "dp", None)
    g = P("rep", "dp", None)
    step = jax.shard_map(step, mesh=mesh, in_specs=(rows, rows, w, w, w), out_specs=(rows, g, g, g), check_vma=False)
    return step
```

time: 640 us -> 634 us (level)
  starting transfers between devices: 73.7 us -> 123 us
  waiting for transfers between devices: 148 us -> 107 us
  Pallas kernels: 273 us -> 260 us
    ppermute x30, starting transfers between devices: 73.7 us -> 123 us  [swap(): t = lax.ppermute(t, 'dp', pairs(of))]
    ppermute x30, waiting for transfers between devices: 148 us -> 107 us  [swap(): t = lax.ppermute(t, 'dp', pairs(of))]
    pallas_call x4, Pallas kernels: 158 us -> 125 us  [call(): pl.pallas_call(kernel, grid=(t // TILE,), in_specs=specs, out_specs=[pl.B...]
    pallas_call x1, Pallas kernels: 115 us -> 135 us  [gather(): pl.pallas_call(gather_kernel, grid=(t // FIRST_TILE,), out_shape=[jax.Sha...]
    unnamed x38 -> x46, local copies, waits for them, and re-layouts: 12.5 us -> 14.6 us
  transfers between devices with their start and end apart: 30 -> 30, of which waited for: 12 -> 11; matrix products, arithmetic and copies ran while one was open for 16% -> 16% of each run, Pallas kernels for 9% -> 10%
where the time goes in v3:
time: 634 us; the launch traced here: 626 us
  Pallas kernels  260 us (41%)
  starting transfers between devices  123 us (19%)
  waiting for transfers between devices  107 us (17%)
  matrix products  72.9 us (11%)
  local copies, waits for them, and re-layouts  32.4 us (5%)
  other arithmetic  30.2 us (5%)
    pallas_call x1, Pallas kernels, gather(): pl.pallas_call(gather_kernel, grid=(t // FIRST_TILE,), out_shape=[jax.Sha...  135 us
    pallas_call x4, Pallas kernels, call(): pl.pallas_call(kernel, grid=(t // TILE,), in_specs=specs, out_specs=[pl.B...  125 us
    ppermute x30, starting transfers between devices, swap(): t = lax.ppermute(t, 'dp', pairs(of))  123 us
    ppermute x30, waiting for transfers between devices, swap(): t = lax.ppermute(t, 'dp', pairs(of))  107 us
    dot_general x6, matrix products, dot(): lax.dot_general(a, b, (((ca,), (cb,)), ((), ())), preferred_element_type=...  72.9 us
    convert_element_type x18, local copies, waits for them, and re-layouts, swap(): t = t.astype(jnp.bfloat16)  17.8 us
    add x6, other arithmetic, scatter_sum(): term = pick(term, c, 2) + got  14.9 us
    unnamed x46, local copies, waits for them, and re-layouts  14.6 us
  transfers between devices with their start and end apart: 30, of which 11 were waited for; matrix products, arithmetic and copies ran while one was open for 16% of the time, Pallas kernels for 10%

profile of v3, /device:TPU:4, one launch (start us, length us, event | category | flops | bytes accessed | tf_op | source)
XLA Modules:
  0.0 626.5 jit_solution(9629960652987730560)
XLA Ops:
  0.6 2.3 pad_maximum_fusion.gu_ref
  2.9 135.0 %shard_map.84 = (bf16[2,2,896,2304]{3,2,1,0:T(8,128)(2,1)}, bf16[2,2304,896]{2,1,0:T(8,128)(2,1)}, bf16[2048,896]{1,0:T(8,128)(2,1)}, bf16[2048,896]{1,0:T(8,128...) custom-call(bf16[2048,896]{1,0:T(8,128)(2,1)} %bitcast.207, ...), custom_call_target="tpu_custom_call" | custom-call | tf_op jit(solution)/shard_map/pallas_call | solution.py:190
  137.9 61.5 %shard_map.85 = (bf16[2048,896]{1,0:T(8,128)(2,1)}, bf16[2048,896]{1,0:T(8,128)(2,1)}, bf16[2048,2304]{1,0:T(8,128)(2,1)}, bf16[2048,2304]{1,0:T(8,128)(2,1)}, bf16[2048,2304]{1,0:T(8,128)(2,1)}) custom-call(bf16[2048,896]{1,0:T(8,128)(2,1)} %get-tuple-element.18.h_ref, bf16[2048,896]{1,0:T(8,128)(2,1)} %bitcast.232, ...), custom_call_target="tpu_custom_call" | custom-call | flops 42278584320 | bytes 31457280 | tf_op jit(solution)/shard_map/pallas_call | solution.py:261
  199.5 15.9 %fusion.60 = f32[2304,896]{1,0:T(8,128)} fusion(bf16[2048,2304]{1,0:T(8,128)(2,1)} %get-tuple-element.30, bf16[2048,896]{1,0:T(8,128)(2,1)} %get-tuple-element.21.dy_ref), kind=kOutput, calls=%fused_computation.113 | convolution fusion | flops 8455716864 | bytes 21364736 | tf_op jit(solution)/shard_map/dot_general | solution.py:273
  215.4 3.8 fusion.4
  219.2 12.8 %fusion.54 = f32[2304,896]{1,0:T(8,128)S(1)} fusion(bf16[2048,2304]{1,0:T(8,128)(2,1)} %get-tuple-element.31, bf16[1,2048,896]{2,1,0:T(8,128)(2,1)S(1)} %copy-done.5), kind=kOutput, calls=%fused_computation.107 | convolution fusion | flops 8455716864 | bytes 21364736 | tf_op jit(solution)/shard_map/dot_general | solution.py:273
  232.0 3.3 copy-done.3
  235.3 1.6 fusion.5
  237.3 27.5 %shard_map.86 = (bf16[2048,2304]{1,0:T(8,128)(2,1)}, bf16[2048,2304]{1,0:T(8,128)(2,1)}) custom-call(bf16[2048,896]{1,0:T(8,128)(2,1)} %get-tuple-element.21.dy_ref, f32[2048,2304]{1,0:T(8,128)} %get-tuple-element.22.gate_ref, f32[2048,2304]{1,0:T(8,128)} %get-tuple-element.23.up_ref, bf16[2,2304,896]{2,1,0:T(8,128)(2,1)} %get-tuple-element.20.wd), custom_call_target="tpu_custom_call" | custom-call | flops 8455716864 | bytes 31457280 | tf_op jit(solution)/shard_map/pallas_call | solution.py:261
  264.9 11.3 %fusion.58 = f32[896,2304]{1,0:T(8,128)S(1)} fusion(bf16[2048,896]{1,0:T(8,128)(2,1)S(1)} %copy-done.6, bf16[2048,2304]{1,0:T(8,128)(2,1)} %get-tuple-element.25.dup_ref), kind=kOutput, calls=%fused_computation.111 | convolution fusion | flops 8455716864 | bytes 21364736 | tf_op jit(solution)/shard_map/dot_general | solution.py:273
  276.2 1.5 fusion.2
  277.8 3.6 copy-done.4
  281.4 12.4 %fusion.59 = f32[896,2304]{1,0:T(8,128)S(1)} fusion(bf16[2048,896]{1,0:T(8,128)(2,1)S(1)} %copy-done.7, bf16[2048,2304]{1,0:T(8,128)(2,1)} %get-tuple-element.29), kind=kOutput, calls=%fused_computation.112 | convolution fusion | flops 8455716864 | bytes 21364736 | tf_op jit(solution)/shard_map/dot_general | solution.py:273
  293.8 1.6 fusion.3
  295.4 3.2 copy-done.2
  298.7 9.2 %fusion.56 = f32[896,2304]{1,0:T(8,128)S(1)} fusion(bf16[2048,896]{1,0:T(8,128)(2,1)S(1)} %copy-done.6, bf16[2048,2304]{1,0:T(8,128)(2,1)S(1)} %bitcast.206), kind=kOutput, calls=%fused_computation.109 | convolution fusion | flops 8455716864 | bytes 21364736 | tf_op jit(solution)/shard_map/dot_general | solution.py:273
  307.9 4.1 copy-done.1
  312.7 11.3 %fusion.57 = f32[896,2304]{1,0:T(8,128)} fusion(bf16[2048,896]{1,0:T(8,128)(2,1)S(1)} %copy-done.8, bf16[2048,2304]{1,0:T(8,128)(2,1)S(1)} %bitcast.234), kind=kOutput, calls=%fused_computation.110 | convolution fusion | flops 8455716864 | bytes 21364736 | tf_op jit(solution)/shard_map/dot_general | solution.py:273
  324.0 17.9 %shard_map.87 = bf16[1024,896]{1,0:T(8,128)(2,1)} custom-call(bf16[2048,896]{1,0:T(8,128)(2,1)} %bitcast.208, bf16[2048,896]{1,0:T(8,128)(2,1)} %get-tuple-element.21.dy_ref, bf16[2048,2304]{1,0:T(8,128)(2,1)} %get-tuple-element.24.dgate_ref, bf16[2048,2304]{1,0:T(8,128)(2,1)} %get-tuple-element.25.dup_ref, ...), custom_call_target="tpu_custom_call" | custom-call | flops 4227858432 | bytes 31457280 | tf_op jit(solution)/shard_map/pallas_call | solution.py:261
  342.0 18.3 %shard_map.88 = bf16[1024,896]{1,0:T(8,128)(2,1)} custom-call(bf16[2048,896]{1,0:T(8,128)(2,1)} %bitcast.209, bf16[2048,896]{1,0:T(8,128)(2,1)} %get-tuple-element.21.dy_ref, bf16[2048,2304]{1,0:T(8,128)(2,1)} %get-tuple-element.24.dgate_ref, bf16[2048,2304]{1,0:T(8,128)(2,1)} %get-tuple-element.25.dup_ref, ...), custom_call_target="tpu_custom_call" | custom-call | flops 4227858432 | bytes 31457280 | tf_op jit(solution)/shard_map/pallas_call | solution.py:261
  360.2 3.6 maximum_bitcast_fusion
  363.9 3.8 fusion.1
  367.8 3.3 bitcast_add_fusion.1
  371.1 1.1 fusion.10
  372.3 2.2 bitcast_add_fusion
  374.4 1.1 fusion.11
  375.6 2.0 collective-permute-start.26
  377.6 2.1 bitcast_add_fusion.3
  379.6 1.1 fusion.8
  380.9 2.2 bitcast_add_fusion.2
  383.1 1.1 fusion.9
  384.2 1.8 collective-permute-start.16
  386.1 3.2 bitcast_add_fusion.5
  389.8 2.1 bitcast_add_fusion.4
  392.0 6.3 collective-permute-done.21
  398.2 1.4 bitcast_add_fusion.7
  399.8 20.6 %collective-permute-done.26 = bf16[4,144,896]{2,1,0:T(8,128)(2,1)} collective-permute-done((bf16[4,144,896]{2,1,0:T(8,128)(2,1)}, bf16[4,144,896]{2,1,0:T(8,128)(2,1)}, u32[]{:S(2)}, u32[]{:S(2)}) %collective-permute-start.26) | collective-permute-done | bytes 1032224 | tf_op jit(solution)/shard_map/ppermute | solution.py:290
  420.3 14.5 %collective-permute-start.22 = (bf16[144,896]{1,0:T(8,128)(2,1)S(1)}, bf16[144,896]{1,0:T(8,128)(2,1)S(1)}, u32[]{:S(2)}, u32[]{:S(2)}) collective-permute-start(bf16[144,896]{1,0:T(8,128)(2,1)S(1)} %get-tuple-element.32), channel_id=1, source_target_pairs={{0,2},{1,3},{2,0},{3,1},{4,6},{5,7},{6,4},{7,5},{8,10},{9,11},{10,... | collective-permute-start | bytes 774152 | tf_op jit(solution)/shard_map/ppermute | solution.py:290
  434.8 1.4 bitcast_add_fusion.6
  436.4 6.1 collective-permute-done.11
  442.5 15.4 %collective-permute-start.23 = (bf16[144,896]{1,0:T(8,128)(2,1)S(1)}, bf16[144,896]{1,0:T(8,128)(2,1)S(1)}, u32[]{:S(2)}, u32[]{:S(2)}) collective-permute-start(bf16[144,896]{1,0:T(8,128)(2,1)S(1)} %get-tuple-element.34), channel_id=1, source_target_pairs={{0,4},{1,5},{2,6},{3,7},{4,0},{5,1},{6,2},{7,3},{8,12},{9,13},{10,... | collective-permute-start | bytes 774152 | tf_op jit(solution)/shard_map/ppermute | solution.py:290
  457.8 1.4 bitcast_add_fusion.9
  459.4 5.2 collective-permute-done.16
  464.6 14.5 %collective-permute-start.12 = (bf16[56,2304]{1,0:T(8,128)(2,1)S(1)}, bf16[56,2304]{1,0:T(8,128)(2,1)S(1)}, u32[]{:S(2)}, u32[]{:S(2)}) collective-permute-start(bf16[56,2304]{1,0:T(8,128)(2,1)S(1)} %get-tuple-element.38), channel_id=1, source_target_pairs={{0,2},{1,3},{2,0},{3,1},{4,6},{5,7},{6,4},{7,5},{8,10},{9,11},{10,... | collective-permute-start | bytes 774152 | tf_op jit(solution)/shard_map/ppermute | solution.py:290
  479.0 1.4 bitcast_add_fusion.8
  480.6 6.0 collective-permute-done.1
  486.6 15.4 %collective-permute-start.13 = (bf16[56,2304]{1,0:T(8,128)(2,1)S(1)}, bf16[56,2304]{1,0:T(8,128)(2,1)S(1)}, u32[]{:S(2)}, u32[]{:S(2)}) collective-permute-start(bf16[56,2304]{1,0:T(8,128)(2,1)S(1)} %get-tuple-element.40), channel_id=1, source_target_pairs={{0,4},{1,5},{2,6},{3,7},{4,0},{5,1},{6,2},{7,3},{8,12},{9,13},{10,... | collective-permute-start | bytes 774152 | tf_op jit(solution)/shard_map/ppermute | solution.py:290
  502.2 5.9 collective-permute-done.6
  508.2 1.4 collective-permute-start.14
  509.9 14.6 %collective-permute-start.17 = (bf16[56,2304]{1,0:T(8,128)(2,1)S(1)}, bf16[56,2304]{1,0:T(8,128)(2,1)S(1)}, u32[]{:S(2)}, u32[]{:S(2)}) collective-permute-start(bf16[56,2304]{1,0:T(8,128)(2,1)S(1)} %get-tuple-element.41), channel_id=1, source_target_pairs={{0,2},{1,3},{2,0},{3,1},{4,6},{5,7},{6,4},{7,5},{8,10},{9,11},{10,... | collective-permute-start | bytes 774152 | tf_op jit(solution)/shard_map/ppermute | solution.py:290
  524.6 2.4 collective-permute-start.19
  527.1 1.5 collective-permute-start.24
  528.6 2.6 collective-permute-done.17
  531.2 4.3 collective-permute-start.27
  535.5 17.9 %collective-permute-done.18 = bf16[56,2304]{1,0:T(8,128)(2,1)S(1)} collective-permute-done((bf16[56,2304]{1,0:T(8,128)(2,1)S(1)}, bf16[56,2304]{1,0:T(8,128)(2,1)S(1)}, u32[]{:S(2)}, u32[]{:S(2)}) %collective-permute-start.18) | collective-permute-done | bytes 258080 | tf_op jit(solution)/shard_map/ppermute | solution.py:290
  553.3 2.7 collective-permute-start.29
  556.2 16.0 %collective-permute-start.2 = (bf16[56,2304]{1,0:T(8,128)(2,1)S(1)}, bf16[56,2304]{1,0:T(8,128)(2,1)S(1)}, u32[]{:S(2)}, u32[]{:S(2)}) collective-permute-start(bf16[56,2304]{1,0:T(8,128)(2,1)S(1)} %get-tuple-element.44), channel_id=1, source_target_pairs={{0,2},{1,3},{2,0},{3,1},{4,6},{5,7},{6,4},{7,5},{8,10},{9,11},{10,... | collective-permute-start | bytes 774152 | tf_op jit(solution)/shard_map/ppermute | solution.py:290
  572.2 4.8 collective-permute-start.3
  577.1 1.5 collective-permute-start.4
  578.6 13.5 %collective-permute-done.28 = bf16[144,896]{1,0:T(8,128)(2,1)S(1)} collective-permute-done((bf16[144,896]{1,0:T(8,128)(2,1)S(1)}, bf16[144,896]{1,0:T(8,128)(2,1)S(1)}, u32[]{:S(2)}, u32[]{:S(2)}) %collective-permute-start.28) | collective-permute-done | bytes 258080 | tf_op jit(solution)/shard_map/ppermute | solution.py:290
  592.1 7.0 %collective-permute-start.8 = (bf16[56,2304]{1,0:T(8,128)(2,1)S(1)}, bf16[56,2304]{1,0:T(8,128)(2,1)S(1)}, u32[]{:S(2)}, u32[]{:S(2)}) collective-permute-start(bf16[56,2304]{1,0:T(8,128)(2,1)S(1)} %get-tuple-element.49), channel_id=1, source_target_pairs={{0,4},{1,5},{2,6},{3,7},{4,0},{5,1},{6,2},{7,3},{8,12},{9,13},{10,... | collective-permute-start | bytes 774152 | tf_op jit(solution)/shard_map/ppermute | solution.py:290
  600.0 1.5 collective-permute-start.9
  601.5 12.7 %collective-permute-done.3 = bf16[56,2304]{1,0:T(8,128)(2,1)S(1)} collective-permute-done((bf16[56,2304]{1,0:T(8,128)(2,1)S(1)}, bf16[56,2304]{1,0:T(8,128)(2,1)S(1)}, u32[]{:S(2)}, u32[]{:S(2)}) %collective-permute-start.3) | collective-permute-done | bytes 258080 | tf_op jit(solution)/shard_map/ppermute | solution.py:290
  615.1 10.1 %collective-permute-done.8 = bf16[56,2304]{1,0:T(8,128)(2,1)S(1)} collective-permute-done((bf16[56,2304]{1,0:T(8,128)(2,1)S(1)}, bf16[56,2304]{1,0:T(8,128)(2,1)S(1)}, u32[]{:S(2)}, u32[]{:S(2)}) %collective-permute-start.8) | collective-permute-done | bytes 258080 | tf_op jit(solution)/shard_map/ppermute | solution.py:290
  (100 shorter events, 6.8 us)
Async XLA Ops:
  215.4 3.8 copy-start.5
  219.2 148.5 %collective-permute-start.20 = (bf16[2,4,144,896]{3,2,1,0:T(8,128)(2,1)}, bf16[2,4,144,896]{3,2,1,0:T(8,128)(2,1)}, u32[]{:S(2)}, u32[]{:S(2)}) collective-permute-start(bf16[2,4,144,896]{3,2,1,0:T(8,128)(2,1)} %fusion.4), channel_id=1, source_target_pairs={{0,1},{1,0},{2,3},{3,2},{4,5},{5,4},{6,7},{7,6},{8,9},{9,8},{10,11... | collective-permute-start | bytes 6193160 | tf_op jit(solution)/shard_map/ppermute | solution.py:290
  232.0 3.3 copy-start.3
  236.8 135.4 %collective-permute-start.25 = (bf16[2,4,144,896]{3,2,1,0:T(8,128)(2,1)}, bf16[2,4,144,896]{3,2,1,0:T(8,128)(2,1)}, u32[]{:S(2)}, u32[]{:S(2)}) collective-permute-start(bf16[2,4,144,896]{3,2,1,0:T(8,128)(2,1)} %fusion.5), channel_id=1, source_target_pairs={{0,1},{1,0},{2,3},{3,2},{4,5},{5,4},{6,7},{7,6},{8,9},{9,8},{10,11... | collective-permute-start | bytes 6193160 | tf_op jit(solution)/shard_map/ppermute | solution.py:290
  237.3 27.5 %copy-start.6 = (bf16[2048,896]{1,0:T(8,128)(2,1)S(1)}, bf16[2048,896]{1,0:T(8,128)(2,1)}, u32[]{:S(2)}) copy-start(bf16[2048,896]{1,0:T(8,128)(2,1)} %get-tuple-element.26) | copy-start | bytes 11010052
  276.2 5.2 copy-start.4
  276.2 5.2 copy-start.7
  276.2 22.5 %slice-start = ((s8[9437184]{0:T(1024)(128)(4,1)}), s8[4194304]{0:T(1024)(128)(4,1)S(1)}, s32[]{:S(2)}) async-start(s8[9437184]{0:T(1024)(128)(4,1)} %bitcast.205), calls=%async_computation | async-start | bytes 8388608
  277.7 97.8 %collective-permute-start.10 = (bf16[2,4,56,2304]{3,2,1,0:T(8,128)(2,1)}, bf16[2,4,56,2304]{3,2,1,0:T(8,128)(2,1)}, u32[]{:S(2)}, u32[]{:S(2)}) collective-permute-start(bf16[2,4,56,2304]{3,2,1,0:T(8,128)(2,1)} %fusion.2), channel_id=1, source_target_pairs={{0,1},{1,0},{2,3},{3,2},{4,5},{5,4},{6,7},{7,6},{8,9},{9,8},{10,11... | collective-permute-start | bytes 6193160 | tf_op jit(solution)/shard_map/ppermute | solution.py:290
  281.4 17.3 %slice-start.1 = ((s8[9437184]{0:T(1024)(128)(4,1)}), s8[4194304]{0:T(1024)(128)(4,1)S(1)}, s32[]{:S(2)}) async-start(s8[9437184]{0:T(1024)(128)(4,1)} %bitcast.205), calls=%async_computation.1 | async-start | bytes 8388608
  281.4 17.3 %slice-start.2 = ((s8[9437184]{0:T(1024)(128)(4,1)}), s8[1048576]{0:T(1024)(128)(4,1)S(1)}, s32[]{:S(2)}) async-start(s8[9437184]{0:T(1024)(128)(4,1)} %bitcast.205), calls=%async_computation.2 | async-start | bytes 2097152
  293.8 4.9 copy-start.2
  293.8 18.5 %slice-start.11 = ((s8[9437184]{0:T(1024)(128)(4,1)}), s8[4194304]{0:T(1024)(128)(4,1)S(1)}, s32[]{:S(2)}) async-start(s8[9437184]{0:T(1024)(128)(4,1)} %bitcast.233), calls=%async_computation.11 | async-start | bytes 8388608
  295.4 85.3 %collective-permute-start.15 = (bf16[2,4,56,2304]{3,2,1,0:T(8,128)(2,1)}, bf16[2,4,56,2304]{3,2,1,0:T(8,128)(2,1)}, u32[]{:S(2)}, u32[]{:S(2)}) collective-permute-start(bf16[2,4,56,2304]{3,2,1,0:T(8,128)(2,1)} %fusion.3), channel_id=1, source_target_pairs={{0,1},{1,0},{2,3},{3,2},{4,5},{5,4},{6,7},{7,6},{8,9},{9,8},{10,11... | collective-permute-start | bytes 6193160 | tf_op jit(solution)/shard_map/ppermute | solution.py:290
  298.7 13.6 %slice-start.12 = ((s8[9437184]{0:T(1024)(128)(4,1)}), s8[4194304]{0:T(1024)(128)(4,1)S(1)}, s32[]{:S(2)}) async-start(s8[9437184]{0:T(1024)(128)(4,1)} %bitcast.233), calls=%async_computation.12 | async-start | bytes 8388608
  298.7 13.6 %slice-start.13 = ((s8[9437184]{0:T(1024)(128)(4,1)}), s8[1048576]{0:T(1024)(128)(4,1)S(1)}, s32[]{:S(2)}) async-start(s8[9437184]{0:T(1024)(128)(4,1)} %bitcast.233), calls=%async_computation.13 | async-start | bytes 2097152
  307.9 4.1 copy-start.1
  307.9 4.8 copy-start.8
  312.2 72.0 %collective-permute-start = (bf16[2,4,56,2304]{3,2,1,0:T(8,128)(2,1)S(1)}, bf16[2,4,56,2304]{3,2,1,0:T(8,128)(2,1)}, u32[]{:S(2)}, u32[]{:S(2)}) collective-permute-start(bf16[2,4,56,2304]{3,2,1,0:T(8,128)(2,1)S(1)} %fusion), channel_id=1, source_target_pairs={{0,1},{1,0},{2,3},{3,2},{4,5},{5,4},{6,7},{7,6},{8,9},{9,8},{10,11... | collective-permute-start | bytes 6193160 | tf_op jit(solution)/shard_map/ppermute | solution.py:290
  341.9 18.3 %copy-start = (bf16[1024,896]{1,0:T(8,128)(2,1)S(1)}, bf16[1024,896]{1,0:T(8,128)(2,1)}, u32[]{:S(2)}) copy-start(bf16[1024,896]{1,0:T(8,128)(2,1)} %shard_map.87) | copy-start | bytes 5505028
  363.9 8.4 %slice-start.7 = ((s8[8257536]{0:T(1024)(128)(4,1)}), s8[4194304]{0:T(1024)(128)(4,1)S(1)}, s32[]{:S(2)}) async-start(s8[8257536]{0:T(1024)(128)(4,1)} %bitcast.221), calls=%async_computation.7 | async-start | bytes 8388608
  367.7 4.6 slice-start.8
  367.7 21.7 %collective-permute-start.5 = (bf16[2,4,56,2304]{3,2,1,0:T(8,128)(2,1)}, bf16[2,4,56,2304]{3,2,1,0:T(8,128)(2,1)}, u32[]{:S(2)}, u32[]{:S(2)}) collective-permute-start(bf16[2,4,56,2304]{3,2,1,0:T(8,128)(2,1)} %fusion.1), channel_id=1, source_target_pairs={{0,1},{1,0},{2,3},{3,2},{4,5},{5,4},{6,7},{7,6},{8,9},{9,8},{10,11... | collective-permute-start | bytes 6193160 | tf_op jit(solution)/shard_map/ppermute | solution.py:290
  367.8 9.8 %slice-start.9 = ((s8[8257536]{0:T(1024)(128)(4,1)}), s8[4194304]{0:T(1024)(128)(4,1)S(1)}, s32[]{:S(2)}) async-start(s8[8257536]{0:T(1024)(128)(4,1)} %bitcast.227), calls=%async_computation.9 | async-start | bytes 8388608
  372.2 5.4 slice-start.10
  372.2 26.0 %collective-permute-start.21 = (bf16[4,144,896]{2,1,0:T(8,128)(2,1)}, bf16[4,144,896]{2,1,0:T(8,128)(2,1)}, u32[]{:S(2)}, u32[]{:S(2)}) collective-permute-start(bf16[4,144,896]{2,1,0:T(8,128)(2,1)} %fusion.10), channel_id=1, source_target_pairs={{0,8},{1,9},{2,10},{3,11},{4,12},{5,13},{6,14},{7,15},{8,0},{9,1},... | collective-permute-start | bytes 3096584 | tf_op jit(solution)/shard_map/ppermute | solution.py:290
  372.2 8.6 %slice-start.5 = ((s8[8257536]{0:T(1024)(128)(4,1)}), s8[4194304]{0:T(1024)(128)(4,1)S(1)}, s32[]{:S(2)}) async-start(s8[8257536]{0:T(1024)(128)(4,1)} %bitcast.217), calls=%async_computation.5 | async-start | bytes 8388608
  375.6 5.3 slice-start.6
  375.6 44.8 %collective-permute-start.26 = (bf16[4,144,896]{2,1,0:T(8,128)(2,1)}, bf16[4,144,896]{2,1,0:T(8,128)(2,1)}, u32[]{:S(2)}, u32[]{:S(2)}) collective-permute-start(bf16[4,144,896]{2,1,0:T(8,128)(2,1)} %fusion.11), channel_id=1, source_target_pairs={{0,8},{1,9},{2,10},{3,11},{4,12},{5,13},{6,14},{7,15},{8,0},{9,1},... | collective-permute-start | bytes 3096584 | tf_op jit(solution)/shard_map/ppermute | solution.py:290
  380.7 61.7 %collective-permute-start.11 = (bf16[4,56,2304]{2,1,0:T(8,128)(2,1)}, bf16[4,56,2304]{2,1,0:T(8,128)(2,1)}, u32[]{:S(2)}, u32[]{:S(2)}) collective-permute-start(bf16[4,56,2304]{2,1,0:T(8,128)(2,1)} %fusion.8), channel_id=1, source_target_pairs={{0,8},{1,9},{2,10},{3,11},{4,12},{5,13},{6,14},{7,15},{8,0},{9,1},... | collective-permute-start | bytes 3096584 | tf_op jit(solution)/shard_map/ppermute | solution.py:290
  380.9 8.9 %slice-start.3 = ((s8[8257536]{0:T(1024)(128)(4,1)}), s8[4194304]{0:T(1024)(128)(4,1)S(1)}, s32[]{:S(2)}) async-start(s8[8257536]{0:T(1024)(128)(4,1)} %bitcast.211), calls=%async_computation.3 | async-start | bytes 8388608
  384.2 5.6 slice-start.4
  384.2 80.4 %collective-permute-start.16 = (bf16[4,56,2304]{2,1,0:T(8,128)(2,1)}, bf16[4,56,2304]{2,1,0:T(8,128)(2,1)}, u32[]{:S(2)}, u32[]{:S(2)}) collective-permute-start(bf16[4,56,2304]{2,1,0:T(8,128)(2,1)} %fusion.9), channel_id=1, source_target_pairs={{0,8},{1,9},{2,10},{3,11},{4,12},{5,13},{6,14},{7,15},{8,0},{9,1},... | collective-permute-start | bytes 3096584 | tf_op jit(solution)/shard_map/ppermute | solution.py:290
  389.4 97.2 %collective-permute-start.1 = (bf16[4,56,2304]{2,1,0:T(8,128)(2,1)S(1)}, bf16[4,56,2304]{2,1,0:T(8,128)(2,1)S(1)}, u32[]{:S(2)}, u32[]{:S(2)}) collective-permute-start(bf16[4,56,2304]{2,1,0:T(8,128)(2,1)S(1)} %fusion.6), channel_id=1, source_target_pairs={{0,8},{1,9},{2,10},{3,11},{4,12},{5,13},{6,14},{7,15},{8,0},{9,1},... | collective-permute-start | bytes 3096584 | tf_op jit(solution)/shard_map/ppermute | solution.py:290
  398.2 110.0 %collective-permute-start.6 = (bf16[4,56,2304]{2,1,0:T(8,128)(2,1)S(1)}, bf16[4,56,2304]{2,1,0:T(8,128)(2,1)S(1)}, u32[]{:S(2)}, u32[]{:S(2)}) collective-permute-start(bf16[4,56,2304]{2,1,0:T(8,128)(2,1)S(1)} %fusion.7), channel_id=1, source_target_pairs={{0,8},{1,9},{2,10},{3,11},{4,12},{5,13},{6,14},{7,15},{8,0},{9,1},... | collective-permute-start | bytes 3096584 | tf_op jit(solution)/shard_map/ppermute | solution.py:290
  420.3 106.7 %collective-permute-start.22 = (bf16[144,896]{1,0:T(8,128)(2,1)S(1)}, bf16[144,896]{1,0:T(8,128)(2,1)S(1)}, u32[]{:S(2)}, u32[]{:S(2)}) collective-permute-start(bf16[144,896]{1,0:T(8,128)(2,1)S(1)} %get-tuple-element.32), channel_id=1, source_target_pairs={{0,2},{1,3},{2,0},{3,1},{4,6},{5,7},{6,4},{7,5},{8,10},{9,11},{10,... | collective-permute-start | bytes 774152 | tf_op jit(solution)/shard_map/ppermute | solution.py:290
  442.5 113.7 %collective-permute-start.23 = (bf16[144,896]{1,0:T(8,128)(2,1)S(1)}, bf16[144,896]{1,0:T(8,128)(2,1)S(1)}, u32[]{:S(2)}, u32[]{:S(2)}) collective-permute-start(bf16[144,896]{1,0:T(8,128)(2,1)S(1)} %get-tuple-element.34), channel_id=1, source_target_pairs={{0,4},{1,5},{2,6},{3,7},{4,0},{5,1},{6,2},{7,3},{8,12},{9,13},{10,... | collective-permute-start | bytes 774152 | tf_op jit(solution)/shard_map/ppermute | solution.py:290
  464.6 45.3 %collective-permute-start.12 = (bf16[56,2304]{1,0:T(8,128)(2,1)S(1)}, bf16[56,2304]{1,0:T(8,128)(2,1)S(1)}, u32[]{:S(2)}, u32[]{:S(2)}) collective-permute-start(bf16[56,2304]{1,0:T(8,128)(2,1)S(1)} %get-tuple-element.38), channel_id=1, source_target_pairs={{0,2},{1,3},{2,0},{3,1},{4,6},{5,7},{6,4},{7,5},{8,10},{9,11},{10,... | collective-permute-start | bytes 774152 | tf_op jit(solution)/shard_map/ppermute | solution.py:290
  486.6 37.9 %collective-permute-start.13 = (bf16[56,2304]{1,0:T(8,128)(2,1)S(1)}, bf16[56,2304]{1,0:T(8,128)(2,1)S(1)}, u32[]{:S(2)}, u32[]{:S(2)}) collective-permute-start(bf16[56,2304]{1,0:T(8,128)(2,1)S(1)} %get-tuple-element.40), channel_id=1, source_target_pairs={{0,4},{1,5},{2,6},{3,7},{4,0},{5,1},{6,2},{7,3},{8,12},{9,13},{10,... | collective-permute-start | bytes 774152 | tf_op jit(solution)/shard_map/ppermute | solution.py:290
  508.2 16.4 %collective-permute-start.14 = (bf16[56,2304]{1,0:T(8,128)(2,1)S(1)}, bf16[56,2304]{1,0:T(8,128)(2,1)S(1)}, u32[]{:S(2)}, u32[]{:S(2)}) collective-permute-start(bf16[56,2304]{1,0:T(8,128)(2,1)S(1)} %get-tuple-element.39), channel_id=1, source_target_pairs={{0,6},{1,7},{2,4},{3,5},{4,2},{5,3},{6,0},{7,1},{8,14},{9,15},{10,... | collective-permute-start | bytes 774152 | tf_op jit(solution)/shard_map/ppermute | solution.py:290
  509.9 21.3 %collective-permute-start.17 = (bf16[56,2304]{1,0:T(8,128)(2,1)S(1)}, bf16[56,2304]{1,0:T(8,128)(2,1)S(1)}, u32[]{:S(2)}, u32[]{:S(2)}) collective-permute-start(bf16[56,2304]{1,0:T(8,128)(2,1)S(1)} %get-tuple-element.41), channel_id=1, source_target_pairs={{0,2},{1,3},{2,0},{3,1},{4,6},{5,7},{6,4},{7,5},{8,10},{9,11},{10,... | collective-permute-start | bytes 774152 | tf_op jit(solution)/shard_map/ppermute | solution.py:290
  524.5 28.9 %collective-permute-start.18 = (bf16[56,2304]{1,0:T(8,128)(2,1)S(1)}, bf16[56,2304]{1,0:T(8,128)(2,1)S(1)}, u32[]{:S(2)}, u32[]{:S(2)}) collective-permute-start(bf16[56,2304]{1,0:T(8,128)(2,1)S(1)} %get-tuple-element.43), channel_id=1, source_target_pairs={{0,4},{1,5},{2,6},{3,7},{4,0},{5,1},{6,2},{7,3},{8,12},{9,13},{10,... | collective-permute-start | bytes 774152 | tf_op jit(solution)/shard_map/ppermute | solution.py:290
  524.6 28.8 %collective-permute-start.19 = (bf16[56,2304]{1,0:T(8,128)(2,1)S(1)}, bf16[56,2304]{1,0:T(8,128)(2,1)S(1)}, u32[]{:S(2)}, u32[]{:S(2)}) collective-permute-start(bf16[56,2304]{1,0:T(8,128)(2,1)S(1)} %get-tuple-element.42), channel_id=1, source_target_pairs={{0,6},{1,7},{2,4},{3,5},{4,2},{5,3},{6,0},{7,1},{8,14},{9,15},{10,... | collective-permute-start | bytes 774152 | tf_op jit(solution)/shard_map/ppermute | solution.py:290
  527.1 45.1 %collective-permute-start.24 = (bf16[144,896]{1,0:T(8,128)(2,1)S(1)}, bf16[144,896]{1,0:T(8,128)(2,1)S(1)}, u32[]{:S(2)}, u32[]{:S(2)}) collective-permute-start(bf16[144,896]{1,0:T(8,128)(2,1)S(1)} %get-tuple-element.33), channel_id=1, source_target_pairs={{0,6},{1,7},{2,4},{3,5},{4,2},{5,3},{6,0},{7,1},{8,14},{9,15},{10,... | collective-permute-start | bytes 774152 | tf_op jit(solution)/shard_map/ppermute | solution.py:290
  531.2 45.9 %collective-permute-start.27 = (bf16[144,896]{1,0:T(8,128)(2,1)S(1)}, bf16[144,896]{1,0:T(8,128)(2,1)S(1)}, u32[]{:S(2)}, u32[]{:S(2)}) collective-permute-start(bf16[144,896]{1,0:T(8,128)(2,1)S(1)} %get-tuple-element.35), channel_id=1, source_target_pairs={{0,2},{1,3},{2,0},{3,1},{4,6},{5,7},{6,4},{7,5},{8,10},{9,11},{10,... | collective-permute-start | bytes 774152 | tf_op jit(solution)/shard_map/ppermute | solution.py:290
  553.3 38.7 %collective-permute-start.28 = (bf16[144,896]{1,0:T(8,128)(2,1)S(1)}, bf16[144,896]{1,0:T(8,128)(2,1)S(1)}, u32[]{:S(2)}, u32[]{:S(2)}) collective-permute-start(bf16[144,896]{1,0:T(8,128)(2,1)S(1)} %get-tuple-element.37), channel_id=1, source_target_pairs={{0,4},{1,5},{2,6},{3,7},{4,0},{5,1},{6,2},{7,3},{8,12},{9,13},{10,... | collective-permute-start | bytes 774152 | tf_op jit(solution)/shard_map/ppermute | solution.py:290
  553.3 38.7 %collective-permute-start.29 = (bf16[144,896]{1,0:T(8,128)(2,1)S(1)}, bf16[144,896]{1,0:T(8,128)(2,1)S(1)}, u32[]{:S(2)}, u32[]{:S(2)}) collective-permute-start(bf16[144,896]{1,0:T(8,128)(2,1)S(1)} %get-tuple-element.36), channel_id=1, source_target_pairs={{0,6},{1,7},{2,4},{3,5},{4,2},{5,3},{6,0},{7,1},{8,14},{9,15},{10,... | collective-permute-start | bytes 774152 | tf_op jit(solution)/shard_map/ppermute | solution.py:290
  556.2 43.8 %collective-permute-start.2 = (bf16[56,2304]{1,0:T(8,128)(2,1)S(1)}, bf16[56,2304]{1,0:T(8,128)(2,1)S(1)}, u32[]{:S(2)}, u32[]{:S(2)}) collective-permute-start(bf16[56,2304]{1,0:T(8,128)(2,1)S(1)} %get-tuple-element.44), channel_id=1, source_target_pairs={{0,2},{1,3},{2,0},{3,1},{4,6},{5,7},{6,4},{7,5},{8,10},{9,11},{10,... | collective-permute-start | bytes 774152 | tf_op jit(solution)/shard_map/ppermute | solution.py:290
  572.2 42.0 %collective-permute-start.3 = (bf16[56,2304]{1,0:T(8,128)(2,1)S(1)}, bf16[56,2304]{1,0:T(8,128)(2,1)S(1)}, u32[]{:S(2)}, u32[]{:S(2)}) collective-permute-start(bf16[56,2304]{1,0:T(8,128)(2,1)S(1)} %get-tuple-element.46), channel_id=1, source_target_pairs={{0,4},{1,5},{2,6},{3,7},{4,0},{5,1},{6,2},{7,3},{8,12},{9,13},{10,... | collective-permute-start | bytes 774152 | tf_op jit(solution)/shard_map/ppermute | solution.py:290
  577.1 37.1 %collective-permute-start.4 = (bf16[56,2304]{1,0:T(8,128)(2,1)S(1)}, bf16[56,2304]{1,0:T(8,128)(2,1)S(1)}, u32[]{:S(2)}, u32[]{:S(2)}) collective-permute-start(bf16[56,2304]{1,0:T(8,128)(2,1)S(1)} %get-tuple-element.45), channel_id=1, source_target_pairs={{0,6},{1,7},{2,4},{3,5},{4,2},{5,3},{6,0},{7,1},{8,14},{9,15},{10,... | collective-permute-start | bytes 774152 | tf_op jit(solution)/shard_map/ppermute | solution.py:290
  592.1 23.1 %collective-permute-start.7 = (bf16[56,2304]{1,0:T(8,128)(2,1)S(1)}, bf16[56,2304]{1,0:T(8,128)(2,1)S(1)}, u32[]{:S(2)}, u32[]{:S(2)}) collective-permute-start(bf16[56,2304]{1,0:T(8,128)(2,1)S(1)} %get-tuple-element.47), channel_id=1, source_target_pairs={{0,2},{1,3},{2,0},{3,1},{4,6},{5,7},{6,4},{7,5},{8,10},{9,11},{10,... | collective-permute-start | bytes 774152 | tf_op jit(solution)/shard_map/ppermute | solution.py:290
  592.1 33.2 %collective-permute-start.8 = (bf16[56,2304]{1,0:T(8,128)(2,1)S(1)}, bf16[56,2304]{1,0:T(8,128)(2,1)S(1)}, u32[]{:S(2)}, u32[]{:S(2)}) collective-permute-start(bf16[56,2304]{1,0:T(8,128)(2,1)S(1)} %get-tuple-element.49), channel_id=1, source_target_pairs={{0,4},{1,5},{2,6},{3,7},{4,0},{5,1},{6,2},{7,3},{8,12},{9,13},{10,... | collective-permute-start | bytes 774152 | tf_op jit(solution)/shard_map/ppermute | solution.py:290
  600.0 25.2 %collective-permute-start.9 = (bf16[56,2304]{1,0:T(8,128)(2,1)S(1)}, bf16[56,2304]{1,0:T(8,128)(2,1)S(1)}, u32[]{:S(2)}, u32[]{:S(2)}) collective-permute-start(bf16[56,2304]{1,0:T(8,128)(2,1)S(1)} %get-tuple-element.48), channel_id=1, source_target_pairs={{0,6},{1,7},{2,4},{3,5},{4,2},{5,3},{6,0},{7,1},{8,14},{9,15},{10,... | collective-permute-start | bytes 774152 | tf_op jit(solution)/shard_map/ppermute | solution.py:290

commit v4 on v3

--- a/solution.py
+++ b/solution.py
@@ -28,12 +28,13 @@
     return [pl.ds(i, CHUNK) for i in range(0, ff, CHUNK)]
 
 
-def forward_kernel(h_ref, wg, wu, wd, next_ref, a_ref, p_ref, gate_ref, up_ref):
+def forward(h_ref, wg, wu, wd, next_ref, a_ref, p_ref, gate_ref, up_ref, between):
     wide, scale = normed(h_ref[...])
     a = (wide * scale).astype(jnp.bfloat16)
     a_ref[...] = a
     total = None
-    for c in chunks(wg.shape[-1]):
+    for n, c in enumerate(chunks(wg.shape[-1])):
+        between(n)
         gate, up = mm(a, wg[:, c]), mm(a, wu[:, c])
         gate_ref[:, c], up_ref[:, c] = gate, up
         p = (gate * jax.nn.sigmoid(gate) * up).astype(jnp.bfloat16)
@@ -152,16 +153,20 @@
         for copy in in_vmem:
             copy.wait()
 
-    done = 0
+    slots, done = {}, 0
     for n in range(1, TOKENS // FIRST_TILE):
-        some = [e for e in late[done:] if e[0] <= 10.5 + 0.9 * n]
-        done += len(some)
-        if some:
-            @pl.when(step == n)
-            def _(some=some):
-                run(some)
-
-    forward_kernel(h_ref, wg, wu, wd, next_ref, a_ref, p_ref, gate_ref, up_ref)
+        for part in range(3):
+            slots[part, n] = [e for e in late[done:] if e[0] <= 10.3 + 0.9 * n + 0.3 * part]
+            done += len(slots[part, n])
+
+    def between(part):
+        for (at_part, n), some in slots.items():
+            if at_part == part and some:
+                @pl.when(step == n)
+                def _(some=some):
+                    run(some)
+
+    forward(h_ref, wg, wu, wd, next_ref, a_ref, p_ref, gate_ref, up_ref, between)
 
     @pl.when(step == steps - 1)
     def _():
@@ -222,7 +227,7 @@
     return (dy.astype(f32) + dh.astype(bf16).astype(f32)).astype(bf16)
 
 
-def last_kernel(h_ref, dy_ref, wg, wu, wd, dh_ref, a_ref, p_ref, dgate_ref, dup_ref):
+def last_kernel(h_ref, dy_ref, wg, wu, wd, dh_ref, a_ref, p_ref, by_ref):
     wide, scale = normed(h_ref[...])
     a = (wide * scale).astype(jnp.bfloat16)
     a_ref[...] = a
@@ -232,7 +237,7 @@
         gate, up = mm(a, wg[:, c]), mm(a, wu[:, c])
         silu, dgate, dup = through_gate(gate, up, mm(dy, wd[c, :], 1))
         p_ref[:, c] = (silu * up).astype(jnp.bfloat16)
-        dgate_ref[:, c], dup_ref[:, c] = dgate, dup
+        by_ref[:, c], by_ref[:, pl.ds(wg.shape[-1] + c.start, CHUNK)] = dgate, dup
         g, u = mm(dgate, wg[:, c], 1), mm(dup, wu[:, c], 1)
         da_gate, da_up = (g, u) if da_gate is None else (da_gate + g, da_up + u)
     dh_ref[...] = through_norm(wide, scale, dy, da_gate, da_up)
@@ -250,19 +255,19 @@
     dh_ref[...] = through_norm(wide, scale, dy_ref[...], da_gate, da_up)
 
 
-def call(kernel, tokens, weights, outs, matmuls, t=None, part=0):
+def call(kernel, tokens, weights, outs, matmuls, t=None, part=0, tile=TILE):
     t = t or tokens[0].shape[0]
-    d, ff, skip = 896, 2304, part * t // TILE
-    specs = [pl.BlockSpec((TILE, v.shape[1]), lambda i: (i + skip, 0)) for v in tokens]
+    d, ff, skip = 896, 2304, part * t // tile
+    specs = [pl.BlockSpec((tile, v.shape[1]), lambda i: (i + skip, 0)) for v in tokens]
     for w, at in weights:
         specs.append(
             pl.BlockSpec((None,) * len(at) + w.shape[-2:], lambda i, at=at: (*at, 0, 0), pipeline_mode=pl.Buffered(1))
         )
     return pl.pallas_call(
         kernel,
-        grid=(t // TILE,),
+        grid=(t // tile,),
         in_specs=specs,
-        out_specs=[pl.BlockSpec((TILE, n), lambda i: (i, 0)) for n, _ in outs],
+        out_specs=[pl.BlockSpec((tile, n), lambda i: (i, 0)) for n, _ in outs],
         out_shape=[jax.ShapeDtypeStruct((t, n), dtype) for n, dtype in outs],
         compiler_params=pltpu.CompilerParams(vmem_limit_bytes=60 * 2**20, dimension_semantics=("arbitrary",)),
         cost_estimate=pl.CostEstimate(flops=2 * t * d * ff * matmuls, bytes_accessed=30 * 2**20, transcendentals=t * ff),
@@ -310,14 +315,14 @@
         gu, down, h, a0, p0, gate, up = gather(x, w_gate, w_up, w_down)
         d, ff = x.shape[1], gu.shape[-1]
         wg, wu, wd = [[(gu, (0, l)) for l in (0, 1)], [(gu, (1, l)) for l in (0, 1)], [(down, (l,)) for l in (0, 1)]]
-        dy0, a1, p1, dgate1, dup1 = call(
-            last_kernel, (h, dy), (wg[1], wu[1], wd[1]), [(d, bf16), (d, bf16), (ff, bf16), (ff, bf16), (ff, bf16)], 5
+        dy0, a1, p1, by1 = call(
+            last_kernel, (h, dy), (wg[1], wu[1], wd[1]), [(d, bf16), (d, bf16), (ff, bf16), (2 * ff, bf16)], 5
         )
         d1 = scatter_sum(dot(p1, dy, 0, 0))
-        g1 = scatter_sum(dot(a1, dgate1, 0, 0))
-        u1 = scatter_sum(dot(a1, dup1, 0, 0))
+        gu1 = scatter_sum(dot(a1, by1, 0, 0))
+        g1, u1 = gu1[:, :ff], gu1[:, ff:]
         d0 = scatter_sum(dot(p0, dy0, 0, 0))
-        dgate0, dup0 = call(gate_kernel, (dy0, gate, up), (wd[0],), [(ff, bf16), (ff, bf16)], 1)
+        dgate0, dup0 = call(gate_kernel, (dy0, gate, up), (wd[0],), [(ff, bf16), (ff, bf16)], 1, tile=256)
         g0 = scatter_sum(dot(a0, dgate0, 0, 0))
         u0 = scatter_sum(dot(a0, dup0, 0, 0))
         half = x.shape[0] // 2

time: 634 us -> 602 us (0.950)
  the two profiles are of different devices: /device:TPU:4 before, /device:TPU:8 now
where the time goes in v4:
time: 602 us; the launch traced here: 597 us
  Pallas kernels  278 us (46%)
  waiting for transfers between devices  160 us (27%)
  matrix products  74.4 us (12%)
  other arithmetic  32.4 us (5%)
  local copies, waits for them, and re-layouts  28.8 us (5%)
  starting transfers between devices  21.9 us (4%)
    ppermute x25, waiting for transfers between devices, swap(): t = lax.ppermute(t, 'dp', pairs(of))  160 us
    pallas_call x1, Pallas kernels, gather(): pl.pallas_call(gather_kernel, grid=(t // FIRST_TILE,), out_shape=[jax.Sha...  153 us
    pallas_call x4, Pallas kernels, call(): pl.pallas_call(kernel, grid=(t // tile,), in_specs=specs, out_specs=[pl.B...  125 us
    dot_general x5, matrix products, dot(): lax.dot_general(a, b, (((ca,), (cb,)), ((), ())), preferred_element_type=...  74.4 us
    ppermute x25, starting transfers between devices, swap(): t = lax.ppermute(t, 'dp', pairs(of))  21.9 us
    convert_element_type x15, local copies, waits for them, and re-layouts, swap(): t = t.astype(jnp.bfloat16)  18 us
    add x5, other arithmetic, scatter_sum(): term = pick(term, c, 2) + got  16.7 us
  transfers between devices with their start and end apart: 25, of which 12 were waited for; matrix products, arithmetic and copies ran while one was open for 17% of the time, Pallas kernels for 11%

profile of v4, /device:TPU:8, one launch (start us, length us, event | category | flops | bytes accessed | tf_op | source)
XLA Modules:
  0.0 597.1 jit_solution(2902104016580298716)
XLA Ops:
  0.6 2.3 pad_maximum_fusion.gu_ref
  2.9 152.9 %shard_map.84 = (bf16[2,2,896,2304]{3,2,1,0:T(8,128)(2,1)}, bf16[2,2304,896]{2,1,0:T(8,128)(2,1)}, bf16[2048,896]{1,0:T(8,128)(2,1)}, bf16[2048,896]{1,0:T(8,128...) custom-call(bf16[2048,896]{1,0:T(8,128)(2,1)} %bitcast.174, ...), custom_call_target="tpu_custom_call" | custom-call | tf_op jit(solution)/shard_map/pallas_call | solution.py:195
  155.8 61.6 %shard_map.85 = (bf16[2048,896]{1,0:T(8,128)(2,1)}, bf16[2048,896]{1,0:T(8,128)(2,1)}, bf16[2048,2304]{1,0:T(8,128)(2,1)}, bf16[2048,4608]{1,0:T(8,128)(2,1)}) custom-call(bf16[2048,896]{1,0:T(8,128)(2,1)} %get-tuple-element.17.h_ref, bf16[2048,896]{1,0:T(8,128)(2,1)} %bitcast.193, bf16[2,2,896,2304]{3,2,1,0:T(8,128)(2,1)} %get-tuple-element.18.wg.wu, ...), custom_call_target="tpu_custom_call" | custom-call | flops 42278584320 | bytes 31457280 | tf_op jit(solution)/shard_map/pallas_call | solution.py:266
  217.4 16.1 %fusion.49 = f32[2304,896]{1,0:T(8,128)} fusion(bf16[2048,2304]{1,0:T(8,128)(2,1)} %get-tuple-element.28, bf16[2048,896]{1,0:T(8,128)(2,1)} %get-tuple-element.20.dy_ref), kind=kOutput, calls=%fused_computation.96 | convolution fusion | flops 8455716864 | bytes 21364736 | tf_op jit(solution)/shard_map/dot_general | solution.py:278
  233.5 3.9 fusion.4
  237.3 12.8 %fusion.44 = f32[2304,896]{1,0:T(8,128)S(1)} fusion(bf16[2048,2304]{1,0:T(8,128)(2,1)} %get-tuple-element.29, bf16[1,2048,896]{2,1,0:T(8,128)(2,1)S(1)} %copy-done.8), kind=kOutput, calls=%fused_computation.91 | convolution fusion | flops 8455716864 | bytes 21364736 | tf_op jit(solution)/shard_map/dot_general | solution.py:278
  250.1 3.3 copy-done.3
  253.6 0.6 collective-permute-start.20
  254.2 27.3 %shard_map.86 = (bf16[2048,2304]{1,0:T(8,128)(2,1)}, bf16[2048,2304]{1,0:T(8,128)(2,1)}) custom-call(bf16[2048,896]{1,0:T(8,128)(2,1)} %get-tuple-element.20.dy_ref, f32[2048,2304]{1,0:T(8,128)} %get-tuple-element.21.gate_ref, f32[2048,2304]{1,0:T(8,128)} %get-tuple-element.22.up_ref, bf16[2,2304,896]{2,1,0:T(8,128)(2,1)} %get-tuple-element.19.wd), custom_call_target="tpu_custom_call" | custom-call | flops 8455716864 | bytes 31457280 | tf_op jit(solution)/shard_map/pallas_call | solution.py:266
  281.5 12.6 %fusion.48 = f32[896,2304]{1,0:T(8,128)S(1)} fusion(bf16[2048,896]{1,0:T(8,128)(2,1)} %get-tuple-element.25, bf16[2048,2304]{1,0:T(8,128)(2,1)} %get-tuple-element.24.dup_ref), kind=kOutput, calls=%fused_computation.95 | convolution fusion | flops 8455716864 | bytes 21364736 | tf_op jit(solution)/shard_map/dot_general | solution.py:278
  294.1 4.1 copy-done.4
  298.2 1.5 fusion.3
  299.8 23.7 %fusion.47 = f32[896,4608]{1,0:T(8,128)} fusion(bf16[2048,896]{1,0:T(8,128)(2,1)S(1)} %copy-done.10, bf16[2048,4608]{1,0:T(8,128)(2,1)} %get-tuple-element.27), kind=kOutput, calls=%fused_computation.94 | convolution fusion | flops 16911433728 | bytes 39059456 | tf_op jit(solution)/shard_map/dot_general | solution.py:278
  323.6 5.9 fusion
  329.7 9.2 %fusion.46 = f32[896,2304]{1,0:T(8,128)S(1)} fusion(bf16[2048,896]{1,0:T(8,128)(2,1)S(1)} %copy-done.9, bf16[2048,2304]{1,0:T(8,128)(2,1)S(1)} %bitcast.173), kind=kOutput, calls=%fused_computation.93 | convolution fusion | flops 8455716864 | bytes 21364736 | tf_op jit(solution)/shard_map/dot_general | solution.py:278
  339.0 3.3 copy-done.5
  342.3 1.5 fusion.2
  343.8 0.3 collective-permute-start
  344.0 18.2 %shard_map.87 = bf16[1024,896]{1,0:T(8,128)(2,1)} custom-call(bf16[2048,896]{1,0:T(8,128)(2,1)} %bitcast.175, bf16[2048,896]{1,0:T(8,128)(2,1)} %get-tuple-element.20.dy_ref, bf16[2048,2304]{1,0:T(8,128)(2,1)} %get-tuple-element.23.dgate_ref, bf16[2048,2304]{1,0:T(8,128)(2,1)} %get-tuple-element.24.dup_ref, ...), custom_call_target="tpu_custom_call" | custom-call | flops 4227858432 | bytes 31457280 | tf_op jit(solution)/shard_map/pallas_call | solution.py:266
  362.2 18.3 %shard_map.88 = bf16[1024,896]{1,0:T(8,128)(2,1)} custom-call(bf16[2048,896]{1,0:T(8,128)(2,1)} %bitcast.176, bf16[2048,896]{1,0:T(8,128)(2,1)} %get-tuple-element.20.dy_ref, bf16[2048,2304]{1,0:T(8,128)(2,1)} %get-tuple-element.23.dgate_ref, bf16[2048,2304]{1,0:T(8,128)(2,1)} %get-tuple-element.24.dup_ref, ...), custom_call_target="tpu_custom_call" | custom-call | flops 4227858432 | bytes 31457280 | tf_op jit(solution)/shard_map/pallas_call | solution.py:266
  380.5 3.8 maximum_bitcast_fusion
  384.3 3.3 bitcast_add_fusion.2
  387.6 1.1 fusion.8
  388.8 2.3 bitcast_add_fusion.1
  391.2 1.9 collective-permute-start.21
  393.0 2.1 bitcast_add_fusion.3
  395.2 0.3 collective-permute-start.11
  395.5 3.2 bitcast_add_fusion.5
  398.7 1.1 fusion.6
  399.8 1.8 collective-permute-start.1
  401.6 13.1 %collective-permute-done.16 = bf16[4,144,896]{2,1,0:T(8,128)(2,1)} collective-permute-done((bf16[4,144,896]{2,1,0:T(8,128)(2,1)}, bf16[4,144,896]{2,1,0:T(8,128)(2,1)}, u32[]{:S(2)}, u32[]{:S(2)}) %collective-permute-start.16) | collective-permute-done | bytes 1032224 | tf_op jit(solution)/shard_map/ppermute | solution.py:295
  414.7 1.4 bitcast_add_fusion.7
  416.2 1.0 fusion.34
  417.2 19.5 %collective-permute-done.21 = bf16[4,144,896]{2,1,0:T(8,128)(2,1)S(1)} collective-permute-done((bf16[4,144,896]{2,1,0:T(8,128)(2,1)S(1)}, bf16[4,144,896]{2,1,0:T(8,128)(2,1)S(1)}, u32[]{:S(2)}, u32[]{:S(2)}) %collective-permute-start.21) | collective-permute-done | bytes 1032224 | tf_op jit(solution)/shard_map/ppermute | solution.py:295
  437.0 1.0 fusion.37
  438.0 20.9 %collective-permute-done.11 = bf16[4,56,2304]{2,1,0:T(8,128)(2,1)S(1)} collective-permute-done((bf16[4,56,2304]{2,1,0:T(8,128)(2,1)S(1)}, bf16[4,56,2304]{2,1,0:T(8,128)(2,1)S(1)}, u32[]{:S(2)}, u32[]{:S(2)}) %collective-permute-start.11) | collective-permute-done | bytes 1032224 | tf_op jit(solution)/shard_map/ppermute | solution.py:295
  458.9 1.5 collective-permute-start.19
  460.6 5.9 bitcast_add_fusion
  466.8 13.5 %collective-permute-done.1 = bf16[4,56,2304]{2,1,0:T(8,128)(2,1)} collective-permute-done((bf16[4,56,2304]{2,1,0:T(8,128)(2,1)}, bf16[4,56,2304]{2,1,0:T(8,128)(2,1)}, u32[]{:S(2)}, u32[]{:S(2)}) %collective-permute-start.1) | collective-permute-done | bytes 1032224 | tf_op jit(solution)/shard_map/ppermute | solution.py:295
  480.4 0.3 collective-permute-start.6
  480.6 1.4 bitcast_add_fusion.9
  482.3 1.7 collective-permute-start.24
  484.1 2.7 collective-permute-start.12
  486.8 1.5 fusion.42
  488.4 1.2 collective-permute-start.13
  489.6 11.0 %collective-permute-done.23 = bf16[144,896]{1,0:T(8,128)(2,1)S(1)} collective-permute-done((bf16[144,896]{1,0:T(8,128)(2,1)S(1)}, bf16[144,896]{1,0:T(8,128)(2,1)S(1)}, u32[]{:S(2)}, u32[]{:S(2)}) %collective-permute-start.23) | collective-permute-done | bytes 258080 | tf_op jit(solution)/shard_map/ppermute | solution.py:295
  500.6 1.9 collective-permute-start.14
  502.5 15.9 %collective-permute-done.24 = bf16[144,896]{1,0:T(8,128)(2,1)S(1)} collective-permute-done((bf16[144,896]{1,0:T(8,128)(2,1)S(1)}, bf16[144,896]{1,0:T(8,128)(2,1)S(1)}, u32[]{:S(2)}, u32[]{:S(2)}) %collective-permute-start.24) | collective-permute-done | bytes 258080 | tf_op jit(solution)/shard_map/ppermute | solution.py:295
  518.4 1.3 fusion.43
  519.7 0.8 pad_maximum_fusion.3
  520.6 2.1 collective-permute-start.3
  522.7 1.7 collective-permute-done.13
  524.3 1.8 collective-permute-start.4
  526.1 14.5 %collective-permute-done.14 = bf16[56,2304]{1,0:T(8,128)(2,1)S(1)} collective-permute-done((bf16[56,2304]{1,0:T(8,128)(2,1)S(1)}, bf16[56,2304]{1,0:T(8,128)(2,1)S(1)}, u32[]{:S(2)}, u32[]{:S(2)}) %collective-permute-start.14) | collective-permute-done | bytes 258080 | tf_op jit(solution)/shard_map/ppermute | solution.py:295
  540.7 0.5 bitcast_add_fusion.4
  541.5 2.1 collective-permute-start.8
  543.6 1.4 collective-permute-start.9
  545.0 9.2 %collective-permute-done.4 = bf16[56,2304]{1,0:T(8,128)(2,1)S(1)} collective-permute-done((bf16[56,2304]{1,0:T(8,128)(2,1)S(1)}, bf16[56,2304]{1,0:T(8,128)(2,1)S(1)}, u32[]{:S(2)}, u32[]{:S(2)}) %collective-permute-start.4) | collective-permute-done | bytes 258080 | tf_op jit(solution)/shard_map/ppermute | solution.py:295
  554.3 2.8 collective-permute-done.7
  557.1 25.9 %collective-permute-done.8 = bf16[56,4608]{1,0:T(8,128)(2,1)S(1)} collective-permute-done((bf16[56,4608]{1,0:T(8,128)(2,1)S(1)}, bf16[56,4608]{1,0:T(8,128)(2,1)S(1)}, u32[]{:S(2)}, u32[]{:S(2)}) %collective-permute-start.8) | collective-permute-done | bytes 516128 | tf_op jit(solution)/shard_map/ppermute | solution.py:295
  583.0 11.6 %collective-permute-done.9 = bf16[56,4608]{1,0:T(8,128)(2,1)S(1)} collective-permute-done((bf16[56,4608]{1,0:T(8,128)(2,1)S(1)}, bf16[56,4608]{1,0:T(8,128)(2,1)S(1)}, u32[]{:S(2)}, u32[]{:S(2)}) %collective-permute-start.9) | collective-permute-done | bytes 516128 | tf_op jit(solution)/shard_map/ppermute | solution.py:295
  594.6 0.2 fusion.12
  594.9 0.8 pad_maximum_fusion.2
  595.7 0.8 pad_maximum_fusion.1
  (71 shorter events, 2.5 us)
Async XLA Ops:
  233.5 3.9 copy-start.8
  237.3 147.0 %collective-permute-start.15 = (bf16[2,4,144,896]{3,2,1,0:T(8,128)(2,1)}, bf16[2,4,144,896]{3,2,1,0:T(8,128)(2,1)}, u32[]{:S(2)}, u32[]{:S(2)}) collective-permute-start(bf16[2,4,144,896]{3,2,1,0:T(8,128)(2,1)} %fusion.4), channel_id=1, source_target_pairs={{0,1},{1,0},{2,3},{3,2},{4,5},{5,4},{6,7},{7,6},{8,9},{9,8},{10,11... | collective-permute-start | bytes 6193160 | tf_op jit(solution)/shard_map/ppermute | solution.py:295
  250.1 3.3 copy-start.3
  253.6 135.1 %collective-permute-start.20 = (bf16[2,4,144,896]{3,2,1,0:T(8,128)(2,1)S(1)}, bf16[2,4,144,896]{3,2,1,0:T(8,128)(2,1)}, u32[]{:S(2)}, u32[]{:S(2)}) collective-permute-start(bf16[2,4,144,896]{3,2,1,0:T(8,128)(2,1)S(1)} %fusion.5), channel_id=1, source_target_pairs={{0,1},{1,0},{2,3},{3,2},{4,5},{5,4},{6,7},{7,6},{8,9},{9,8},{10,11... | collective-permute-start | bytes 6193160 | tf_op jit(solution)/shard_map/ppermute | solution.py:295
  294.1 4.1 copy-start.4
  294.1 5.7 copy-start.10
  298.2 31.5 %slice-start = ((s8[9437184]{0:T(1024)(128)(4,1)}), s8[4194304]{0:T(1024)(128)(4,1)S(1)}, s32[]{:S(2)}) async-start(s8[9437184]{0:T(1024)(128)(4,1)} %bitcast.172), calls=%async_computation | async-start | bytes 8388608
  299.7 93.3 %collective-permute-start.10 = (bf16[2,4,56,2304]{3,2,1,0:T(8,128)(2,1)}, bf16[2,4,56,2304]{3,2,1,0:T(8,128)(2,1)}, u32[]{:S(2)}, u32[]{:S(2)}) collective-permute-start(bf16[2,4,56,2304]{3,2,1,0:T(8,128)(2,1)} %fusion.3), channel_id=1, source_target_pairs={{0,1},{1,0},{2,3},{3,2},{4,5},{5,4},{6,7},{7,6},{8,9},{9,8},{10,11... | collective-permute-start | bytes 6193160 | tf_op jit(solution)/shard_map/ppermute | solution.py:295
  299.8 29.9 %slice-start.1 = ((s8[9437184]{0:T(1024)(128)(4,1)}), s8[4194304]{0:T(1024)(128)(4,1)S(1)}, s32[]{:S(2)}) async-start(s8[9437184]{0:T(1024)(128)(4,1)} %bitcast.172), calls=%async_computation.1 | async-start | bytes 8388608
  299.8 29.9 %slice-start.2 = ((s8[9437184]{0:T(1024)(128)(4,1)}), s8[1048576]{0:T(1024)(128)(4,1)S(1)}, s32[]{:S(2)}) async-start(s8[9437184]{0:T(1024)(128)(4,1)} %bitcast.172), calls=%async_computation.2 | async-start | bytes 2097152
  323.5 6.2 %copy-start.9 = (bf16[2048,896]{1,0:T(8,128)(2,1)S(1)}, bf16[2048,896]{1,0:T(8,128)(2,1)}, u32[]{:S(2)}) copy-start(bf16[2048,896]{1,0:T(8,128)(2,1)} %get-tuple-element.25) | copy-start | bytes 11010052
  329.5 131.1 %collective-permute-start.5 = (bf16[2,4,56,4608]{3,2,1,0:T(8,128)(2,1)}, bf16[2,4,56,4608]{3,2,1,0:T(8,128)(2,1)}, u32[]{:S(2)}, u32[]{:S(2)}) collective-permute-start(bf16[2,4,56,4608]{3,2,1,0:T(8,128)(2,1)} %fusion), channel_id=1, source_target_pairs={{0,1},{1,0},{2,3},{3,2},{4,5},{5,4},{6,7},{7,6},{8,9},{9,8},{10,11... | collective-permute-start | bytes 12386312 | tf_op jit(solution)/shard_map/ppermute | solution.py:295
  339.0 3.3 copy-start.5
  343.8 51.7 %collective-permute-start = (bf16[2,4,56,2304]{3,2,1,0:T(8,128)(2,1)}, bf16[2,4,56,2304]{3,2,1,0:T(8,128)(2,1)}, u32[]{:S(2)}, u32[]{:S(2)}) collective-permute-start(bf16[2,4,56,2304]{3,2,1,0:T(8,128)(2,1)} %fusion.2), channel_id=1, source_target_pairs={{0,1},{1,0},{2,3},{3,2},{4,5},{5,4},{6,7},{7,6},{8,9},{9,8},{10,11... | collective-permute-start | bytes 6193160 | tf_op jit(solution)/shard_map/ppermute | solution.py:295
  362.2 18.3 %copy-start = (bf16[1024,896]{1,0:T(8,128)(2,1)S(1)}, bf16[1024,896]{1,0:T(8,128)(2,1)}, u32[]{:S(2)}) copy-start(bf16[1024,896]{1,0:T(8,128)(2,1)} %shard_map.87) | copy-start | bytes 5505028
  380.5 8.2 %slice-start.3 = ((s8[8257536]{0:T(1024)(128)(4,1)}), s8[4194304]{0:T(1024)(128)(4,1)S(1)}, s32[]{:S(2)}) async-start(s8[8257536]{0:T(1024)(128)(4,1)} %bitcast.180), calls=%async_computation.3 | async-start | bytes 8388608
  384.3 4.4 slice-start.4
  384.3 8.7 %slice-start.5 = ((s8[8257536]{0:T(1024)(128)(4,1)}), s8[4194304]{0:T(1024)(128)(4,1)S(1)}, s32[]{:S(2)}) async-start(s8[8257536]{0:T(1024)(128)(4,1)} %bitcast.186), calls=%async_computation.5 | async-start | bytes 8388608
  388.7 4.3 slice-start.6
  388.7 26.0 %collective-permute-start.16 = (bf16[4,144,896]{2,1,0:T(8,128)(2,1)}, bf16[4,144,896]{2,1,0:T(8,128)(2,1)}, u32[]{:S(2)}, u32[]{:S(2)}) collective-permute-start(bf16[4,144,896]{2,1,0:T(8,128)(2,1)} %fusion.8), channel_id=1, source_target_pairs={{0,8},{1,9},{2,10},{3,11},{4,12},{5,13},{6,14},{7,15},{8,0},{9,1},... | collective-permute-start | bytes 3096584 | tf_op jit(solution)/shard_map/ppermute | solution.py:295
  391.2 45.6 %collective-permute-start.21 = (bf16[4,144,896]{2,1,0:T(8,128)(2,1)S(1)}, bf16[4,144,896]{2,1,0:T(8,128)(2,1)S(1)}, u32[]{:S(2)}, u32[]{:S(2)}) collective-permute-start(bf16[4,144,896]{2,1,0:T(8,128)(2,1)S(1)} %fusion.9), channel_id=1, source_target_pairs={{0,8},{1,9},{2,10},{3,11},{4,12},{5,13},{6,14},{7,15},{8,0},{9,1},... | collective-permute-start | bytes 3096584 | tf_op jit(solution)/shard_map/ppermute | solution.py:295
  395.2 63.6 %collective-permute-start.11 = (bf16[4,56,2304]{2,1,0:T(8,128)(2,1)S(1)}, bf16[4,56,2304]{2,1,0:T(8,128)(2,1)S(1)}, u32[]{:S(2)}, u32[]{:S(2)}) collective-permute-start(bf16[4,56,2304]{2,1,0:T(8,128)(2,1)S(1)} %fusion.7), channel_id=1, source_target_pairs={{0,8},{1,9},{2,10},{3,11},{4,12},{5,13},{6,14},{7,15},{8,0},{9,1},... | collective-permute-start | bytes 3096584 | tf_op jit(solution)/shard_map/ppermute | solution.py:295
  399.8 80.6 %collective-permute-start.1 = (bf16[4,56,2304]{2,1,0:T(8,128)(2,1)}, bf16[4,56,2304]{2,1,0:T(8,128)(2,1)}, u32[]{:S(2)}, u32[]{:S(2)}) collective-permute-start(bf16[4,56,2304]{2,1,0:T(8,128)(2,1)} %fusion.6), channel_id=1, source_target_pairs={{0,8},{1,9},{2,10},{3,11},{4,12},{5,13},{6,14},{7,15},{8,0},{9,1},... | collective-permute-start | bytes 3096584 | tf_op jit(solution)/shard_map/ppermute | solution.py:295
  416.2 20.6 %copy-start.2 = (f32[4,144,896]{2,1,0:T(8,128)}, f32[4,144,896]{2,1,0:T(8,128)S(1)}, u32[]{:S(2)}) copy-start(f32[4,144,896]{2,1,0:T(8,128)S(1)} %bitcast_add_fusion.7) | copy-start | bytes 6193156
  417.2 64.9 %collective-permute-start.17 = (bf16[144,896]{1,0:T(8,128)(2,1)}, bf16[144,896]{1,0:T(8,128)(2,1)}, u32[]{:S(2)}, u32[]{:S(2)}) collective-permute-start(bf16[144,896]{1,0:T(8,128)(2,1)} %get-tuple-element.33), channel_id=1, source_target_pairs={{0,2},{1,3},{2,0},{3,1},{4,6},{5,7},{6,4},{7,5},{8,10},{9,11},{10,... | collective-permute-start | bytes 774152 | tf_op jit(solution)/shard_map/ppermute | solution.py:295
  436.8 45.5 %collective-permute-start.18 = (bf16[144,896]{1,0:T(8,128)(2,1)}, bf16[144,896]{1,0:T(8,128)(2,1)}, u32[]{:S(2)}, u32[]{:S(2)}) collective-permute-start(bf16[144,896]{1,0:T(8,128)(2,1)} %get-tuple-element.35), channel_id=1, source_target_pairs={{0,4},{1,5},{2,6},{3,7},{4,0},{5,1},{6,2},{7,3},{8,12},{9,13},{10,... | collective-permute-start | bytes 774152 | tf_op jit(solution)/shard_map/ppermute | solution.py:295
  437.0 23.6 %copy-start.1 = (f32[4,144,896]{2,1,0:T(8,128)}, f32[4,144,896]{2,1,0:T(8,128)S(1)}, u32[]{:S(2)}) copy-start(f32[4,144,896]{2,1,0:T(8,128)S(1)} %bitcast_add_fusion.6) | copy-start | bytes 6193156
  458.9 25.3 %collective-permute-start.19 = (bf16[144,896]{1,0:T(8,128)(2,1)}, bf16[144,896]{1,0:T(8,128)(2,1)}, u32[]{:S(2)}, u32[]{:S(2)}) collective-permute-start(bf16[144,896]{1,0:T(8,128)(2,1)} %get-tuple-element.34), channel_id=1, source_target_pairs={{0,6},{1,7},{2,4},{3,5},{4,2},{5,3},{6,0},{7,1},{8,14},{9,15},{10,... | collective-permute-start | bytes 774152 | tf_op jit(solution)/shard_map/ppermute | solution.py:295
  460.6 27.8 %collective-permute-start.22 = (bf16[144,896]{1,0:T(8,128)(2,1)}, bf16[144,896]{1,0:T(8,128)(2,1)}, u32[]{:S(2)}, u32[]{:S(2)}) collective-permute-start(bf16[144,896]{1,0:T(8,128)(2,1)} %get-tuple-element.36), channel_id=1, source_target_pairs={{0,2},{1,3},{2,0},{3,1},{4,6},{5,7},{6,4},{7,5},{8,10},{9,11},{10,... | collective-permute-start | bytes 774152 | tf_op jit(solution)/shard_map/ppermute | solution.py:295
  466.8 15.4 %copy-start.7 = (bf16[144,896]{1,0:T(8,128)(2,1)S(1)}, bf16[144,896]{1,0:T(8,128)(2,1)}, u32[]{:S(2)}) copy-start(bf16[144,896]{1,0:T(8,128)(2,1)} %get-tuple-element.38) | copy-start | bytes 774148
  466.8 15.5 %copy-start.6 = (bf16[144,896]{1,0:T(8,128)(2,1)S(1)}, bf16[144,896]{1,0:T(8,128)(2,1)}, u32[]{:S(2)}) copy-start(bf16[144,896]{1,0:T(8,128)(2,1)} %get-tuple-element.37) | copy-start | bytes 774148
  480.4 60.4 %collective-permute-start.6 = (bf16[4,56,4608]{2,1,0:T(8,128)(2,1)S(1)}, bf16[4,56,4608]{2,1,0:T(8,128)(2,1)S(1)}, u32[]{:S(2)}, u32[]{:S(2)}) collective-permute-start(bf16[4,56,4608]{2,1,0:T(8,128)(2,1)S(1)} %fusion.1), channel_id=1, source_target_pairs={{0,8},{1,9},{2,10},{3,11},{4,12},{5,13},{6,14},{7,15},{8,0},{9,1},... | collective-permute-start | bytes 6193160 | tf_op jit(solution)/shard_map/ppermute | solution.py:295
  482.2 18.4 %collective-permute-start.23 = (bf16[144,896]{1,0:T(8,128)(2,1)S(1)}, bf16[144,896]{1,0:T(8,128)(2,1)S(1)}, u32[]{:S(2)}, u32[]{:S(2)}) collective-permute-start(bf16[144,896]{1,0:T(8,128)(2,1)S(1)} %copy-done.7), channel_id=1, source_target_pairs={{0,4},{1,5},{2,6},{3,7},{4,0},{5,1},{6,2},{7,3},{8,12},{9,13},{10,... | collective-permute-start | bytes 774152 | tf_op jit(solution)/shard_map/ppermute | solution.py:295
  482.3 36.2 %collective-permute-start.24 = (bf16[144,896]{1,0:T(8,128)(2,1)S(1)}, bf16[144,896]{1,0:T(8,128)(2,1)S(1)}, u32[]{:S(2)}, u32[]{:S(2)}) collective-permute-start(bf16[144,896]{1,0:T(8,128)(2,1)S(1)} %copy-done.6), channel_id=1, source_target_pairs={{0,6},{1,7},{2,4},{3,5},{4,2},{5,3},{6,0},{7,1},{8,14},{9,15},{10,... | collective-permute-start | bytes 774152 | tf_op jit(solution)/shard_map/ppermute | solution.py:295
  484.1 36.4 %collective-permute-start.12 = (bf16[56,2304]{1,0:T(8,128)(2,1)S(1)}, bf16[56,2304]{1,0:T(8,128)(2,1)S(1)}, u32[]{:S(2)}, u32[]{:S(2)}) collective-permute-start(bf16[56,2304]{1,0:T(8,128)(2,1)S(1)} %get-tuple-element.39), channel_id=1, source_target_pairs={{0,2},{1,3},{2,0},{3,1},{4,6},{5,7},{6,4},{7,5},{8,10},{9,11},{10,... | collective-permute-start | bytes 774152 | tf_op jit(solution)/shard_map/ppermute | solution.py:295
  488.4 36.0 %collective-permute-start.13 = (bf16[56,2304]{1,0:T(8,128)(2,1)S(1)}, bf16[56,2304]{1,0:T(8,128)(2,1)S(1)}, u32[]{:S(2)}, u32[]{:S(2)}) collective-permute-start(bf16[56,2304]{1,0:T(8,128)(2,1)S(1)} %get-tuple-element.41), channel_id=1, source_target_pairs={{0,4},{1,5},{2,6},{3,7},{4,0},{5,1},{6,2},{7,3},{8,12},{9,13},{10,... | collective-permute-start | bytes 774152 | tf_op jit(solution)/shard_map/ppermute | solution.py:295
  500.6 40.0 %collective-permute-start.14 = (bf16[56,2304]{1,0:T(8,128)(2,1)S(1)}, bf16[56,2304]{1,0:T(8,128)(2,1)S(1)}, u32[]{:S(2)}, u32[]{:S(2)}) collective-permute-start(bf16[56,2304]{1,0:T(8,128)(2,1)S(1)} %get-tuple-element.40), channel_id=1, source_target_pairs={{0,6},{1,7},{2,4},{3,5},{4,2},{5,3},{6,0},{7,1},{8,14},{9,15},{10,... | collective-permute-start | bytes 774152 | tf_op jit(solution)/shard_map/ppermute | solution.py:295
  518.4 25.1 %collective-permute-start.2 = (bf16[56,2304]{1,0:T(8,128)(2,1)S(1)}, bf16[56,2304]{1,0:T(8,128)(2,1)S(1)}, u32[]{:S(2)}, u32[]{:S(2)}) collective-permute-start(bf16[56,2304]{1,0:T(8,128)(2,1)S(1)} %get-tuple-element.42), channel_id=1, source_target_pairs={{0,2},{1,3},{2,0},{3,1},{4,6},{5,7},{6,4},{7,5},{8,10},{9,11},{10,... | collective-permute-start | bytes 774152 | tf_op jit(solution)/shard_map/ppermute | solution.py:295
  520.6 24.4 %collective-permute-start.3 = (bf16[56,2304]{1,0:T(8,128)(2,1)S(1)}, bf16[56,2304]{1,0:T(8,128)(2,1)S(1)}, u32[]{:S(2)}, u32[]{:S(2)}) collective-permute-start(bf16[56,2304]{1,0:T(8,128)(2,1)S(1)} %get-tuple-element.44), channel_id=1, source_target_pairs={{0,4},{1,5},{2,6},{3,7},{4,0},{5,1},{6,2},{7,3},{8,12},{9,13},{10,... | collective-permute-start | bytes 774152 | tf_op jit(solution)/shard_map/ppermute | solution.py:295
  524.3 29.9 %collective-permute-start.4 = (bf16[56,2304]{1,0:T(8,128)(2,1)S(1)}, bf16[56,2304]{1,0:T(8,128)(2,1)S(1)}, u32[]{:S(2)}, u32[]{:S(2)}) collective-permute-start(bf16[56,2304]{1,0:T(8,128)(2,1)S(1)} %get-tuple-element.43), channel_id=1, source_target_pairs={{0,6},{1,7},{2,4},{3,5},{4,2},{5,3},{6,0},{7,1},{8,14},{9,15},{10,... | collective-permute-start | bytes 774152 | tf_op jit(solution)/shard_map/ppermute | solution.py:295
  541.4 15.7 %collective-permute-start.7 = (bf16[56,4608]{1,0:T(8,128)(2,1)S(1)}, bf16[56,4608]{1,0:T(8,128)(2,1)S(1)}, u32[]{:S(2)}, u32[]{:S(2)}) collective-permute-start(bf16[56,4608]{1,0:T(8,128)(2,1)S(1)} %get-tuple-element.30), channel_id=1, source_target_pairs={{0,2},{1,3},{2,0},{3,1},{4,6},{5,7},{6,4},{7,5},{8,10},{9,11},{10,... | collective-permute-start | bytes 1548296 | tf_op jit(solution)/shard_map/ppermute | solution.py:295
  541.5 41.5 %collective-permute-start.8 = (bf16[56,4608]{1,0:T(8,128)(2,1)S(1)}, bf16[56,4608]{1,0:T(8,128)(2,1)S(1)}, u32[]{:S(2)}, u32[]{:S(2)}) collective-permute-start(bf16[56,4608]{1,0:T(8,128)(2,1)S(1)} %get-tuple-element.32), channel_id=1, source_target_pairs={{0,4},{1,5},{2,6},{3,7},{4,0},{5,1},{6,2},{7,3},{8,12},{9,13},{10,... | collective-permute-start | bytes 1548296 | tf_op jit(solution)/shard_map/ppermute | solution.py:295
  543.6 51.0 %collective-permute-start.9 = (bf16[56,4608]{1,0:T(8,128)(2,1)S(1)}, bf16[56,4608]{1,0:T(8,128)(2,1)S(1)}, u32[]{:S(2)}, u32[]{:S(2)}) collective-permute-start(bf16[56,4608]{1,0:T(8,128)(2,1)S(1)} %get-tuple-element.31), channel_id=1, source_target_pairs={{0,6},{1,7},{2,4},{3,5},{4,2},{5,3},{6,0},{7,1},{8,14},{9,15},{10,... | collective-permute-start | bytes 1548296 | tf_op jit(solution)/shard_map/ppermute | solution.py:295

commit v5 on v4

--- a/solution.py
+++ b/solution.py
@@ -28,13 +28,12 @@
     return [pl.ds(i, CHUNK) for i in range(0, ff, CHUNK)]
 
 
-def forward(h_ref, wg, wu, wd, next_ref, a_ref, p_ref, gate_ref, up_ref, between):
+def forward(h_ref, wg, wu, wd, next_ref, a_ref, p_ref, gate_ref, up_ref):
     wide, scale = normed(h_ref[...])
     a = (wide * scale).astype(jnp.bfloat16)
     a_ref[...] = a
     total = None
-    for n, c in enumerate(chunks(wg.shape[-1])):
-        between(n)
+    for c in chunks(wg.shape[-1]):
         gate, up = mm(a, wg[:, c]), mm(a, wu[:, c])
         gate_ref[:, c], up_ref[:, c] = gate, up
         p = (gate * jax.nn.sigmoid(gate) * up).astype(jnp.bfloat16)
@@ -85,20 +84,20 @@
         fourth[g].append(copy)
         return copy
 
-    begin, events = [], []
+    begin, events = ([], []), []
     for g, (l, gu) in enumerate(groups):
         for k in (1, 2, 3):
             peer = (x, at(y, zs[k], c))
             first[g, k] = remote(own(l, gu, x), place(l, gu, me, x), s1s.at[g, k - 1], s1r.at[g, k - 1], peer)
-            begin.append(first[g, k])
+            begin[l].append(first[g, k])
     for g, (l, gu) in enumerate(groups):
         second[g, 0] = remote(own(l, gu, x), place(l, gu, me, x), s2s.at[g, 0], s2r.at[g, 0], y_peer)
-        begin.append(second[g, 0])
+        begin[l].append(second[g, 0])
         for m in (0, 1) if gu else (0,):
             src, dst = own(l, gu, m), place(l, gu, me, m)
-            begin.append(to_core(g, src, dst))
+            begin[l].append(to_core(g, src, dst))
             locals_.append(pltpu.make_async_copy(src, dst, loc.at[2 * g + m]))
-            begin.append(locals_[-1])
+            begin[l].append(locals_[-1])
     for g, (l, gu) in enumerate(groups):
         for k in (1, 2, 3):
             ref = place(l, gu, at(y, zs[k], c), x)
@@ -107,7 +106,8 @@
             if gu:
                 third[g, k - 1] = remote(ref, ref, s3s.at[g // 2, k - 1], s3r.at[g // 2, k - 1], x_peer)
                 starts.append(third[g, k - 1])
-            events.append((4 * g + k + 1.0, l, first[g, k], starts + [to_core(g, ref, ref)]))
+            starts.append(to_core(g, ref, ref))
+            events.append((4 * g + k + 1.0, l, first[g, k], starts + (begin[1] if (g, k) == (1, 3) else [])))
         for k in range(4):
             ref = place(l, gu, at(1 - y, zs[k], c), x)
             starts = []
@@ -141,7 +141,7 @@
         for peer in peers:
             pl.semaphore_signal(barrier, inc=1, device_id=peer, device_id_type=MESH)
         pl.semaphore_wait(barrier, len(peers))
-        for copy in begin:
+        for copy in begin[0]:
             copy.start()
         run(early)
         for copy in fourth[0] + fourth[1]:
@@ -153,20 +153,16 @@
         for copy in in_vmem:
             copy.wait()
 
-    slots, done = {}, 0
+    done = 0
     for n in range(1, TOKENS // FIRST_TILE):
-        for part in range(3):
-            slots[part, n] = [e for e in late[done:] if e[0] <= 10.3 + 0.9 * n + 0.3 * part]
-            done += len(slots[part, n])
-
-    def between(part):
-        for (at_part, n), some in slots.items():
-            if at_part == part and some:
-                @pl.when(step == n)
-                def _(some=some):
-                    run(some)
-
-    forward(h_ref, wg, wu, wd, next_ref, a_ref, p_ref, gate_ref, up_ref, between)
+        some = [e for e in late[done:] if e[0] <= 10.5 + 0.9 * n]
+        done += len(some)
+        if some:
+            @pl.when(step == n)
+            def _(some=some):
+                run(some)
+
+    forward(h_ref, wg, wu, wd, next_ref, a_ref, p_ref, gate_ref, up_ref)
 
     @pl.when(step == steps - 1)
     def _():
@@ -255,7 +251,7 @@
     dh_ref[...] = through_norm(wide, scale, dy_ref[...], da_gate, da_up)
 
 
-def call(kernel, tokens, weights, outs, matmuls, t=None, part=0, tile=TILE):
+def call(kernel, tokens, weights, outs, matmuls, t=None, part=0, tile=TILE, into=None):
     t = t or tokens[0].shape[0]
     d, ff, skip = 896, 2304, part * t // tile
     specs = [pl.BlockSpec((tile, v.shape[1]), lambda i: (i + skip, 0)) for v in tokens]
@@ -263,15 +259,24 @@
         specs.append(
             pl.BlockSpec((None,) * len(at) + w.shape[-2:], lambda i, at=at: (*at, 0, 0), pipeline_mode=pl.Buffered(1))
         )
+    more, alias = [], {}
+    if into is not None:
+        specs.append(pl.BlockSpec(memory_space=pl.ANY))
+        more, alias, inner = [into], {len(tokens) + len(weights): 0}, kernel
+
+        def kernel(*refs):
+            inner(*refs[: -len(outs) - 1], *refs[-len(outs) :])
+
     return pl.pallas_call(
         kernel,
         grid=(t // tile,),
         in_specs=specs,
-        out_specs=[pl.BlockSpec((tile, n), lambda i: (i, 0)) for n, _ in outs],
-        out_shape=[jax.ShapeDtypeStruct((t, n), dtype) for n, dtype in outs],
+        out_specs=[pl.BlockSpec((tile, n), lambda i: (i + skip, 0)) for n, _ in outs],
+        input_output_aliases=alias,
+        out_shape=[jax.ShapeDtypeStruct((tokens[0].shape[0], n), dtype) for n, dtype in outs],
         compiler_params=pltpu.CompilerParams(vmem_limit_bytes=60 * 2**20, dimension_semantics=("arbitrary",)),
         cost_estimate=pl.CostEstimate(flops=2 * t * d * ff * matmuls, bytes_accessed=30 * 2**20, transcendentals=t * ff),
-    )(*tokens, *(w for w, _ in weights))
+    )(*tokens, *(w for w, _ in weights), *more)
 
 
 def dot(a, b, ca, cb):
@@ -325,11 +330,9 @@
         dgate0, dup0 = call(gate_kernel, (dy0, gate, up), (wd[0],), [(ff, bf16), (ff, bf16)], 1, tile=256)
         g0 = scatter_sum(dot(a0, dgate0, 0, 0))
         u0 = scatter_sum(dot(a0, dup0, 0, 0))
-        half = x.shape[0] // 2
-        dx = jnp.concatenate([
-            call(input_kernel, (x, dy0, dgate0, dup0), (wg[0], wu[0]), [(d, bf16)], 1, half, n)[0]
-            for n in (0, 1)
-        ])
+        half, dx = x.shape[0] // 2, None
+        for n in (0, 1):
+            (dx,) = call(input_kernel, (x, dy0, dgate0, dup0), (wg[0], wu[0]), [(d, bf16)], 1, half, n, into=dx)
         return dx[None], jnp.stack([g0, g1]), jnp.stack([u0, u1]), jnp.stack([d0, d1])
 
     rows = P(("rep", "dp"), None, None)

time: 602 us -> 593 us (0.985)
  the two profiles are of different devices: /device:TPU:8 before, /device:TPU:9 now
where the time goes in v5:
time: 593 us; the launch traced here: 589 us
  Pallas kernels  273 us (46%)
  waiting for transfers between devices  160 us (27%)
  matrix products  74.5 us (13%)
  local copies, waits for them, and re-layouts  29.8 us (5%)
  other arithmetic  29.7 us (5%)
  starting transfers between devices  20.5 us (3%)
    ppermute x25, waiting for transfers between devices, swap(): t = lax.ppermute(t, 'dp', pairs(of))  160 us
    pallas_call x1, Pallas kernels, gather(): pl.pallas_call(gather_kernel, grid=(t // FIRST_TILE,), out_shape=[jax.Sha...  148 us
    pallas_call x4, Pallas kernels, call(): pl.pallas_call(kernel, grid=(t // tile,), in_specs=specs, out_specs=[pl.B...  125 us
    dot_general x5, matrix products, dot(): lax.dot_general(a, b, (((ca,), (cb,)), ((), ())), preferred_element_type=...  74.5 us
    ppermute x25, starting transfers between devices, swap(): t = lax.ppermute(t, 'dp', pairs(of))  20.5 us
    convert_element_type x15, local copies, waits for them, and re-layouts, swap(): t = t.astype(jnp.bfloat16)  19.1 us
    add x5, other arithmetic, scatter_sum(): term = pick(term, c, 2) + got  16.6 us
  transfers between devices with their start and end apart: 25, of which 11 were waited for; matrix products, arithmetic and copies ran while one was open for 17% of the time, Pallas kernels for 11%

profile of v5, /device:TPU:9, one launch (start us, length us, event | category | flops | bytes accessed | tf_op | source)
XLA Modules:
  0.0 589.0 jit_solution(5182525010506843584)
XLA Ops:
  0.6 2.3 pad_maximum_fusion.gu_ref
  2.9 147.6 %shard_map.84 = (bf16[2,2,896,2304]{3,2,1,0:T(8,128)(2,1)}, bf16[2,2304,896]{2,1,0:T(8,128)(2,1)}, bf16[2048,896]{1,0:T(8,128)(2,1)}, bf16[2048,896]{1,0:T(8,128...) custom-call(bf16[2048,896]{1,0:T(8,128)(2,1)} %bitcast.173, ...), custom_call_target="tpu_custom_call" | custom-call | tf_op jit(solution)/shard_map/pallas_call | solution.py:191
  150.5 61.6 %shard_map.85 = (bf16[2048,896]{1,0:T(8,128)(2,1)}, bf16[2048,896]{1,0:T(8,128)(2,1)}, bf16[2048,2304]{1,0:T(8,128)(2,1)}, bf16[2048,4608]{1,0:T(8,128)(2,1)}) custom-call(bf16[2048,896]{1,0:T(8,128)(2,1)} %get-tuple-element.17.h_ref, bf16[2048,896]{1,0:T(8,128)(2,1)} %bitcast.193, bf16[2,2,896,2304]{3,2,1,0:T(8,128)(2,1)} %get-tuple-element.18.wg.wu.refs_4_.refs_5_, ...), custom_call_target="tpu_custom_call" | custom-call | flops 42278584320 | bytes 31457280 | tf_op jit(solution)/shard_map/pallas_call | solution.py:270
  212.1 16.1 %fusion.49 = f32[2304,896]{1,0:T(8,128)} fusion(bf16[2048,2304]{1,0:T(8,128)(2,1)} %get-tuple-element.28, bf16[2048,896]{1,0:T(8,128)(2,1)} %get-tuple-element.20.dy_ref.refs_1_), kind=kOutput, calls=%fused_computation.95 | convolution fusion | flops 8455716864 | bytes 21364736 | tf_op jit(solution)/shard_map/dot_general | solution.py:283
  228.2 3.9 fusion.4
  232.0 12.8 %fusion.44 = f32[2304,896]{1,0:T(8,128)S(1)} fusion(bf16[2048,2304]{1,0:T(8,128)(2,1)} %get-tuple-element.29, bf16[1,2048,896]{2,1,0:T(8,128)(2,1)S(1)} %copy-done.7), kind=kOutput, calls=%fused_computation.90 | convolution fusion | flops 8455716864 | bytes 21364736 | tf_op jit(solution)/shard_map/dot_general | solution.py:283
  244.8 3.3 copy-done.2
  248.3 0.6 collective-permute-start.20
  248.9 27.4 %shard_map.86 = (bf16[2048,2304]{1,0:T(8,128)(2,1)}, bf16[2048,2304]{1,0:T(8,128)(2,1)}) custom-call(bf16[2048,896]{1,0:T(8,128)(2,1)} %get-tuple-element.20.dy_ref.refs_1_, f32[2048,2304]{1,0:T(8,128)} %get-tuple-element.21.gate_ref, f32[2048,2304]{1,0:T(8,128)} %get-tuple-element.22.up_ref, bf16[2,2304,896]{2,1,0:T(8,128)(2,1)} %get-tuple-element.19.wd), custom_call_target="tpu_custom_call" | custom-call | flops 8455716864 | bytes 31457280 | tf_op jit(solution)/shard_map/pallas_call | solution.py:270
  276.3 12.6 %fusion.48 = f32[896,2304]{1,0:T(8,128)S(1)} fusion(bf16[2048,896]{1,0:T(8,128)(2,1)} %get-tuple-element.25, bf16[2048,2304]{1,0:T(8,128)(2,1)} %get-tuple-element.24.dup_ref.refs_3_), kind=kOutput, calls=%fused_computation.94 | convolution fusion | flops 8455716864 | bytes 21364736 | tf_op jit(solution)/shard_map/dot_general | solution.py:283
  288.9 4.1 copy-done.3
  293.0 1.5 fusion.3
  294.5 23.8 %fusion.47 = f32[896,4608]{1,0:T(8,128)} fusion(bf16[2048,896]{1,0:T(8,128)(2,1)S(1)} %copy-done.9, bf16[2048,4608]{1,0:T(8,128)(2,1)} %get-tuple-element.27), kind=kOutput, calls=%fused_computation.93 | convolution fusion | flops 16911433728 | bytes 39059456 | tf_op jit(solution)/shard_map/dot_general | solution.py:283
  318.3 5.9 %fusion = bf16[2,4,56,4608]{3,2,1,0:T(8,128)(2,1)} fusion(f32[2,4,2,56,4608]{4,3,2,1,0:T(8,128)} %bitcast.177, s32[]{:T(128)S(6)} %select_n.109), kind=kLoop, calls=%fused_computation.2 | loop fusion | bytes 8257540 | tf_op jit(solution)/shard_map/convert_element_type | solution.py:299
  324.5 9.2 %fusion.46 = f32[896,2304]{1,0:T(8,128)S(1)} fusion(bf16[2048,896]{1,0:T(8,128)(2,1)S(1)} %copy-done.8, bf16[2048,2304]{1,0:T(8,128)(2,1)S(1)} %bitcast.172), kind=kOutput, calls=%fused_computation.92 | convolution fusion | flops 8455716864 | bytes 21364736 | tf_op jit(solution)/shard_map/dot_general | solution.py:283
  333.8 3.3 copy-done.4
  337.1 1.6 fusion.2
  338.9 18.2 %shard_map.87.refs_6_ = bf16[2048,896]{1,0:T(8,128)(2,1)} custom-call(bf16[2048,896]{1,0:T(8,128)(2,1)} %bitcast.174, bf16[2048,896]{1,0:T(8,128)(2,1)} %get-tuple-element.20.dy_ref.refs_1_, bf16[2048,2304]{1,0:T(8,128)(2,1)} %get-tuple-element.23.dgate_ref.refs_2_, bf16[2048,2304]{1,0:T(8,128)(2,1)} %get-tuple-element.24.dup_ref.refs_3_, ...), custom_call_target="tpu_custom_call" | custom-call | flops 4227858432 | bytes 31457280 | tf_op jit(solution)/shard_map/pallas_call | solution.py:270
  357.0 18.2 %shard_map.88 = bf16[2048,896]{1,0:T(8,128)(2,1)} custom-call(bf16[2048,896]{1,0:T(8,128)(2,1)} %bitcast.175, bf16[2048,896]{1,0:T(8,128)(2,1)} %get-tuple-element.20.dy_ref.refs_1_, bf16[2048,2304]{1,0:T(8,128)(2,1)} %get-tuple-element.23.dgate_ref.refs_2_, bf16[2048,2304]{1,0:T(8,128)(2,1)} %get-tuple-element.24.dup_ref.refs_3_, ...), custom_call_target="tpu_custom_call", output_to_operand_aliasing={{}: (6, {})} | custom-call | flops 4227858432 | bytes 31457280 | tf_op jit(solution)/shard_map/pallas_call | solution.py:270
  375.3 3.3 bitcast_add_fusion.2
  378.6 1.1 fusion.8
  379.9 3.3 bitcast_add_fusion.1
  383.2 1.1 fusion.9
  384.3 1.2 collective-permute-start.21
  385.6 2.1 bitcast_add_fusion.3
  387.8 0.4 collective-permute-start.11
  388.2 2.1 bitcast_add_fusion.5
  390.3 1.1 fusion.6
  391.4 1.1 collective-permute-start.1
  392.5 11.6 %collective-permute-done.16 = bf16[4,144,896]{2,1,0:T(8,128)(2,1)} collective-permute-done((bf16[4,144,896]{2,1,0:T(8,128)(2,1)}, bf16[4,144,896]{2,1,0:T(8,128)(2,1)}, u32[]{:S(2)}, u32[]{:S(2)}) %collective-permute-start.16) | collective-permute-done | bytes 1032224 | tf_op jit(solution)/shard_map/ppermute | solution.py:300
  404.1 1.4 bitcast_add_fusion.7
  405.6 1.0 fusion.34
  406.6 0.9 collective-permute-start.17
  407.5 18.7 %collective-permute-done.21 = bf16[4,144,896]{2,1,0:T(8,128)(2,1)} collective-permute-done((bf16[4,144,896]{2,1,0:T(8,128)(2,1)}, bf16[4,144,896]{2,1,0:T(8,128)(2,1)}, u32[]{:S(2)}, u32[]{:S(2)}) %collective-permute-start.21) | collective-permute-done | bytes 1032224 | tf_op jit(solution)/shard_map/ppermute | solution.py:300
  426.6 1.4 bitcast_add_fusion.6
  428.0 1.0 fusion.37
  428.9 19.3 %collective-permute-done.11 = bf16[4,56,2304]{2,1,0:T(8,128)(2,1)S(1)} collective-permute-done((bf16[4,56,2304]{2,1,0:T(8,128)(2,1)S(1)}, bf16[4,56,2304]{2,1,0:T(8,128)(2,1)S(1)}, u32[]{:S(2)}, u32[]{:S(2)}) %collective-permute-start.11) | collective-permute-done | bytes 1032224 | tf_op jit(solution)/shard_map/ppermute | solution.py:300
  448.2 1.2 collective-permute-start.19
  449.7 0.4 collective-permute-start.22
  450.1 5.9 %bitcast_add_fusion = f32[2,4,56,4608]{3,2,1,0:T(8,128)S(1)} fusion(bf16[2,4,56,4608]{3,2,1,0:T(8,128)(2,1)} %collective-permute-done.5, f32[2,4,2,56,4608]{4,3,2,1,0:T(8,128)} %bitcast.178, s32[]{:T(128)S(6)} %select_n.108), kind=kLoop, calls=%fused_computation.1 | loop fusion | flops 4128768 | bytes 20643844 | tf_op jit(solution)/shard_map/add | solution.py:304
  456.2 14.2 %collective-permute-done.1 = bf16[4,56,2304]{2,1,0:T(8,128)(2,1)} collective-permute-done((bf16[4,56,2304]{2,1,0:T(8,128)(2,1)}, bf16[4,56,2304]{2,1,0:T(8,128)(2,1)}, u32[]{:S(2)}, u32[]{:S(2)}) %collective-permute-start.1) | collective-permute-done | bytes 1032224 | tf_op jit(solution)/shard_map/ppermute | solution.py:300
  470.7 1.4 bitcast_add_fusion.9
  472.2 1.4 collective-permute-start.23
  473.6 1.3 collective-permute-start.24
  475.1 0.9 collective-permute-start.12
  476.0 1.5 fusion.42
  477.6 1.2 collective-permute-start.13
  478.7 11.0 %collective-permute-done.23 = bf16[144,896]{1,0:T(8,128)(2,1)S(1)} collective-permute-done((bf16[144,896]{1,0:T(8,128)(2,1)S(1)}, bf16[144,896]{1,0:T(8,128)(2,1)S(1)}, u32[]{:S(2)}, u32[]{:S(2)}) %collective-permute-start.23) | collective-permute-done | bytes 258080 | tf_op jit(solution)/shard_map/ppermute | solution.py:300
  489.8 3.2 collective-permute-start.14
  492.9 16.1 %collective-permute-done.24 = bf16[144,896]{1,0:T(8,128)(2,1)S(1)} collective-permute-done((bf16[144,896]{1,0:T(8,128)(2,1)S(1)}, bf16[144,896]{1,0:T(8,128)(2,1)S(1)}, u32[]{:S(2)}, u32[]{:S(2)}) %collective-permute-start.24) | collective-permute-done | bytes 258080 | tf_op jit(solution)/shard_map/ppermute | solution.py:300
  509.0 1.3 fusion.43
  510.3 0.8 pad_maximum_fusion.3
  511.2 0.7 collective-permute-start.3
  511.9 1.9 collective-permute-start.4
  513.9 17.3 %collective-permute-done.14 = bf16[56,2304]{1,0:T(8,128)(2,1)S(1)} collective-permute-done((bf16[56,2304]{1,0:T(8,128)(2,1)S(1)}, bf16[56,2304]{1,0:T(8,128)(2,1)S(1)}, u32[]{:S(2)}, u32[]{:S(2)}) %collective-permute-start.14) | collective-permute-done | bytes 258080 | tf_op jit(solution)/shard_map/ppermute | solution.py:300
  531.3 0.5 bitcast_add_fusion.4
  532.1 0.7 collective-permute-start.8
  532.8 1.9 collective-permute-start.9
  534.7 7.6 %collective-permute-done.4 = bf16[56,2304]{1,0:T(8,128)(2,1)S(1)} collective-permute-done((bf16[56,2304]{1,0:T(8,128)(2,1)S(1)}, bf16[56,2304]{1,0:T(8,128)(2,1)S(1)}, u32[]{:S(2)}, u32[]{:S(2)}) %collective-permute-start.4) | collective-permute-done | bytes 258080 | tf_op jit(solution)/shard_map/ppermute | solution.py:300
  542.4 7.2 %collective-permute-done.7 = bf16[56,4608]{1,0:T(8,128)(2,1)S(1)} collective-permute-done((bf16[56,4608]{1,0:T(8,128)(2,1)S(1)}, bf16[56,4608]{1,0:T(8,128)(2,1)S(1)}, u32[]{:S(2)}, u32[]{:S(2)}) %collective-permute-start.7) | collective-permute-done | bytes 516128 | tf_op jit(solution)/shard_map/ppermute | solution.py:300
  549.6 23.3 %collective-permute-done.8 = bf16[56,4608]{1,0:T(8,128)(2,1)S(1)} collective-permute-done((bf16[56,4608]{1,0:T(8,128)(2,1)S(1)}, bf16[56,4608]{1,0:T(8,128)(2,1)S(1)}, u32[]{:S(2)}, u32[]{:S(2)}) %collective-permute-start.8) | collective-permute-done | bytes 516128 | tf_op jit(solution)/shard_map/ppermute | solution.py:300
  572.9 13.7 %collective-permute-done.9 = bf16[56,4608]{1,0:T(8,128)(2,1)S(1)} collective-permute-done((bf16[56,4608]{1,0:T(8,128)(2,1)S(1)}, bf16[56,4608]{1,0:T(8,128)(2,1)S(1)}, u32[]{:S(2)}, u32[]{:S(2)}) %collective-permute-start.9) | collective-permute-done | bytes 516128 | tf_op jit(solution)/shard_map/ppermute | solution.py:300
  586.8 0.8 pad_maximum_fusion.2
  587.6 0.8 pad_maximum_fusion.1
  (68 shorter events, 3.2 us)
Async XLA Ops:
  228.2 3.9 copy-start.7
  232.0 143.2 %collective-permute-start.15 = (bf16[2,4,144,896]{3,2,1,0:T(8,128)(2,1)}, bf16[2,4,144,896]{3,2,1,0:T(8,128)(2,1)}, u32[]{:S(2)}, u32[]{:S(2)}) collective-permute-start(bf16[2,4,144,896]{3,2,1,0:T(8,128)(2,1)} %fusion.4), channel_id=1, source_target_pairs={{0,1},{1,0},{2,3},{3,2},{4,5},{5,4},{6,7},{7,6},{8,9},{9,8},{10,11... | collective-permute-start | bytes 6193160 | tf_op jit(solution)/shard_map/ppermute | solution.py:300
  244.8 3.3 copy-start.2
  248.3 131.6 %collective-permute-start.20 = (bf16[2,4,144,896]{3,2,1,0:T(8,128)(2,1)S(1)}, bf16[2,4,144,896]{3,2,1,0:T(8,128)(2,1)}, u32[]{:S(2)}, u32[]{:S(2)}) collective-permute-start(bf16[2,4,144,896]{3,2,1,0:T(8,128)(2,1)S(1)} %fusion.5), channel_id=1, source_target_pairs={{0,1},{1,0},{2,3},{3,2},{4,5},{5,4},{6,7},{7,6},{8,9},{9,8},{10,11... | collective-permute-start | bytes 6193160 | tf_op jit(solution)/shard_map/ppermute | solution.py:300
  288.9 4.1 copy-start.3
  288.9 5.6 copy-start.9
  293.0 31.5 %slice-start = ((s8[9437184]{0:T(1024)(128)(4,1)}), s8[4194304]{0:T(1024)(128)(4,1)S(1)}, s32[]{:S(2)}) async-start(s8[9437184]{0:T(1024)(128)(4,1)} %bitcast.171), calls=%async_computation | async-start | bytes 8388608
  294.5 91.1 %collective-permute-start.10 = (bf16[2,4,56,2304]{3,2,1,0:T(8,128)(2,1)}, bf16[2,4,56,2304]{3,2,1,0:T(8,128)(2,1)}, u32[]{:S(2)}, u32[]{:S(2)}) collective-permute-start(bf16[2,4,56,2304]{3,2,1,0:T(8,128)(2,1)} %fusion.3), channel_id=1, source_target_pairs={{0,1},{1,0},{2,3},{3,2},{4,5},{5,4},{6,7},{7,6},{8,9},{9,8},{10,11... | collective-permute-start | bytes 6193160 | tf_op jit(solution)/shard_map/ppermute | solution.py:300
  294.5 30.0 %slice-start.1 = ((s8[9437184]{0:T(1024)(128)(4,1)}), s8[4194304]{0:T(1024)(128)(4,1)S(1)}, s32[]{:S(2)}) async-start(s8[9437184]{0:T(1024)(128)(4,1)} %bitcast.171), calls=%async_computation.1 | async-start | bytes 8388608
  294.5 30.0 %slice-start.2 = ((s8[9437184]{0:T(1024)(128)(4,1)}), s8[1048576]{0:T(1024)(128)(4,1)S(1)}, s32[]{:S(2)}) async-start(s8[9437184]{0:T(1024)(128)(4,1)} %bitcast.171), calls=%async_computation.2 | async-start | bytes 2097152
  318.3 6.2 %copy-start.8 = (bf16[2048,896]{1,0:T(8,128)(2,1)S(1)}, bf16[2048,896]{1,0:T(8,128)(2,1)}, u32[]{:S(2)}) copy-start(bf16[2048,896]{1,0:T(8,128)(2,1)} %get-tuple-element.25) | copy-start | bytes 11010052
  324.3 125.4 %collective-permute-start.5 = (bf16[2,4,56,4608]{3,2,1,0:T(8,128)(2,1)}, bf16[2,4,56,4608]{3,2,1,0:T(8,128)(2,1)}, u32[]{:S(2)}, u32[]{:S(2)}) collective-permute-start(bf16[2,4,56,4608]{3,2,1,0:T(8,128)(2,1)} %fusion), channel_id=1, source_target_pairs={{0,1},{1,0},{2,3},{3,2},{4,5},{5,4},{6,7},{7,6},{8,9},{9,8},{10,11... | collective-permute-start | bytes 12386312 | tf_op jit(solution)/shard_map/ppermute | solution.py:300
  333.8 3.3 copy-start.4
  338.6 49.6 %collective-permute-start = (bf16[2,4,56,2304]{3,2,1,0:T(8,128)(2,1)}, bf16[2,4,56,2304]{3,2,1,0:T(8,128)(2,1)}, u32[]{:S(2)}, u32[]{:S(2)}) collective-permute-start(bf16[2,4,56,2304]{3,2,1,0:T(8,128)(2,1)} %fusion.2), channel_id=1, source_target_pairs={{0,1},{1,0},{2,3},{3,2},{4,5},{5,4},{6,7},{7,6},{8,9},{9,8},{10,11... | collective-permute-start | bytes 6193160 | tf_op jit(solution)/shard_map/ppermute | solution.py:300
  375.3 10.3 %slice-start.3 = ((s8[8257536]{0:T(1024)(128)(4,1)}), s8[4194304]{0:T(1024)(128)(4,1)S(1)}, s32[]{:S(2)}) async-start(s8[8257536]{0:T(1024)(128)(4,1)} %bitcast.184), calls=%async_computation.3 | async-start | bytes 8388608
  379.7 5.9 %slice-start.4 = ((s8[8257536]{0:T(1024)(128)(4,1)}), s8[4063232]{0:T(1024)(128)(4,1)S(1)}, s32[]{:S(2)}) async-start(s8[8257536]{0:T(1024)(128)(4,1)} %bitcast.184), calls=%async_computation.4 | async-start | bytes 8126464
  379.7 24.4 %collective-permute-start.16 = (bf16[4,144,896]{2,1,0:T(8,128)(2,1)}, bf16[4,144,896]{2,1,0:T(8,128)(2,1)}, u32[]{:S(2)}, u32[]{:S(2)}) collective-permute-start(bf16[4,144,896]{2,1,0:T(8,128)(2,1)} %fusion.8), channel_id=1, source_target_pairs={{0,8},{1,9},{2,10},{3,11},{4,12},{5,13},{6,14},{7,15},{8,0},{9,1},... | collective-permute-start | bytes 3096584 | tf_op jit(solution)/shard_map/ppermute | solution.py:300
  379.9 8.3 %slice-start.5 = ((s8[8257536]{0:T(1024)(128)(4,1)}), s8[4194304]{0:T(1024)(128)(4,1)S(1)}, s32[]{:S(2)}) async-start(s8[8257536]{0:T(1024)(128)(4,1)} %bitcast.188), calls=%async_computation.5 | async-start | bytes 8388608
  384.3 3.9 slice-start.6
  384.3 41.9 %collective-permute-start.21 = (bf16[4,144,896]{2,1,0:T(8,128)(2,1)}, bf16[4,144,896]{2,1,0:T(8,128)(2,1)}, u32[]{:S(2)}, u32[]{:S(2)}) collective-permute-start(bf16[4,144,896]{2,1,0:T(8,128)(2,1)} %fusion.9), channel_id=1, source_target_pairs={{0,8},{1,9},{2,10},{3,11},{4,12},{5,13},{6,14},{7,15},{8,0},{9,1},... | collective-permute-start | bytes 3096584 | tf_op jit(solution)/shard_map/ppermute | solution.py:300
  387.8 60.4 %collective-permute-start.11 = (bf16[4,56,2304]{2,1,0:T(8,128)(2,1)S(1)}, bf16[4,56,2304]{2,1,0:T(8,128)(2,1)S(1)}, u32[]{:S(2)}, u32[]{:S(2)}) collective-permute-start(bf16[4,56,2304]{2,1,0:T(8,128)(2,1)S(1)} %fusion.7), channel_id=1, source_target_pairs={{0,8},{1,9},{2,10},{3,11},{4,12},{5,13},{6,14},{7,15},{8,0},{9,1},... | collective-permute-start | bytes 3096584 | tf_op jit(solution)/shard_map/ppermute | solution.py:300
  391.4 79.1 %collective-permute-start.1 = (bf16[4,56,2304]{2,1,0:T(8,128)(2,1)}, bf16[4,56,2304]{2,1,0:T(8,128)(2,1)}, u32[]{:S(2)}, u32[]{:S(2)}) collective-permute-start(bf16[4,56,2304]{2,1,0:T(8,128)(2,1)} %fusion.6), channel_id=1, source_target_pairs={{0,8},{1,9},{2,10},{3,11},{4,12},{5,13},{6,14},{7,15},{8,0},{9,1},... | collective-permute-start | bytes 3096584 | tf_op jit(solution)/shard_map/ppermute | solution.py:300
  405.5 20.7 %copy-start.1 = (f32[4,144,896]{2,1,0:T(8,128)}, f32[4,144,896]{2,1,0:T(8,128)S(1)}, u32[]{:S(2)}) copy-start(f32[4,144,896]{2,1,0:T(8,128)S(1)} %bitcast_add_fusion.7) | copy-start | bytes 6193156
  406.6 65.6 %collective-permute-start.17 = (bf16[144,896]{1,0:T(8,128)(2,1)}, bf16[144,896]{1,0:T(8,128)(2,1)}, u32[]{:S(2)}, u32[]{:S(2)}) collective-permute-start(bf16[144,896]{1,0:T(8,128)(2,1)} %get-tuple-element.33), channel_id=1, source_target_pairs={{0,2},{1,3},{2,0},{3,1},{4,6},{5,7},{6,4},{7,5},{8,10},{9,11},{10,... | collective-permute-start | bytes 774152 | tf_op jit(solution)/shard_map/ppermute | solution.py:300
  426.2 47.4 %collective-permute-start.18 = (bf16[144,896]{1,0:T(8,128)(2,1)}, bf16[144,896]{1,0:T(8,128)(2,1)}, u32[]{:S(2)}, u32[]{:S(2)}) collective-permute-start(bf16[144,896]{1,0:T(8,128)(2,1)} %get-tuple-element.35), channel_id=1, source_target_pairs={{0,4},{1,5},{2,6},{3,7},{4,0},{5,1},{6,2},{7,3},{8,12},{9,13},{10,... | collective-permute-start | bytes 774152 | tf_op jit(solution)/shard_map/ppermute | solution.py:300
  427.9 21.7 %copy-start = (f32[4,144,896]{2,1,0:T(8,128)}, f32[4,144,896]{2,1,0:T(8,128)S(1)}, u32[]{:S(2)}) copy-start(f32[4,144,896]{2,1,0:T(8,128)S(1)} %bitcast_add_fusion.6) | copy-start | bytes 6193156
  448.2 26.8 %collective-permute-start.19 = (bf16[144,896]{1,0:T(8,128)(2,1)}, bf16[144,896]{1,0:T(8,128)(2,1)}, u32[]{:S(2)}, u32[]{:S(2)}) collective-permute-start(bf16[144,896]{1,0:T(8,128)(2,1)} %get-tuple-element.34), channel_id=1, source_target_pairs={{0,6},{1,7},{2,4},{3,5},{4,2},{5,3},{6,0},{7,1},{8,14},{9,15},{10,... | collective-permute-start | bytes 774152 | tf_op jit(solution)/shard_map/ppermute | solution.py:300
  449.7 27.9 %collective-permute-start.22 = (bf16[144,896]{1,0:T(8,128)(2,1)}, bf16[144,896]{1,0:T(8,128)(2,1)}, u32[]{:S(2)}, u32[]{:S(2)}) collective-permute-start(bf16[144,896]{1,0:T(8,128)(2,1)} %get-tuple-element.36), channel_id=1, source_target_pairs={{0,2},{1,3},{2,0},{3,1},{4,6},{5,7},{6,4},{7,5},{8,10},{9,11},{10,... | collective-permute-start | bytes 774152 | tf_op jit(solution)/shard_map/ppermute | solution.py:300
  456.2 16.0 %copy-start.6 = (bf16[144,896]{1,0:T(8,128)(2,1)S(1)}, bf16[144,896]{1,0:T(8,128)(2,1)}, u32[]{:S(2)}) copy-start(bf16[144,896]{1,0:T(8,128)(2,1)} %get-tuple-element.38) | copy-start | bytes 774148
  456.2 17.4 %copy-start.5 = (bf16[144,896]{1,0:T(8,128)(2,1)S(1)}, bf16[144,896]{1,0:T(8,128)(2,1)}, u32[]{:S(2)}) copy-start(bf16[144,896]{1,0:T(8,128)(2,1)} %get-tuple-element.37) | copy-start | bytes 774148
  470.5 60.8 %collective-permute-start.6 = (bf16[4,56,4608]{2,1,0:T(8,128)(2,1)S(1)}, bf16[4,56,4608]{2,1,0:T(8,128)(2,1)S(1)}, u32[]{:S(2)}, u32[]{:S(2)}) collective-permute-start(bf16[4,56,4608]{2,1,0:T(8,128)(2,1)S(1)} %fusion.1), channel_id=1, source_target_pairs={{0,8},{1,9},{2,10},{3,11},{4,12},{5,13},{6,14},{7,15},{8,0},{9,1},... | collective-permute-start | bytes 6193160 | tf_op jit(solution)/shard_map/ppermute | solution.py:300
  472.2 17.6 %collective-permute-start.23 = (bf16[144,896]{1,0:T(8,128)(2,1)S(1)}, bf16[144,896]{1,0:T(8,128)(2,1)S(1)}, u32[]{:S(2)}, u32[]{:S(2)}) collective-permute-start(bf16[144,896]{1,0:T(8,128)(2,1)S(1)} %copy-done.6), channel_id=1, source_target_pairs={{0,4},{1,5},{2,6},{3,7},{4,0},{5,1},{6,2},{7,3},{8,12},{9,13},{10,... | collective-permute-start | bytes 774152 | tf_op jit(solution)/shard_map/ppermute | solution.py:300
  473.6 35.4 %collective-permute-start.24 = (bf16[144,896]{1,0:T(8,128)(2,1)S(1)}, bf16[144,896]{1,0:T(8,128)(2,1)S(1)}, u32[]{:S(2)}, u32[]{:S(2)}) collective-permute-start(bf16[144,896]{1,0:T(8,128)(2,1)S(1)} %copy-done.5), channel_id=1, source_target_pairs={{0,6},{1,7},{2,4},{3,5},{4,2},{5,3},{6,0},{7,1},{8,14},{9,15},{10,... | collective-permute-start | bytes 774152 | tf_op jit(solution)/shard_map/ppermute | solution.py:300
  475.1 36.1 %collective-permute-start.12 = (bf16[56,2304]{1,0:T(8,128)(2,1)S(1)}, bf16[56,2304]{1,0:T(8,128)(2,1)S(1)}, u32[]{:S(2)}, u32[]{:S(2)}) collective-permute-start(bf16[56,2304]{1,0:T(8,128)(2,1)S(1)} %get-tuple-element.39), channel_id=1, source_target_pairs={{0,2},{1,3},{2,0},{3,1},{4,6},{5,7},{6,4},{7,5},{8,10},{9,11},{10,... | collective-permute-start | bytes 774152 | tf_op jit(solution)/shard_map/ppermute | solution.py:300
  477.6 34.4 %collective-permute-start.13 = (bf16[56,2304]{1,0:T(8,128)(2,1)S(1)}, bf16[56,2304]{1,0:T(8,128)(2,1)S(1)}, u32[]{:S(2)}, u32[]{:S(2)}) collective-permute-start(bf16[56,2304]{1,0:T(8,128)(2,1)S(1)} %get-tuple-element.41), channel_id=1, source_target_pairs={{0,4},{1,5},{2,6},{3,7},{4,0},{5,1},{6,2},{7,3},{8,12},{9,13},{10,... | collective-permute-start | bytes 774152 | tf_op jit(solution)/shard_map/ppermute | solution.py:300
  489.8 41.4 %collective-permute-start.14 = (bf16[56,2304]{1,0:T(8,128)(2,1)S(1)}, bf16[56,2304]{1,0:T(8,128)(2,1)S(1)}, u32[]{:S(2)}, u32[]{:S(2)}) collective-permute-start(bf16[56,2304]{1,0:T(8,128)(2,1)S(1)} %get-tuple-element.40), channel_id=1, source_target_pairs={{0,6},{1,7},{2,4},{3,5},{4,2},{5,3},{6,0},{7,1},{8,14},{9,15},{10,... | collective-permute-start | bytes 774152 | tf_op jit(solution)/shard_map/ppermute | solution.py:300
  509.0 23.8 %collective-permute-start.2 = (bf16[56,2304]{1,0:T(8,128)(2,1)S(1)}, bf16[56,2304]{1,0:T(8,128)(2,1)S(1)}, u32[]{:S(2)}, u32[]{:S(2)}) collective-permute-start(bf16[56,2304]{1,0:T(8,128)(2,1)S(1)} %get-tuple-element.42), channel_id=1, source_target_pairs={{0,2},{1,3},{2,0},{3,1},{4,6},{5,7},{6,4},{7,5},{8,10},{9,11},{10,... | collective-permute-start | bytes 774152 | tf_op jit(solution)/shard_map/ppermute | solution.py:300
  511.2 23.6 %collective-permute-start.3 = (bf16[56,2304]{1,0:T(8,128)(2,1)S(1)}, bf16[56,2304]{1,0:T(8,128)(2,1)S(1)}, u32[]{:S(2)}, u32[]{:S(2)}) collective-permute-start(bf16[56,2304]{1,0:T(8,128)(2,1)S(1)} %get-tuple-element.44), channel_id=1, source_target_pairs={{0,4},{1,5},{2,6},{3,7},{4,0},{5,1},{6,2},{7,3},{8,12},{9,13},{10,... | collective-permute-start | bytes 774152 | tf_op jit(solution)/shard_map/ppermute | solution.py:300
  511.9 30.4 %collective-permute-start.4 = (bf16[56,2304]{1,0:T(8,128)(2,1)S(1)}, bf16[56,2304]{1,0:T(8,128)(2,1)S(1)}, u32[]{:S(2)}, u32[]{:S(2)}) collective-permute-start(bf16[56,2304]{1,0:T(8,128)(2,1)S(1)} %get-tuple-element.43), channel_id=1, source_target_pairs={{0,6},{1,7},{2,4},{3,5},{4,2},{5,3},{6,0},{7,1},{8,14},{9,15},{10,... | collective-permute-start | bytes 774152 | tf_op jit(solution)/shard_map/ppermute | solution.py:300
  532.0 17.6 %collective-permute-start.7 = (bf16[56,4608]{1,0:T(8,128)(2,1)S(1)}, bf16[56,4608]{1,0:T(8,128)(2,1)S(1)}, u32[]{:S(2)}, u32[]{:S(2)}) collective-permute-start(bf16[56,4608]{1,0:T(8,128)(2,1)S(1)} %get-tuple-element.30), channel_id=1, source_target_pairs={{0,2},{1,3},{2,0},{3,1},{4,6},{5,7},{6,4},{7,5},{8,10},{9,11},{10,... | collective-permute-start | bytes 1548296 | tf_op jit(solution)/shard_map/ppermute | solution.py:300
  532.1 40.8 %collective-permute-start.8 = (bf16[56,4608]{1,0:T(8,128)(2,1)S(1)}, bf16[56,4608]{1,0:T(8,128)(2,1)S(1)}, u32[]{:S(2)}, u32[]{:S(2)}) collective-permute-start(bf16[56,4608]{1,0:T(8,128)(2,1)S(1)} %get-tuple-element.32), channel_id=1, source_target_pairs={{0,4},{1,5},{2,6},{3,7},{4,0},{5,1},{6,2},{7,3},{8,12},{9,13},{10,... | collective-permute-start | bytes 1548296 | tf_op jit(solution)/shard_map/ppermute | solution.py:300
  532.8 53.7 %collective-permute-start.9 = (bf16[56,4608]{1,0:T(8,128)(2,1)S(1)}, bf16[56,4608]{1,0:T(8,128)(2,1)S(1)}, u32[]{:S(2)}, u32[]{:S(2)}) collective-permute-start(bf16[56,4608]{1,0:T(8,128)(2,1)S(1)} %get-tuple-element.31), channel_id=1, source_target_pairs={{0,6},{1,7},{2,4},{3,5},{4,2},{5,3},{6,0},{7,1},{8,14},{9,15},{10,... | collective-permute-start | bytes 1548296 | tf_op jit(solution)/shard_map/ppermute | solution.py:300
